TPU v7x, 16 devices: a whole 2x2x2 slice. The times are simulated.
16 devices in a mesh: tp: 2 (over z), ep: 8 (over y, x, core).
Axes of the slice: x: 2, y: 2, z: 2, core: 2. Of those that a mesh axis runs over, the one named last changes fastest.
Arguments:
- act_in: bfloat16 [4096, 1536], P('ep')
- w_router: float32 [1536, 64], replicated
- choice_one: int32 [4096], P('ep')
- choice_two: int32 [4096], P('ep')
- w_gelu: bfloat16 [64, 1536, 512], P('ep', None, 'tp')
- w_lin: bfloat16 [64, 1536, 512], P('ep', None, 'tp')
- w_out: bfloat16 [64, 512, 1536], P('ep', 'tp')
- grad_out: bfloat16 [4096, 1536], P('ep')
Outputs:
- output 1: bfloat16 [4096, 1536], P('ep')
- output 2: bfloat16 [4096, 1536], P('ep')
- output 3: float32 [64, 1536, 512], P('ep', None, 'tp')
- output 4: float32 [64, 1536, 512], P('ep', None, 'tp')
- output 5: float32 [64, 512, 1536], P('ep', 'tp')
- output 6: float32 [1536, 64], replicated
All inputs are finite; a program needn't handle non-finite values.
Results may differ from a plain program's by a relative error of at most 0.00999651.
Values are sent between devices in bfloat16 or wider.
A program may use at most 1 GiB of HBM per device.

v0:
```python
import jax
import jax.numpy as jnp
from jax import lax
from jax.sharding import PartitionSpec as P

GELU_COEF = 0.7978845608028654


def gelu_parts(pre_act):
    inner_arg = GELU_COEF * (pre_act + 0.044715 * pre_act * pre_act * pre_act)
    tanh_val = jnp.tanh(inner_arg)
    gelu_val = 0.5 * pre_act * (1.0 + tanh_val)
    gelu_slope = 0.5 * (1.0 + tanh_val) + 0.5 * pre_act * (1.0 - tanh_val * tanh_val) * GELU_COEF * (1.0 + 0.134145 * pre_act * pre_act)
    return gelu_val, gelu_slope


def route_shard(x_rows, w_router, first_ids, second_ids, slot_cap):
    n_experts = w_router.shape[1]
    logits = jnp.dot(x_rows.astype(jnp.float32), w_router, precision=lax.Precision.HIGHEST)
    router_prob = jax.nn.softmax(logits, axis=-1)
    expert_ids = jnp.arange(n_experts, dtype=jnp.int32)
    hot_one = (first_ids[:, None] == expert_ids[None, :]).astype(jnp.int32)
    hot_two = (second_ids[:, None] == expert_ids[None, :]).astype(jnp.int32)
    prob_one = jnp.sum(router_prob * hot_one, axis=-1)
    prob_two = jnp.sum(router_prob * hot_two, axis=-1)
    fill_one = jnp.sum(hot_one, axis=0)
    pos_one = jnp.sum((jnp.cumsum(hot_one, axis=0) - hot_one) * hot_one, axis=-1)
    pos_two = jnp.sum((jnp.cumsum(hot_two, axis=0) - hot_two + fill_one[None, :]) * hot_two, axis=-1)
    slot_one = jnp.where(pos_one < slot_cap, first_ids * slot_cap + pos_one, n_experts * slot_cap)
    slot_two = jnp.where(pos_two < slot_cap, second_ids * slot_cap + pos_two, n_experts * slot_cap)
    gate_sum = prob_one + prob_two
    return (router_prob, hot_one, hot_two, prob_one, prob_two, prob_one / gate_sum, prob_two / gate_sum, slot_one, slot_two)


def fill_slots(slot_one, slot_two, gate_one, gate_two, n_slots):
    n_tokens = slot_one.shape[0]
    token_rows = jnp.arange(n_tokens, dtype=jnp.int32)
    source = jnp.full((n_slots,), n_tokens, jnp.int32).at[slot_one].set(token_rows, mode="drop").at[slot_two].set(token_rows, mode="drop")
    weight = jnp.zeros((n_slots,), jnp.float32).at[slot_one].set(gate_one, mode="drop").at[slot_two].set(gate_two, mode="drop")
    return source, weight


def combine_tokens(routed, merged_tok, grad_tok, dy_rows, w_router):
    (router_prob, hot_one, hot_two, prob_one, prob_two, gate_one, gate_two, slot_one, slot_two) = routed
    out_one = jnp.take(merged_tok, slot_one, axis=0, mode="fill", fill_value=0).astype(jnp.float32)
    out_two = jnp.take(merged_tok, slot_two, axis=0, mode="fill", fill_value=0).astype(jnp.float32)
    act_out = (gate_one[:, None] * out_one + gate_two[:, None] * out_two).astype(jnp.bfloat16)
    dy_f32 = dy_rows.astype(jnp.float32)
    dgate_one = jnp.sum(dy_f32 * out_one, axis=-1)
    dgate_two = jnp.sum(dy_f32 * out_two, axis=-1)
    shared = dgate_one * gate_one + dgate_two * gate_two
    gate_sum = prob_one + prob_two
    dprob_one = (dgate_one - shared) / gate_sum
    dprob_two = (dgate_two - shared) / gate_sum
    centre = dprob_one * prob_one + dprob_two * prob_two
    grad_logits = router_prob * (dprob_one[:, None] * hot_one + dprob_two[:, None] * hot_two - centre[:, None])
    back_one = jnp.take(grad_tok, slot_one, axis=0, mode="fill", fill_value=0).astype(jnp.float32)
    back_two = jnp.take(grad_tok, slot_two, axis=0, mode="fill", fill_value=0).astype(jnp.float32)
    router_back = jnp.einsum("se,de->sd", grad_logits, w_router, precision=lax.Precision.HIGHEST)
    grad_in = (back_one + back_two + router_back).astype(jnp.bfloat16)
    return act_out, grad_in, grad_logits


def solution(mesh):
    tp_size = mesh.shape["tp"]

    def local_step(x_rows, w_router, first_ids, second_ids, w_gelu, w_lin, w_out, dy_rows):
        n_tokens, model_width = x_rows.shape
        n_experts = w_router.shape[1]
        slot_cap = 2 * n_tokens // n_experts
        routed = route_shard(x_rows, w_router, first_ids, second_ids, slot_cap)
        source, weight = fill_slots(routed[7], routed[8], routed[5], routed[6], n_experts * slot_cap)
        disp_tok = jnp.take(x_rows, source, axis=0, mode="fill", fill_value=0).reshape(n_experts, slot_cap, model_width)
        dout_tok = (weight[:, None] * jnp.take(dy_rows, source, axis=0, mode="fill", fill_value=0).astype(jnp.float32)).astype(jnp.bfloat16).reshape(n_experts, slot_cap, model_width)
        disp_exp = lax.all_to_all(disp_tok, "ep", 0, 1, tiled=True)
        dout_exp = lax.all_to_all(dout_tok, "ep", 0, 1, tiled=True)
        pre_a = jnp.einsum("erd,edf->erf", disp_exp, w_gelu, preferred_element_type=jnp.float32)
        pre_b = jnp.einsum("erd,edf->erf", disp_exp, w_lin, preferred_element_type=jnp.float32)
        gelu_val, gelu_slope = gelu_parts(pre_a)
        hidden = (gelu_val * pre_b).astype(jnp.bfloat16)
        part_out = jnp.einsum("erf,efd->erd", hidden, w_out, preferred_element_type=jnp.float32).astype(jnp.bfloat16)
        merged = jnp.sum(lax.all_gather(part_out, "tp").astype(jnp.float32), axis=0).astype(jnp.bfloat16)
        merged_tok = lax.all_to_all(merged, "ep", 1, 0, tiled=True).reshape(n_experts * slot_cap, model_width)
        grad_hidden = jnp.einsum("erd,efd->erf", dout_exp, w_out, preferred_element_type=jnp.float32)
        grad_a = (grad_hidden * pre_b * gelu_slope).astype(jnp.bfloat16)
        grad_b = (grad_hidden * gelu_val).astype(jnp.bfloat16)
        grad_wc = jnp.einsum("erf,erd->efd", hidden, dout_exp, preferred_element_type=jnp.float32)
        grad_wa = jnp.einsum("erd,erf->edf", disp_exp, grad_a, preferred_element_type=jnp.float32)
        grad_wb = jnp.einsum("erd,erf->edf", disp_exp, grad_b, preferred_element_type=jnp.float32)
        part_in = (jnp.einsum("erf,edf->erd", grad_a, w_gelu, preferred_element_type=jnp.float32) + jnp.einsum("erf,edf->erd", grad_b, w_lin, preferred_element_type=jnp.float32)).astype(jnp.bfloat16)
        grad_disp = jnp.sum(lax.all_gather(part_in, "tp").astype(jnp.float32), axis=0).astype(jnp.bfloat16)
        grad_tok = lax.all_to_all(grad_disp, "ep", 1, 0, tiled=True).reshape(n_experts * slot_cap, model_width)
        act_out, grad_in, grad_logits = combine_tokens(routed, merged_tok, grad_tok, dy_rows, w_router)
        part_rows = n_tokens // tp_size
        row_start = lax.axis_index("tp") * part_rows
        x_part = lax.dynamic_slice_in_dim(x_rows, row_start, part_rows, 0).astype(jnp.float32)
        logit_part = lax.dynamic_slice_in_dim(grad_logits, row_start, part_rows, 0)
        grad_router = lax.psum(jnp.einsum("sd,se->de", x_part, logit_part, precision=lax.Precision.HIGHEST), ("ep", "tp"))
        return act_out, grad_in, grad_wa, grad_wb, grad_wc, grad_router

    return jax.shard_map(local_step, mesh=mesh, in_specs=(P("ep", None), P(), P("ep"), P("ep"), P("ep", None, "tp"), P("ep", None, "tp"), P("ep", "tp", None), P("ep", None)), out_specs=(P("ep", None), P("ep", None), P("ep", None, "tp"), P("ep", None, "tp"), P("ep", "tp", None), P()), check_vma=False)
```

profile of v0, /device:TPU:0, one launch (start us, length us, event | category | flops | bytes accessed | tf_op | source)
XLA Modules:
  0.0 479.3 jit_solution(2399545787038827553)
XLA Ops:
  19.6 5.6 %gather_fusion = bf16[1024,1536]{1,0:T(8,128)(2,1)} fusion(bf16[512,1536]{1,0:T(8,128)(2,1)S(1)} %copy-done, s32[1024]{0:T(1024)S(1)} %fusion.33), kind=kCustom, calls=%fused_computation.clone | custom fusion | bytes 6295552 | tf_op jit(solution)/shard_map/jit(_take)/gather | solution.py:73
  27.5 43.2 %all_to_all.66 = bf16[64,16,1536]{2,1,0:T(8,128)(2,1)S(1)} all-to-all(bf16[64,16,1536]{2,1,0:T(8,128)(2,1)S(1)} %bitcast.91), channel_id=1, replica_groups=mesh['tp'=2,'ep'=8] {'ep'}, dimensions={0} | all-to-all | bytes 6291456 | tf_op jit(solution)/shard_map/all_to_all | solution.py:75
  80.4 78.5 %all-gather.5.cloned.1.call-done = bf16[16,128,1536]{2,1,0:T(8,128)(2,1)} async-done(((bf16[8,128,1536]{2,1,0:T(8,128)(2,1)}), bf16[16,128,1536]{2,1,0:T(8,128)(2,1)}) %all-gather.5.cloned.1.call-update) | async-done | bytes 6291472 | tf_op jit(solution)/shard_map/all_gather | solution.py:82
  159.0 6.6 %reduce_sum.102 = bf16[8,128,1536]{2,1,0:T(8,128)(2,1)} reduce(bf16[2,8,128,1536]{3,2,1,0:T(8,128)(2,1)} %bitcast.93, bf16[]{:T(256)} %constant.17.clone.1), dimensions={0}, to_apply=%region_13.15 | reduce | flops 1572864 | bytes 9437186 | tf_op jit(solution)/shard_map/reduce_sum | solution.py:82
  165.5 5.3 %copy.42 = bf16[8,128,1536]{2,0,1:T(8,128)(2,1)} copy(bf16[8,128,1536]{2,1,0:T(8,128)(2,1)} %reduce_sum.102) | data formatting | bytes 6291456 | tf_op jit(solution)/shard_map/reduce_sum | solution.py:82
  175.7 5.6 %gather_fusion.3 = bf16[1024,1536]{1,0:T(8,128)(2,1)} fusion(bf16[512,1536]{1,0:T(8,128)(2,1)S(1)} %copy-done.1, s32[1024]{0:T(1024)S(1)} %fusion.33), kind=kCustom, calls=%fused_computation.2.clone | custom fusion | bytes 6295552 | tf_op jit(solution)/shard_map/jit(_take)/gather | solution.py:74
  185.4 27.8 %all-to-all-done.1 = bf16[8,128,1536]{2,0,1:T(8,128)(2,1)} async-done(((bf16[8,128,1536]{2,0,1:T(8,128)(2,1)}), bf16[8,128,1536]{2,0,1:T(8,128)(2,1)}, u32[]{:S(2)}, u32[]{:S(2)}) %all-to-all-start.1) | async-done | bytes 3145760 | tf_op jit(solution)/shard_map/all_to_all | solution.py:83
  213.2 4.6 copy.44
  217.8 6.7 %gather_fusion.1 = bf16[512,1536]{1,0:T(8,128)(2,1)} fusion(bf16[1024,1536]{1,0:T(8,128)(2,1)} %bitcast.68, s32[1024]{0:T(1024)S(1)} %copy-done.22), kind=kCustom, calls=%fused_computation.1.clone | custom fusion | bytes 3147776 | tf_op jit(solution)/shard_map/jit(_take)/gather | solution.py:45
  224.5 6.7 %gather_fusion.2 = bf16[512,1536]{1,0:T(8,128)(2,1)} fusion(bf16[1024,1536]{1,0:T(8,128)(2,1)} %bitcast.69, s32[1024]{0:T(1024)S(1)} %copy-done.24), kind=kCustom, calls=%fused_computation.3.clone | custom fusion | bytes 3147776 | tf_op jit(solution)/shard_map/jit(_take)/gather | solution.py:46
  242.6 40.8 %all_to_all.67 = bf16[64,16,1536]{2,1,0:T(8,128)(2,1)S(1)} all-to-all(bf16[64,16,1536]{2,1,0:T(8,128)(2,1)S(1)} %bitcast.88), channel_id=1, replica_groups=mesh['tp'=2,'ep'=8] {'ep'}, dimensions={0} | all-to-all | bytes 6291456 | tf_op jit(solution)/shard_map/all_to_all | solution.py:76
  296.1 77.5 %all-gather.7.cloned.1.call-done = bf16[16,128,1536]{2,1,0:T(8,128)(2,1)} async-done(((bf16[8,128,1536]{2,1,0:T(8,128)(2,1)}), bf16[16,128,1536]{2,1,0:T(8,128)(2,1)}) %all-gather.7.cloned.1.call-update) | async-done | bytes 6291472 | tf_op jit(solution)/shard_map/all_gather | solution.py:91
  373.6 6.6 %reduce_sum.103 = bf16[8,128,1536]{2,1,0:T(8,128)(2,1)} reduce(bf16[2,8,128,1536]{3,2,1,0:T(8,128)(2,1)} %bitcast.92, bf16[]{:T(256)} %constant.17.clone.1), dimensions={0}, to_apply=%region_16.19 | reduce | flops 1572864 | bytes 9437186 | tf_op jit(solution)/shard_map/reduce_sum | solution.py:91
  380.1 5.3 %copy.46 = bf16[8,128,1536]{2,0,1:T(8,128)(2,1)} copy(bf16[8,128,1536]{2,1,0:T(8,128)(2,1)} %reduce_sum.103) | data formatting | bytes 6291456 | tf_op jit(solution)/shard_map/reduce_sum | solution.py:91
  385.5 4.6 all-to-all-start.3
  395.7 6.6 %fusion.42 = f32[8,1536,256]{2,1,0:T(8,128)} fusion(bf16[8,128,1536]{2,1,0:T(8,128)(2,1)S(1)} %bitcast.72, bf16[8,128,256]{2,1,0:T(8,128)(2,1)S(1)} %copy-done.14), kind=kOutput, calls=%fused_computation.96 | convolution fusion | flops 805306368 | bytes 16252928 | tf_op jit(solution)/shard_map/erd,erf->edf/dot_general | solution.py:88
  402.3 6.6 %fusion.43 = f32[8,1536,256]{2,1,0:T(8,128)} fusion(bf16[8,128,1536]{2,1,0:T(8,128)(2,1)S(1)} %bitcast.73, bf16[8,128,256]{2,1,0:T(8,128)(2,1)S(1)} %copy-done.13), kind=kOutput, calls=%fused_computation.97 | convolution fusion | flops 805306368 | bytes 16252928 | tf_op jit(solution)/shard_map/erd,erf->edf/dot_general | solution.py:89
  408.9 6.6 %fusion.44 = f32[8,256,1536]{2,1,0:T(8,128)} fusion(bf16[8,128,256]{2,1,0:T(8,128)(2,1)S(1)} %copy-done.8, bf16[8,128,1536]{2,1,0:T(8,128)(2,1)S(1)} %bitcast.83), kind=kOutput, calls=%fused_computation.98 | convolution fusion | flops 805306368 | bytes 16252928 | tf_op jit(solution)/shard_map/erf,erd->efd/dot_general | solution.py:87
  415.5 13.7 %all-to-all-done.3 = bf16[8,128,1536]{2,0,1:T(8,128)(2,1)} async-done(((bf16[8,128,1536]{2,0,1:T(8,128)(2,1)}), bf16[8,128,1536]{2,0,1:T(8,128)(2,1)}, u32[]{:S(2)}, u32[]{:S(2)}) %all-to-all-start.3) | async-done | bytes 3145760 | tf_op jit(solution)/shard_map/all_to_all | solution.py:92
  429.2 4.6 copy.48
  433.9 5.9 %gather_fusion.5 = bf16[512,1536]{1,0:T(8,128)(2,1)S(1)} fusion(bf16[1024,1536]{1,0:T(8,128)(2,1)} %bitcast.66, s32[1024]{0:T(1024)S(1)} %copy-done.24), kind=kCustom, calls=%fused_computation.5.clone | custom fusion | bytes 3147776 | tf_op jit(solution)/shard_map/jit(_take)/gather | solution.py:58
  439.8 6.7 %gather_fusion.4 = bf16[512,1536]{1,0:T(8,128)(2,1)} fusion(bf16[1024,1536]{1,0:T(8,128)(2,1)} %bitcast.67, s32[1024]{0:T(1024)S(1)} %copy-done.23), kind=kCustom, calls=%fused_computation.4.clone | custom fusion | bytes 3147776 | tf_op jit(solution)/shard_map/jit(_take)/gather | solution.py:57
  446.5 5.3 %fusion.4 = bf16[512,1536]{1,0:T(8,128)(2,1)} fusion(f32[512,64]{0,1:T(8,128)} %copy-done.19, f32[1536,64]{0,1:T(8,128)S(1)} %copy-done.18, bf16[512,1536]{1,0:T(8,128)(2,1)S(1)} %gather_fusion.5, bf16[512,1536]{1,0:T(8,128)(2,1)} %gather_fusion.4, pred[512]{0:T(512)(128)(4,1)S(1)} %copy-done.31, pred[512]{0:T(512)(128)(4,1)S(1)} %copy-done.34), kind=kOutput, calls=%fused_computation.23 | convolution fusion | flops 609484800 | bytes 5243904 | tf_op jit(solution)/shard_map/se,de->sd/dot_general | solution.py:59
  451.8 18.7 %all-reduce.2.cloned.1.call-done = f32[1536,64]{0,1:T(8,128)} async-done(((f32[1536,64]{0,1:T(8,128)}), f32[1536,64]{0,1:T(8,128)}) %all-reduce.2.cloned.1.call-update) | async-done | bytes 393232 | tf_op jit(solution)/shard_map/psum | solution.py:98
  (149 shorter events, 64.5 us)
Async XLA Ops:
  7.2 12.5 %copy-start = (bf16[512,1536]{1,0:T(8,128)(2,1)S(1)}, bf16[512,1536]{1,0:T(8,128)(2,1)}, u32[]{:S(2)}) copy-start(bf16[512,1536]{1,0:T(8,128)(2,1)} %param.12) | copy-start | bytes 4718596
  7.2 151.8 %all-gather.5.cloned.1.call-start = ((), (), s32[]{:S(2)}) async-start(), calls=%async_computation.5 | async-start | bytes 9437184 | tf_op jit(solution)/shard_map/all_gather | solution.py:82
  25.2 45.8 %slice-start = ((s8[6291456]{0:T(1024)(128)(4,1)}), s8[4194304]{0:T(1024)(128)(4,1)S(1)}, s32[]{:S(2)}) async-start(s8[6291456]{0:T(1024)(128)(4,1)} %bitcast.74), calls=%async_computation.7 | async-start | bytes 8388608
  27.5 43.5 %slice-start.1 = ((s8[6291456]{0:T(1024)(128)(4,1)}), s8[2097152]{0:T(1024)(128)(4,1)S(1)}, s32[]{:S(2)}) async-start(s8[6291456]{0:T(1024)(128)(4,1)} %bitcast.74), calls=%async_computation.8 | async-start | bytes 4194304
  170.8 42.3 %all-to-all-start.1 = ((bf16[8,128,1536]{2,0,1:T(8,128)(2,1)}), bf16[8,128,1536]{2,0,1:T(8,128)(2,1)}, u32[]{:S(2)}, u32[]{:S(2)}) async-start(bf16[8,128,1536]{2,0,1:T(8,128)(2,1)} %copy.42), calls=%async_computation.1 | async-start | bytes 6291456 | tf_op jit(solution)/shard_map/all_to_all | solution.py:83
  175.4 7.7 %copy-start.17 = (f32[1536,64]{0,1:T(8,128)S(1)}, f32[1536,64]{0,1:T(8,128)}, u32[]{:S(2)}) copy-start(f32[1536,64]{0,1:T(8,128)} %param.13) | copy-start | bytes 1179652
  175.4 9.9 %copy-start.20 = (s32[512]{0:T(512)S(1)}, s32[512]{0:T(512)}, u32[]{:S(2)}) copy-start(s32[512]{0:T(512)} %param.14) | copy-start | bytes 6148
  175.4 9.9 %copy-start.21 = (s32[512]{0:T(512)S(1)}, s32[512]{0:T(512)}, u32[]{:S(2)}) copy-start(s32[512]{0:T(512)} %param.15) | copy-start | bytes 6148
  175.4 198.1 %all-gather.7.cloned.1.call-start = ((), (), s32[]{:S(2)}) async-start(), calls=%async_computation.6 | async-start | bytes 9437184 | tf_op jit(solution)/shard_map/all_gather | solution.py:91
  217.8 6.7 %copy-start.24 = (s32[1024]{0:T(1024)S(1)}, s32[1024]{0:T(1024)}, u32[]{:S(2)}) copy-start(s32[1024]{0:T(1024)} %pad_clamp_fusion) | copy-start | bytes 12292
  224.5 6.7 %copy-start.32 = (pred[512]{0:T(512)(128)(4,1)S(1)}, pred[512]{0:T(512)(128)(4,1)}, u32[]{:S(2)}) copy-start(pred[512]{0:T(512)(128)(4,1)} %get-tuple-element.29) | copy-start | bytes 1540
  240.0 43.7 %slice-start.10 = ((s8[6291456]{0:T(1024)(128)(4,1)}), s8[4194304]{0:T(1024)(128)(4,1)S(1)}, s32[]{:S(2)}) async-start(s8[6291456]{0:T(1024)(128)(4,1)} %bitcast.86), calls=%async_computation.17 | async-start | bytes 8388608
  242.6 41.1 %slice-start.11 = ((s8[6291456]{0:T(1024)(128)(4,1)}), s8[2097152]{0:T(1024)(128)(4,1)S(1)}, s32[]{:S(2)}) async-start(s8[6291456]{0:T(1024)(128)(4,1)} %bitcast.86), calls=%async_computation.18 | async-start | bytes 4194304
  242.6 41.1 %copy-start.10 = (f32[8,128,256]{2,1,0:T(8,128)S(1)}, f32[8,128,256]{2,1,0:T(8,128)}, u32[]{:S(2)}) copy-start(f32[8,128,256]{2,1,0:T(8,128)} %copy-done.9) | copy-start | bytes 3145732
  242.6 41.1 %copy-start.11 = (f32[8,128,256]{2,1,0:T(8,128)S(1)}, f32[8,128,256]{2,1,0:T(8,128)}, u32[]{:S(2)}) copy-start(f32[8,128,256]{2,1,0:T(8,128)} %get-tuple-element.28) | copy-start | bytes 3145732
  283.4 8.8 %slice-start.6 = ((s8[6291456]{0:T(1024)(128)(4,1)}), s8[4194304]{0:T(1024)(128)(4,1)S(1)}, s32[]{:S(2)}) async-start(s8[6291456]{0:T(1024)(128)(4,1)} %bitcast.80), calls=%async_computation.13 | async-start | bytes 8388608
  283.7 8.4 %slice-start.7 = ((s8[6291456]{0:T(1024)(128)(4,1)}), s8[2097152]{0:T(1024)(128)(4,1)S(1)}, s32[]{:S(2)}) async-start(s8[6291456]{0:T(1024)(128)(4,1)} %bitcast.80), calls=%async_computation.14 | async-start | bytes 4194304
  385.4 7.0 %copy-start.6 = (bf16[512,1536]{1,0:T(8,128)(2,1)S(1)}, bf16[512,1536]{1,0:T(8,128)(2,1)}, u32[]{:S(2)}) copy-start(bf16[512,1536]{1,0:T(8,128)(2,1)} %gather_fusion.1) | copy-start | bytes 4718596
  385.5 7.0 %copy-start.31 = (pred[512]{0:T(512)(128)(4,1)S(1)}, pred[512]{0:T(512)(128)(4,1)}, u32[]{:S(2)}) copy-start(pred[512]{0:T(512)(128)(4,1)} %get-tuple-element.19) | copy-start | bytes 1540
  385.5 7.0 %copy-start.33 = (pred[512]{0:T(512)(128)(4,1)S(1)}, pred[512]{0:T(512)(128)(4,1)}, u32[]{:S(2)}) copy-start(pred[512]{0:T(512)(128)(4,1)} %get-tuple-element.29) | copy-start | bytes 1540
  385.5 43.8 %all-to-all-start.3 = ((bf16[8,128,1536]{2,0,1:T(8,128)(2,1)}), bf16[8,128,1536]{2,0,1:T(8,128)(2,1)}, u32[]{:S(2)}, u32[]{:S(2)}) async-start(bf16[8,128,1536]{2,0,1:T(8,128)(2,1)} %copy.46), calls=%async_computation.3 | async-start | bytes 6291456 | tf_op jit(solution)/shard_map/all_to_all | solution.py:92
  390.1 80.5 %all-reduce.2.cloned.1.call-start = ((), (), s32[]{:S(2)}) async-start(), calls=%async_computation.4 | async-start | bytes 786432 | tf_op jit(solution)/shard_map/psum | solution.py:98
  439.8 6.8 %copy-start.18 = (f32[1536,64]{0,1:T(8,128)S(1)}, f32[1536,64]{0,1:T(8,128)}, u32[]{:S(2)}) copy-start(f32[1536,64]{0,1:T(8,128)} %param.13) | copy-start | bytes 1179652
  439.8 6.8 %copy-start.34 = (pred[512]{0:T(512)(128)(4,1)S(1)}, pred[512]{0:T(512)(128)(4,1)}, u32[]{:S(2)}) copy-start(pred[512]{0:T(512)(128)(4,1)} %get-tuple-element.29) | copy-start | bytes 1540
  (28 other events, 116.8 us)
Sparse Core Ops, SparseCore 0:
  80.6 78.3 all-gather.4
  296.2 77.3 all-gather.6
  395.6 74.8 all-reduce.1
where the time goes:
time: 488 us; the launch traced here: 479 us
  waiting for transfers between devices  216 us (44%)
  blocking collectives  83.9 us (17%)
  local copies, waits for them, and re-layouts  76.6 us (16%)
  matrix products  44 us (9%)
  other arithmetic  34 us (7%)
  between operations  14.8 us (3%)
  starting transfers between devices  9.72 us (2%)
    all_gather x1, waiting for transfers between devices, local_step(): lax.all_gather(part_out, 'tp').astype(jnp.float32)  78.5 us
    all_gather x1, waiting for transfers between devices, local_step(): lax.all_gather(part_in, 'tp').astype(jnp.float32)  77.5 us
    all_to_all x1, blocking collectives, local_step(): disp_exp = lax.all_to_all(disp_tok, 'ep', 0, 1, tiled=True)  43.2 us
    all_to_all x1, blocking collectives, local_step(): dout_exp = lax.all_to_all(dout_tok, 'ep', 0, 1, tiled=True)  40.8 us
    all_to_all x1, waiting for transfers between devices, local_step(): lax.all_to_all(merged, 'ep', 1, 0, tiled=True)  27.8 us
    psum x1, waiting for transfers between devices, local_step(): lax.psum(jnp.einsum('sd,se->de', x_part, logit_part, precision=lax.Precis...  18.7 us
    all_to_all x1, waiting for transfers between devices, local_step(): lax.all_to_all(grad_disp, 'ep', 1, 0, tiled=True)  13.7 us
  transfers between devices with their start and end apart: 5, of which 5 were waited for; matrix products, arithmetic and copies ran while one was open for 12% of the time, Pallas kernels for 0%

commit v1 on v0

v1 whole, which is shorter than its diff:
```python
import functools

import jax
import jax.numpy as jnp
from jax import lax
from jax.experimental import pallas as pl
from jax.experimental.pallas import tpu as pltpu
from jax.sharding import PartitionSpec as P

BF = jnp.bfloat16
F32 = jnp.float32
I32 = jnp.int32
MESH = pl.DeviceIdType.MESH
GELU_COEF = 0.7978845608028654
NN = (((1,), (0,)), ((), ()))
NT = (((1,), (1,)), ((), ()))
TN = (((0,), (0,)), ((), ()))


def dot(a, b, dims=NN):
    return lax.dot_general(a, b, dims, preferred_element_type=F32)


def split3(v):
    hi = v.astype(BF)
    rest = v - hi.astype(F32)
    mid = rest.astype(BF)
    low = (rest - mid.astype(F32)).astype(BF)
    return hi, mid, low


def moe_kernel(
    tp_size, ep_size, cap,
    ids1_ref, ids2_ref, x_hbm, dy_hbm, wr_hbm, wa_hbm, wb_hbm, wc_hbm,
    y_out, dx_out, dwr_out, xe_out, de_out, h_out, da_out, db_out,
    x_v, dy_v, wr_v, wa_v, wb_v, wc_v,
    xs, ds, xr, dr, h_v, da_v, db_v, bs_v, gv_v,
    ps, pr, pdr, orr, dxr, y_v, dx_v,
    s1r, s2r, g1r, g2r, s1c, s2c, g1c, g2c, q1c, q2c, i1c, i2c, prob_v, dl_v,
    dwp, dwi, dwf,
    in_sem, w_sem, out_sem,
    xs_sem, xr_sem, ds_sem, dr_sem,
    ps_sem, pr_sem, pds_sem, pdr_sem,
    os_sem, or_sem, dxs_sem, dxr_sem,
    ys_sem, yr_sem, dys_sem, dyr_sem,
    rs_sem, rr_sem, fs_sem, fr_sem,
):
    k = lax.axis_index("tp")
    r = lax.axis_index("ep")
    n_loc = wa_v.shape[0]
    n_tok, width = x_v.shape
    hid = wa_v.shape[2]
    n_exp = n_loc * ep_size
    blk = ep_size * cap
    half = ep_size // tp_size
    my_place = (r % tp_size) * half + r // tp_size
    owner = (r % tp_size) == k
    other = 1 - k

    ins = [
        pltpu.make_async_copy(x_hbm, x_v, in_sem.at[0]),
        pltpu.make_async_copy(dy_hbm, dy_v, in_sem.at[1]),
        pltpu.make_async_copy(wr_hbm, wr_v, in_sem.at[2]),
    ]
    ins[0].start()
    ins[1].start()
    ins[2].start()

    def weight_copies(j):
        return [
            pltpu.make_async_copy(wa_hbm.at[j], wa_v.at[j], w_sem.at[0, j]),
            pltpu.make_async_copy(wb_hbm.at[j], wb_v.at[j], w_sem.at[1, j]),
            pltpu.make_async_copy(wc_hbm.at[j], wc_v.at[j], w_sem.at[2, j]),
        ]

    @pl.loop(0, n_loc)
    def _(j):
        for c in weight_copies(j):
            c.start()

    n_dev = tp_size * ep_size
    barrier = pltpu.get_barrier_semaphore()
    for d in range(1, n_dev):
        flat = (k * ep_size + r + d) % n_dev
        pl.semaphore_signal(barrier, inc=1, device_id=(flat // ep_size, flat % ep_size), device_id_type=MESH)

    ids1 = ids1_ref[...]
    ids2 = ids2_ref[...]
    e_iota = lax.broadcasted_iota(I32, (n_exp, n_tok), 0)
    hot1 = jnp.where(ids1 == e_iota, 1.0, 0.0).astype(F32)
    hot2 = jnp.where(ids2 == e_iota, 1.0, 0.0).astype(F32)
    before = jnp.where(
        lax.broadcasted_iota(I32, (n_tok, n_tok), 0) < lax.broadcasted_iota(I32, (n_tok, n_tok), 1), 1.0, 0.0
    ).astype(BF)
    cum1 = dot(hot1.astype(BF), before)
    cum2 = dot(hot2.astype(BF), before)
    fill1 = jnp.sum(hot1, axis=1, keepdims=True)
    pos1 = jnp.sum(cum1 * hot1, axis=0, keepdims=True)
    pos2 = jnp.sum((cum2 + fill1) * hot2, axis=0, keepdims=True)

    def place(ids, pos):
        spot = (ids & (n_loc - 1)) * blk + (ids // n_loc) * cap
        return jnp.where(pos < cap, spot.astype(F32) + pos, float(n_exp * cap))

    s1r[...] = place(ids1, pos1)
    s2r[...] = place(ids2, pos2)

    def masks(j):
        spot = (lax.broadcasted_iota(I32, (blk, n_tok), 0) + j * blk).astype(F32)
        return s1r[...] == spot, s2r[...] == spot

    def send_rows(src, dst, send_sem, recv_sem, j):
        for d in range(1, ep_size):
            q = (r + d) % ep_size
            pltpu.make_async_remote_copy(
                src_ref=src.at[j, q], dst_ref=dst.at[j, my_place],
                send_sem=send_sem, recv_sem=recv_sem.at[j],
                device_id=(k, q), device_id_type=MESH,
            ).start()

    def wait_recv(view, sem):
        pltpu.make_async_remote_copy(
            src_ref=view, dst_ref=view, send_sem=sem, recv_sem=sem, device_id=(k, r), device_id_type=MESH
        ).wait_recv()

    def wait_send(view, sem):
        pltpu.make_async_remote_copy(
            src_ref=view, dst_ref=view, send_sem=sem, recv_sem=sem, device_id=(k, r), device_id_type=MESH
        ).wait_send()

    ins[0].wait()
    pl.semaphore_wait(barrier, n_dev - 1)

    @pl.loop(0, n_loc)
    def _(j):
        m1, m2 = masks(j)
        pick = jnp.where(m1 | m2, 1.0, 0.0).astype(BF)
        for c in range(0, width, 512):
            rows = dot(pick, x_v[:, c:c + 512]).astype(BF)
            xs[j, :, :, c:c + 512] = rows.reshape(ep_size, cap, 512)
        send_rows(xs, xr, xs_sem, xr_sem, j)
        xr[j, my_place] = xs[j, r]

    def column(row):
        return jnp.transpose(jnp.broadcast_to(row, (128, n_tok)))

    s1c[...] = column(s1r[...])
    s2c[...] = column(s2r[...])
    i1c[...] = column(ids1.astype(F32))
    i2c[...] = column(ids2.astype(F32))
    ins[2].wait()
    wr_hi, wr_mid, wr_low = split3(wr_v[...])
    xv = x_v[...]
    logits = dot(xv, wr_hi, NT) + (dot(xv, wr_mid, NT) + dot(xv, wr_low, NT))
    ex = jnp.exp(logits - jnp.max(logits, axis=1, keepdims=True))
    prob = ex / jnp.sum(ex, axis=1, keepdims=True)
    prob_v[...] = prob
    lane = lax.broadcasted_iota(I32, (n_tok, n_exp), 1).astype(F32)
    q1 = jnp.sum(jnp.where(i1c[:, :n_exp] == lane, prob, 0.0), axis=1, keepdims=True)
    q2 = jnp.sum(jnp.where(i2c[:, :n_exp] == lane, prob, 0.0), axis=1, keepdims=True)
    g1 = jnp.broadcast_to(q1 / (q1 + q2), (n_tok, 128))
    g2 = jnp.broadcast_to(q2 / (q1 + q2), (n_tok, 128))
    g1c[...] = g1
    g2c[...] = g2
    q1c[...] = jnp.broadcast_to(q1, (n_tok, 128))
    q2c[...] = jnp.broadcast_to(q2, (n_tok, 128))
    g1r[...] = jnp.transpose(g1)[0:1, :]
    g2r[...] = jnp.transpose(g2)[0:1, :]
    ins[1].wait()

    @pl.loop(0, n_loc)
    def _(j):
        m1, m2 = masks(j)
        pick = jnp.where(m1 | m2, 1.0, 0.0).astype(BF)
        gate = jnp.sum(jnp.where(m1, g1r[...], 0.0) + jnp.where(m2, g2r[...], 0.0), axis=1, keepdims=True)
        for c in range(0, width, 512):
            rows = (gate * dot(pick, dy_v[:, c:c + 512])).astype(BF)
            ds[j, :, :, c:c + 512] = rows.reshape(ep_size, cap, 512)
        send_rows(ds, dr, ds_sem, dr_sem, j)
        dr[j, my_place] = ds[j, r]

    def send_half(src, dst, send_sem, recv_sem, j):
        pltpu.make_async_remote_copy(
            src_ref=src.at[j, pl.ds(other * half, half)], dst_ref=dst.at[j],
            send_sem=send_sem, recv_sem=recv_sem.at[j],
            device_id=(other, r), device_id_type=MESH,
        ).start()

    def merge_and_return(src, got, got_sem, dst, send_sem, recv_sem, j):
        wait_recv(got.at[j], got_sem.at[j])
        mine = pl.ds(k * half, half)
        src[j, mine] = (src[j, mine].astype(F32) + got[j].astype(F32)).astype(BF)
        for d in range(half):
            c = (r // tp_size + d) % half
            q = tp_size * c + k

            @pl.when(q != r)
            def _():
                pltpu.make_async_remote_copy(
                    src_ref=src.at[j, k * half + c], dst_ref=dst.at[j, r],
                    send_sem=send_sem, recv_sem=recv_sem.at[j],
                    device_id=(k, q), device_id_type=MESH,
                ).start()

            @pl.when(q == r)
            def _():
                dst[j, r] = src[j, k * half + c]

    @pl.loop(0, n_loc)
    def _(j):
        for c in weight_copies(j):
            c.wait()
        wait_recv(xr.at[j, pl.ds(0, ep_size - 1)], xr_sem.at[j])
        rows = xr[j].reshape(blk, width)
        pa = dot(rows, wa_v[j])
        pb = dot(rows, wb_v[j])
        th = jnp.tanh(GELU_COEF * (pa + 0.044715 * pa * pa * pa))
        gv = 0.5 * pa * (1.0 + th)
        slope = 0.5 * (1.0 + th) + 0.5 * pa * (1.0 - th * th) * GELU_COEF * (1.0 + 0.134145 * pa * pa)
        gv_v[j] = gv
        bs_v[j] = pb * slope
        hidden = (gv * pb).astype(BF)
        h_v[j] = hidden
        for c in range(0, width, 512):
            ps[j, :, :, c:c + 512] = dot(hidden, wc_v[j, :, c:c + 512]).astype(BF).reshape(ep_size, cap, 512)
        send_half(ps, pr, ps_sem, pr_sem, j)

        @pl.when(j > 0)
        def _():
            merge_and_return(ps, pr, pr_sem, orr, os_sem, or_sem, j - 1)

    merge_and_return(ps, pr, pr_sem, orr, os_sem, or_sem, n_loc - 1)

    wait_send(xs.at[:, pl.ds(0, ep_size - 1)], xs_sem)

    @pl.loop(0, n_loc)
    def _(j):
        wait_recv(dr.at[j, pl.ds(0, ep_size - 1)], dr_sem.at[j])
        rows = dr[j].reshape(blk, width)
        dh = dot(rows, wc_v[j], NT)
        da = (dh * bs_v[j]).astype(BF)
        db = (dh * gv_v[j]).astype(BF)
        da_v[j] = da
        db_v[j] = db
        for c in range(0, width, 512):
            part = dot(da, wa_v[j, c:c + 512, :], NT) + dot(db, wb_v[j, c:c + 512, :], NT)
            xs[j, :, :, c:c + 512] = part.astype(BF).reshape(ep_size, cap, 512)
        send_half(xs, pdr, pds_sem, pdr_sem, j)

        @pl.when(j > 0)
        def _():
            merge_and_return(xs, pdr, pdr_sem, dxr, dxs_sem, dxr_sem, j - 1)

    merge_and_return(xs, pdr, pdr_sem, dxr, dxs_sem, dxr_sem, n_loc - 1)

    outs = [
        pltpu.make_async_copy(xr, xe_out, out_sem.at[0]),
        pltpu.make_async_copy(dr, de_out, out_sem.at[1]),
        pltpu.make_async_copy(h_v, h_out, out_sem.at[2]),
        pltpu.make_async_copy(da_v, da_out, out_sem.at[3]),
        pltpu.make_async_copy(db_v, db_out, out_sem.at[4]),
    ]
    for c in outs:
        c.start()

    tb = 128
    n_tb = n_tok // tb

    def spots(col, toks):
        lanes = lax.broadcasted_iota(I32, (tb, 128), 1).astype(F32)
        base = col[toks, :]
        return jnp.concatenate([base == lanes + float(u * 128) for u in range(n_exp * cap // 128)], axis=1)

    def ship(buf, toks, send_sem, recv_sem):
        pltpu.make_async_remote_copy(
            src_ref=buf.at[toks], dst_ref=buf.at[toks], send_sem=send_sem, recv_sem=recv_sem,
            device_id=(other, r), device_id_type=MESH,
        ).start()

    @pl.when(owner)
    def _():
        @pl.loop(0, n_loc)
        def _(j):
            wait_recv(orr.at[j, pl.ds(0, ep_size - 1)], or_sem.at[j])

        @pl.loop(0, n_tb)
        def _(t):
            toks = pl.ds(pl.multiple_of(t * tb, tb), tb)
            pick1 = jnp.where(spots(s1c, toks), 1.0, 0.0).astype(BF)
            pick2 = jnp.where(spots(s2c, toks), 1.0, 0.0).astype(BF)
            dg1 = jnp.zeros((tb, 1), F32)
            dg2 = jnp.zeros((tb, 1), F32)
            ga = g1c[toks, 0:1]
            gb = g2c[toks, 0:1]
            for c in range(0, width, 512):
                rows = orr[:, :, :, c:c + 512].reshape(n_exp * cap, 512)
                o1 = dot(pick1, rows)
                o2 = dot(pick2, rows)
                y_v[toks, c:c + 512] = (ga * o1 + gb * o2).astype(BF)
                dyf = dy_v[toks, c:c + 512].astype(F32)
                dg1 = dg1 + jnp.sum(dyf * o1, axis=1, keepdims=True)
                dg2 = dg2 + jnp.sum(dyf * o2, axis=1, keepdims=True)
            ship(y_v, toks, ys_sem, yr_sem)
            qa = q1c[toks, 0:1]
            qb = q2c[toks, 0:1]
            shared = dg1 * ga + dg2 * gb
            dq1 = (dg1 - shared) / (qa + qb)
            dq2 = (dg2 - shared) / (qa + qb)
            centre = dq1 * qa + dq2 * qb
            lanes = lax.broadcasted_iota(I32, (tb, n_exp), 1).astype(F32)
            pull = jnp.where(i1c[toks, :n_exp] == lanes, dq1, 0.0) + jnp.where(i2c[toks, :n_exp] == lanes, dq2, 0.0)
            dl_v[toks, :] = prob_v[toks, :] * (pull - centre)

        d_hi, d_mid, d_low = split3(dl_v[...])
        for c in range(0, width, 512):
            xc = x_v[:, c:c + 512]
            piece = dot(d_hi, xc, TN) + (dot(d_mid, xc, TN) + dot(d_low, xc, TN))
            dwp[:, :, c:c + 512] = piece.reshape(ep_size, n_loc, 512)
        for d in range(1, ep_size):
            q = (r + d) % ep_size
            pltpu.make_async_remote_copy(
                src_ref=dwp.at[q], dst_ref=dwi.at[r], send_sem=rs_sem, recv_sem=rr_sem,
                device_id=(q % tp_size, q), device_id_type=MESH,
            ).start()
        dwi[r] = dwp[r]

        @pl.loop(0, n_loc)
        def _(j):
            wait_recv(dxr.at[j, pl.ds(0, ep_size - 1)], dxr_sem.at[j])

        @pl.loop(0, n_tb)
        def _(t):
            toks = pl.ds(pl.multiple_of(t * tb, tb), tb)
            pick = jnp.where(spots(s1c, toks) | spots(s2c, toks), 1.0, 0.0).astype(BF)
            dl = dl_v[toks, :]
            for c in range(0, width, 512):
                rows = dxr[:, :, :, c:c + 512].reshape(n_exp * cap, 512)
                back = dot(pick, rows)
                router = lax.dot_general(
                    dl, wr_v[:, c:c + 512], NN, precision=lax.Precision.HIGHEST, preferred_element_type=F32
                )
                dx_v[toks, c:c + 512] = (back + router).astype(BF)
            ship(dx_v, toks, dys_sem, dyr_sem)

        wait_recv(dwi.at[pl.ds(0, ep_size - 1)], rr_sem)
        total = dwi[0]
        for q in range(1, ep_size):
            total = total + dwi[q]
        dwf[r] = total
        for d in range(1, n_dev):
            flat = (k * ep_size + r + d) % n_dev
            pltpu.make_async_remote_copy(
                src_ref=dwf.at[r], dst_ref=dwf.at[r], send_sem=fs_sem, recv_sem=fr_sem,
                device_id=(flat // ep_size, flat % ep_size), device_id_type=MESH,
            ).start()
        wait_recv(dwf.at[pl.ds(0, ep_size - 1)], fr_sem)
        wait_send(dwp.at[pl.ds(0, ep_size - 1)], rs_sem)
        for half_sends in range(n_dev - 1):
            wait_send(dwf.at[r], fs_sem)
        wait_send(y_v, ys_sem)
        wait_send(dx_v, dys_sem)
        wait_send(orr.at[:, pl.ds(0, half - 1)], os_sem)
        wait_send(dxr.at[:, pl.ds(0, half - 1)], dxs_sem)

    @pl.when(jnp.logical_not(owner))
    def _():
        wait_recv(y_v, yr_sem)
        wait_recv(dx_v, dyr_sem)
        wait_recv(dwf, fr_sem)
        wait_send(orr.at[:, pl.ds(0, half)], os_sem)
        wait_send(dxr.at[:, pl.ds(0, half)], dxs_sem)

    finals = [
        pltpu.make_async_copy(y_v, y_out, in_sem.at[0]),
        pltpu.make_async_copy(dx_v, dx_out, in_sem.at[1]),
        pltpu.make_async_copy(dwf, dwr_out, in_sem.at[2]),
    ]
    for c in finals:
        c.start()
    wait_send(ds.at[:, pl.ds(0, ep_size - 1)], ds_sem)
    wait_send(ps.at[:, pl.ds(0, half)], ps_sem)
    wait_send(xs.at[:, pl.ds(0, half)], pds_sem)
    for c in outs + finals:
        c.wait()


def weight_kernel(xe, de, h, da, db, ga_out, gb_out, gc_out):
    rows = xe[0]
    ga_out[0] = dot(rows, da[0], TN)
    gb_out[0] = dot(rows, db[0], TN)
    gc_out[0] = dot(h[0], de[0], TN)


def solution(mesh):
    tp_size = mesh.shape["tp"]
    ep_size = mesh.shape["ep"]

    def local_step(x_rows, w_router, first_ids, second_ids, w_gelu, w_lin, w_out, dy_rows):
        n_tok, width = x_rows.shape
        n_exp = w_router.shape[1]
        n_loc, _, hid = w_gelu.shape
        cap = 2 * n_tok // n_exp
        blk = ep_size * cap
        half = ep_size // tp_size
        dma = pltpu.SemaphoreType.DMA
        any_spec = pl.BlockSpec(memory_space=pl.ANY)
        vmem_spec = pl.BlockSpec(memory_space=pltpu.VMEM)
        sds = jax.ShapeDtypeStruct
        rows_shape = (n_loc, ep_size, cap, width)
        half_shape = (n_loc, half, cap, width)
        hid_shape = (n_loc, blk, hid)
        col = pltpu.VMEM((n_tok, 128), F32)
        row = pltpu.VMEM((1, n_tok), F32)
        outs = pl.pallas_call(
            functools.partial(moe_kernel, tp_size, ep_size, cap),
            name="moe",
            in_specs=[vmem_spec] * 2 + [any_spec] * 6,
            out_specs=[any_spec] * 8,
            out_shape=[
                sds((n_tok, width), BF), sds((n_tok, width), BF), sds((ep_size, n_loc, width), F32),
                sds(rows_shape, BF), sds(rows_shape, BF), sds(hid_shape, BF), sds(hid_shape, BF), sds(hid_shape, BF),
            ],
            scratch_shapes=[
                pltpu.VMEM((n_tok, width), BF), pltpu.VMEM((n_tok, width), BF), pltpu.VMEM((n_exp, width), F32),
                pltpu.VMEM((n_loc, width, hid), BF), pltpu.VMEM((n_loc, width, hid), BF), pltpu.VMEM((n_loc, hid, width), BF),
                pltpu.VMEM(rows_shape, BF), pltpu.VMEM(rows_shape, BF), pltpu.VMEM(rows_shape, BF), pltpu.VMEM(rows_shape, BF),
                pltpu.VMEM(hid_shape, BF), pltpu.VMEM(hid_shape, BF), pltpu.VMEM(hid_shape, BF),
                pltpu.VMEM(hid_shape, F32), pltpu.VMEM(hid_shape, F32),
                pltpu.VMEM(rows_shape, BF), pltpu.VMEM(half_shape, BF), pltpu.VMEM(half_shape, BF),
                pltpu.VMEM(rows_shape, BF), pltpu.VMEM(rows_shape, BF),
                pltpu.VMEM((n_tok, width), BF), pltpu.VMEM((n_tok, width), BF),
                row, row, row, row, col, col, col, col, col, col, col, col,
                pltpu.VMEM((n_tok, n_exp), F32), pltpu.VMEM((n_tok, n_exp), F32),
                pltpu.VMEM((ep_size, n_loc, width), F32), pltpu.VMEM((ep_size, n_loc, width), F32),
                pltpu.VMEM((ep_size, n_loc, width), F32),
                dma((3,)), dma((3, n_loc)), dma((5,)),
                dma(()), dma((n_loc,)), dma(()), dma((n_loc,)),
                dma(()), dma((n_loc,)), dma(()), dma((n_loc,)),
                dma(()), dma((n_loc,)), dma(()), dma((n_loc,)),
                dma(()), dma(()), dma(()), dma(()),
                dma(()), dma(()), dma(()), dma(()),
            ],
            compiler_params=pltpu.CompilerParams(
                collective_id=0, has_side_effects=True, vmem_limit_bytes=67043328
            ),
        )(
            first_ids.reshape(1, n_tok), second_ids.reshape(1, n_tok), x_rows, dy_rows, w_router.T,
            w_gelu, w_lin, w_out,
        )
        act_out, grad_in, grad_router, xe, de, h, da, db = outs
        xe = xe.reshape(n_loc, blk, width)
        de = de.reshape(n_loc, blk, width)

        def spec(*shape):
            return pl.BlockSpec((1,) + shape, lambda e: (e, 0, 0))

        grad_wa, grad_wb, grad_wc = pl.pallas_call(
            weight_kernel,
            name="weight_grads",
            grid=(n_loc,),
            in_specs=[spec(blk, width), spec(blk, width), spec(blk, hid), spec(blk, hid), spec(blk, hid)],
            out_specs=[spec(width, hid), spec(width, hid), spec(hid, width)],
            out_shape=[
                sds((n_loc, width, hid), F32), sds((n_loc, width, hid), F32), sds((n_loc, hid, width), F32),
            ],
            compiler_params=pltpu.CompilerParams(
                dimension_semantics=("arbitrary",), vmem_limit_bytes=40 * 1024 * 1024
            ),
        )(xe, de, h, da, db)
        return act_out, grad_in, grad_wa, grad_wb, grad_wc, grad_router.reshape(n_exp, width).T

    return jax.shard_map(
        local_step,
        mesh=mesh,
        in_specs=(P("ep", None), P(), P("ep"), P("ep"), P("ep", None, "tp"), P("ep", None, "tp"), P("ep", "tp", None), P("ep", None)),
        out_specs=(P("ep", None), P("ep", None), P("ep", None, "tp"), P("ep", None, "tp"), P("ep", "tp", None), P()),
        check_vma=False,
    )
```

time: 488 us -> 162 us (0.33); the launches traced: 479 us -> 162 us
  waiting for transfers between devices: 216 us -> 0 us
  Pallas kernels: 0 us -> 150 us
  blocking collectives: 83.9 us -> 0 us
  local copies, waits for them, and re-layouts: 76.6 us -> 10.8 us
  matrix products: 44 us -> 0 us
  other arithmetic: 34 us -> 0 us
  between operations: 14.8 us -> 0.66 us
  starting transfers between devices: 9.72 us -> 0 us
    all_gather x2 -> x0, waiting for transfers between devices: 156 us -> none  [the longest x1 78.5 us: local_step(): lax.all_gather(part_out, 'tp').astype(jnp.float32)]
    pallas_call x0 -> x2, Pallas kernels: none -> 150 us  [the longest x1 137 us: local_step(): pl.pallas_call(functools.partial(moe_kernel, tp_size, ep_size, cap), name...]
    all_to_all x2 -> x0, blocking collectives: 83.9 us -> none  [the longest x1 43.2 us: local_step(): disp_exp = lax.all_to_all(disp_tok, 'ep', 0, 1, tiled=True)]
    dot_general x12 -> x0, matrix products: 44 us -> none  [the longest x1 6.62 us: local_step(): jnp.einsum('erd,erf->edf', disp_exp, grad_b, preferred_element_type=jnp.f...]
    all_to_all x2 -> x0, waiting for transfers between devices: 41.5 us -> none  [the longest x1 27.8 us: local_step(): lax.all_to_all(merged, 'ep', 1, 0, tiled=True)]
    gather x6 -> x0, local copies, waits for them, and re-layouts: 37.1 us -> none  [the longest x1 6.74 us: combine_tokens(): jnp.take(grad_tok, slot_one, axis=0, mode='fill', fill_value=0)]
    psum x1 -> x0, waiting for transfers between devices: 18.7 us -> none  [local_step(): lax.psum(jnp.einsum('sd,se->de', x_part, logit_part, precision=lax.Precis...]
    reduce_sum x7 -> x0, other arithmetic: 18.2 us -> none  [the longest x1 6.58 us: local_step(): jnp.sum(lax.all_gather(part_out, 'tp').astype(jnp.float32), axis=0)]
  transfers between devices with their start and end apart: 5 -> 0, of which waited for: 5 -> 0; matrix products, arithmetic and copies ran while one was open for 12% -> 0% of each run, Pallas kernels for 0% -> 0%
where the time goes in v1:
time: 162 us
  Pallas kernels  150 us (93%)
  local copies, waits for them, and re-layouts  10.8 us (7%)
    pallas_call x1, Pallas kernels, local_step(): pl.pallas_call(functools.partial(moe_kernel, tp_size, ep_size, cap), name...  137 us
    pallas_call x1, Pallas kernels, local_step(): pl.pallas_call(weight_kernel, name='weight_grads', grid=(n_loc,), in_spec...  12.7 us
    unnamed x19, local copies, waits for them, and re-layouts  10.8 us

profile of v1, /device:TPU:0, one launch (start us, length us, event | category | flops | bytes accessed | tf_op | source)
XLA Modules:
  0.0 161.6 jit_solution(8742823579973467296)
XLA Ops:
  0.6 137.4 %moe.1 = (bf16[512,1536]{1,0:T(8,128)(2,1)}, bf16[512,1536]{1,0:T(8,128)(2,1)}, f32[8,8,1536]{2,1,0:T(8,128)}, bf16[8,8,16,1536]{3,2,1,0:T(8,128)(2,1)}, bf16[8,...) custom-call(s32[1,512]{1,0:T(1,128)} %bitcast.12, ...), custom_call_target="tpu_custom_call" | custom-call | tf_op jit(solution)/shard_map/moe/pallas_call | solution.py:414
  138.0 0.0 copy-start
  138.0 1.9 %copy-done = bf16[8,8,16,1536]{3,2,1,0:T(8,128)(2,1)S(1)} copy-done((bf16[8,8,16,1536]{3,2,1,0:T(8,128)(2,1)S(1)}, bf16[8,8,16,1536]{3,2,1,0:T(8,128)(2,1)}, u32[]{:S(2)}) %copy-start) | copy-done | bytes 3145752
  139.9 0.0 copy-start.1
  139.9 1.9 %copy-done.1 = bf16[8,8,16,1536]{3,2,1,0:T(8,128)(2,1)S(1)} copy-done((bf16[8,8,16,1536]{3,2,1,0:T(8,128)(2,1)S(1)}, bf16[8,8,16,1536]{3,2,1,0:T(8,128)(2,1)}, u32[]{:S(2)}) %copy-start.1) | copy-done | bytes 3145752
  141.8 0.0 copy-start.2
  141.8 1.0 copy-done.2
  142.9 0.0 copy-start.3
  142.9 1.0 copy-done.3
  143.9 0.0 copy-start.4
  143.9 1.0 copy-done.4
  144.9 0.0 copy-start.6
  144.9 12.7 %weight_grads.1 = (f32[8,1536,256]{2,1,0:T(8,128)}, f32[8,1536,256]{2,1,0:T(8,128)}, f32[8,256,1536]{2,1,0:T(8,128)}) custom-call(bf16[8,128,1536]{2,1,0:T(8,128)(2,1)S(1)} %bitcast.8, bf16[8,128,1536]{2,1,0:T(8,128)(2,1)S(1)} %bitcast.9, bf16[8,128,256]{2,1,0:T(8,128)(2,1)S(1)} %copy-done.2, bf16[8,128,256]{2,1,0:T(8,128)(2,1)S(1)} %copy-done.3, ...), custom_call_target="tpu_custom_call" | custom-call | tf_op jit(solution)/shard_map/weight_grads/pallas_call | solution.py:457
  157.7 0.0 copy-start.5
  157.7 0.0 copy-done.6
  157.7 0.0 copy-start.7
  157.7 1.1 copy.17
  158.8 0.8 copy-done.5
  159.7 1.1 copy.18
  160.8 0.0 copy-done.7
  160.8 0.7 copy.19
Async XLA Ops:
  138.0 1.9 %copy-start = (bf16[8,8,16,1536]{3,2,1,0:T(8,128)(2,1)S(1)}, bf16[8,8,16,1536]{3,2,1,0:T(8,128)(2,1)}, u32[]{:S(2)}) copy-start(bf16[8,8,16,1536]{3,2,1,0:T(8,128)(2,1)} %get-tuple-element.19) | copy-start | bytes 9437188
  139.9 1.9 %copy-start.1 = (bf16[8,8,16,1536]{3,2,1,0:T(8,128)(2,1)S(1)}, bf16[8,8,16,1536]{3,2,1,0:T(8,128)(2,1)}, u32[]{:S(2)}) copy-start(bf16[8,8,16,1536]{3,2,1,0:T(8,128)(2,1)} %get-tuple-element.20) | copy-start | bytes 9437188
  141.8 1.0 copy-start.2
  142.9 1.0 copy-start.3
  143.9 1.0 copy-start.4
  144.9 12.8 %copy-start.6 = (bf16[512,1536]{1,0:T(8,128)(2,1)S(1)}, bf16[512,1536]{1,0:T(8,128)(2,1)}, u32[]{:S(2)}) copy-start(bf16[512,1536]{1,0:T(8,128)(2,1)} %get-tuple-element.34) | copy-start | bytes 4718596
  157.7 2.0 %copy-start.5 = (bf16[512,1536]{1,0:T(8,128)(2,1)S(1)}, bf16[512,1536]{1,0:T(8,128)(2,1)}, u32[]{:S(2)}) copy-start(bf16[512,1536]{1,0:T(8,128)(2,1)} %get-tuple-element.35) | copy-start | bytes 4718596
  157.7 3.1 %copy-start.7 = (f32[8,8,1536]{2,1,0:T(8,128)S(1)}, f32[8,8,1536]{2,1,0:T(8,128)}, u32[]{:S(2)}) copy-start(f32[8,8,1536]{2,1,0:T(8,128)} %get-tuple-element.27) | copy-start | bytes 1179652

commit v2 on v1

--- a/solution.py
+++ b/solution.py
@@ -42,7 +42,7 @@
     xs_sem, xr_sem, ds_sem, dr_sem,
     ps_sem, pr_sem, pds_sem, pdr_sem,
     os_sem, or_sem, dxs_sem, dxr_sem,
-    ys_sem, yr_sem, dys_sem, dyr_sem,
+    ys_sem, yr_sem,
     rs_sem, rr_sem, fs_sem, fr_sem,
 ):
     k = lax.axis_index("tp")
@@ -328,6 +328,17 @@
         def _(j):
             wait_recv(dxr.at[j, pl.ds(0, ep_size - 1)], dxr_sem.at[j])
 
+        wait_recv(dwi.at[pl.ds(0, ep_size - 1)], rr_sem)
+        total = dwi[0]
+        for q in range(1, ep_size):
+            total = total + dwi[q]
+        dwf[r] = total
+        for d in range(1, n_dev):
+            flat = (k * ep_size + r + d) % n_dev
+            pltpu.make_async_remote_copy(
+                src_ref=dwf.at[r], dst_ref=dwf.at[r], send_sem=fs_sem, recv_sem=fr_sem,
+                device_id=(flat // ep_size, flat % ep_size), device_id_type=MESH,
+            ).start()
         @pl.loop(0, n_tb)
         def _(t):
             toks = pl.ds(pl.multiple_of(t * tb, tb), tb)
@@ -340,43 +351,32 @@
                     dl, wr_v[:, c:c + 512], NN, precision=lax.Precision.HIGHEST, preferred_element_type=F32
                 )
                 dx_v[toks, c:c + 512] = (back + router).astype(BF)
-            ship(dx_v, toks, dys_sem, dyr_sem)
-
-        wait_recv(dwi.at[pl.ds(0, ep_size - 1)], rr_sem)
-        total = dwi[0]
-        for q in range(1, ep_size):
-            total = total + dwi[q]
-        dwf[r] = total
-        for d in range(1, n_dev):
-            flat = (k * ep_size + r + d) % n_dev
-            pltpu.make_async_remote_copy(
-                src_ref=dwf.at[r], dst_ref=dwf.at[r], send_sem=fs_sem, recv_sem=fr_sem,
-                device_id=(flat // ep_size, flat % ep_size), device_id_type=MESH,
-            ).start()
+            pltpu.make_async_copy(dx_v.at[toks], dx_out.at[toks], in_sem.at[1]).start()
+
         wait_recv(dwf.at[pl.ds(0, ep_size - 1)], fr_sem)
         wait_send(dwp.at[pl.ds(0, ep_size - 1)], rs_sem)
         for half_sends in range(n_dev - 1):
             wait_send(dwf.at[r], fs_sem)
         wait_send(y_v, ys_sem)
-        wait_send(dx_v, dys_sem)
         wait_send(orr.at[:, pl.ds(0, half - 1)], os_sem)
         wait_send(dxr.at[:, pl.ds(0, half - 1)], dxs_sem)
 
     @pl.when(jnp.logical_not(owner))
     def _():
+        dx_v[...] = jnp.zeros_like(dx_v)
+        pltpu.make_async_copy(dx_v, dx_out, in_sem.at[1]).start()
         wait_recv(y_v, yr_sem)
-        wait_recv(dx_v, dyr_sem)
         wait_recv(dwf, fr_sem)
         wait_send(orr.at[:, pl.ds(0, half)], os_sem)
         wait_send(dxr.at[:, pl.ds(0, half)], dxs_sem)
 
     finals = [
         pltpu.make_async_copy(y_v, y_out, in_sem.at[0]),
-        pltpu.make_async_copy(dx_v, dx_out, in_sem.at[1]),
         pltpu.make_async_copy(dwf, dwr_out, in_sem.at[2]),
     ]
     for c in finals:
         c.start()
+    finals.append(pltpu.make_async_copy(dx_v, dx_out, in_sem.at[1]))
     wait_send(ds.at[:, pl.ds(0, ep_size - 1)], ds_sem)
     wait_send(ps.at[:, pl.ds(0, half)], ps_sem)
     wait_send(xs.at[:, pl.ds(0, half)], pds_sem)
@@ -437,7 +437,7 @@
                 dma(()), dma((n_loc,)), dma(()), dma((n_loc,)),
                 dma(()), dma((n_loc,)), dma(()), dma((n_loc,)),
                 dma(()), dma((n_loc,)), dma(()), dma((n_loc,)),
-                dma(()), dma(()), dma(()), dma(()),
+                dma(()), dma(()),
                 dma(()), dma(()), dma(()), dma(()),
             ],
             compiler_params=pltpu.CompilerParams(
@@ -448,6 +448,12 @@
             w_gelu, w_lin, w_out,
         )
         act_out, grad_in, grad_router, xe, de, h, da, db = outs
+        partners = [
+            ((q % tp_size) * ep_size + q, (1 - q % tp_size) * ep_size + q) for q in range(ep_size)
+        ]
+        passed = lax.ppermute(grad_in, ("tp", "ep"), partners)
+        owner = lax.axis_index("ep") % tp_size == lax.axis_index("tp")
+        grad_in = jnp.where(owner, grad_in, passed)
         xe = xe.reshape(n_loc, blk, width)
         de = de.reshape(n_loc, blk, width)
 
@@ -464,7 +470,11 @@
                 sds((n_loc, width, hid), F32), sds((n_loc, width, hid), F32), sds((n_loc, hid, width), F32),
             ],
             compiler_params=pltpu.CompilerParams(
-                dimension_semantics=("arbitrary",), vmem_limit_bytes=40 * 1024 * 1024
+                dimension_semantics=("arbitrary",), vmem_limit_bytes=67043328
+            ),
+            cost_estimate=pl.CostEstimate(
+                flops=6 * n_loc * blk * width * hid, transcendentals=0,
+                bytes_accessed=12 * n_loc * width * hid + 4 * n_loc * blk * width + 6 * n_loc * blk * hid,
             ),
         )(xe, de, h, da, db)
         return act_out, grad_in, grad_wa, grad_wb, grad_wc, grad_router.reshape(n_exp, width).T

time: 162 us -> 151 us (0.932)
  Pallas kernels: 150 us -> 140 us
  local copies, waits for them, and re-layouts: 10.8 us -> 1.98 us
  starting transfers between devices: 0 us -> 4.01 us
  other arithmetic: 0 us -> 2.72 us
    pallas_call x1, Pallas kernels: 137 us -> 124 us  [local_step(): pl.pallas_call(functools.partial(moe_kernel, tp_size, ep_size, cap), name...]
    unnamed x19 -> x6, local copies, waits for them, and re-layouts: 10.8 us -> 1.98 us
    ppermute x0 -> x1, starting transfers between devices: none -> 4.01 us  [local_step(): passed = lax.ppermute(grad_in, ('tp', 'ep'), partners)]
    pallas_call x1, Pallas kernels: 12.7 us -> 15.5 us  [local_step(): pl.pallas_call(weight_kernel, name='weight_grads', grid=(n_loc,), in_spec...]
    select_n x0 -> x1, other arithmetic: none -> 2.72 us  [local_step(): grad_in = jnp.where(owner, grad_in, passed)]
  transfers between devices with their start and end apart: 0 -> 1, of which waited for: 0 -> 1; matrix products, arithmetic and copies ran while one was open for 0% -> 0% of each run, Pallas kernels for 0% -> 10%
where the time goes in v2:
time: 151 us; the launch traced here: 150 us
  Pallas kernels  140 us (93%)
  starting transfers between devices  4.01 us (3%)
  other arithmetic  2.72 us (2%)
  local copies, waits for them, and re-layouts  1.98 us (1%)
    pallas_call x1, Pallas kernels, local_step(): pl.pallas_call(functools.partial(moe_kernel, tp_size, ep_size, cap), name...  124 us
    pallas_call x1, Pallas kernels, local_step(): pl.pallas_call(weight_kernel, name='weight_grads', grid=(n_loc,), in_spec...  15.5 us
    ppermute x1, starting transfers between devices, local_step(): passed = lax.ppermute(grad_in, ('tp', 'ep'), partners)  4.01 us
  transfers between devices with their start and end apart: 1, of which 1 were waited for; matrix products, arithmetic and copies ran while one was open for 0% of the time, Pallas kernels for 10%

profile of v2, /device:TPU:0, one launch (start us, length us, event | category | flops | bytes accessed | tf_op | source)
XLA Modules:
  0.0 150.2 jit_solution(10716432163788416404)
XLA Ops:
  0.6 124.1 %moe.1 = (bf16[512,1536]{1,0:T(8,128)(2,1)}, bf16[512,1536]{1,0:T(8,128)(2,1)}, f32[8,8,1536]{2,1,0:T(8,128)}, bf16[8,8,16,1536]{3,2,1,0:T(8,128)(2,1)}, bf16[8,...) custom-call(s32[1,512]{1,0:T(1,128)} %bitcast.10, ...), custom_call_target="tpu_custom_call" | custom-call | tf_op jit(solution)/shard_map/moe/pallas_call | solution.py:414
  124.8 4.0 %collective-permute-start = (bf16[512,1536]{1,0:T(8,128)(2,1)}, bf16[512,1536]{1,0:T(8,128)(2,1)}, u32[]{:S(2)}, u32[]{:S(2)}) collective-permute-start(bf16[512,1536]{1,0:T(8,128)(2,1)} %get-tuple-element.18), channel_id=1, source_target_pairs={{0,8},{9,1},{2,10},{11,3},{4,12},{13,5},{6,14},{15,7}} | collective-permute-start | bytes 4718600 | tf_op jit(solution)/shard_map/ppermute | solution.py:454
  128.8 15.5 %weight_grads.1 = (f32[8,1536,256]{2,1,0:T(8,128)}, f32[8,1536,256]{2,1,0:T(8,128)}, f32[8,256,1536]{2,1,0:T(8,128)}) custom-call(bf16[8,128,1536]{2,1,0:T(8,128)(2,1)} %bitcast.12, bf16[8,128,1536]{2,1,0:T(8,128)(2,1)} %bitcast.13, bf16[8,128,256]{2,1,0:T(8,128)(2,1)} %get-tuple-element.21.h, bf16[8,128,256]{2,1,0:T(8,128)(2,1)} %get-tuple-element.22.da, ...), custom_call_target="tpu_custom_call" | custom-call | flops 2415919104 | bytes 45613056 | tf_op jit(solution)/shard_map/weight_grads/pallas_call | solution.py:463
  144.3 0.0 copy-start
  144.3 1.2 collective-permute-done
  145.5 2.7 %broadcast_select_fusion = bf16[512,1536]{1,0:T(8,128)(2,1)} fusion(bf16[512,1536]{1,0:T(8,128)(2,1)} %get-tuple-element.18, bf16[512,1536]{1,0:T(8,128)(2,1)} %collective-permute-done, pred[]{:T(512)S(6)} %eq.5), kind=kLoop, calls=%fused_computation | loop fusion | flops 786432 | bytes 4718593 | tf_op jit(solution)/shard_map/jit(_where)/select_n | solution.py:456
  148.2 0.0 copy-done
  148.2 0.0 copy-start.1
  148.2 1.1 copy.16
  149.4 0.1 copy-done.1
  149.4 0.7 copy.17
Async XLA Ops:
  124.8 20.7 %collective-permute-start = (bf16[512,1536]{1,0:T(8,128)(2,1)}, bf16[512,1536]{1,0:T(8,128)(2,1)}, u32[]{:S(2)}, u32[]{:S(2)}) collective-permute-start(bf16[512,1536]{1,0:T(8,128)(2,1)} %get-tuple-element.18), channel_id=1, source_target_pairs={{0,8},{9,1},{2,10},{11,3},{4,12},{13,5},{6,14},{15,7}} | collective-permute-start | bytes 4718600 | tf_op jit(solution)/shard_map/ppermute | solution.py:454
  144.3 4.0 %copy-start = (bf16[512,1536]{1,0:T(8,128)(2,1)S(1)}, bf16[512,1536]{1,0:T(8,128)(2,1)}, u32[]{:S(2)}) copy-start(bf16[512,1536]{1,0:T(8,128)(2,1)} %get-tuple-element.34) | copy-start | bytes 4718596
  148.2 1.2 copy-start.1

commit v3 on v2

--- a/solution.py
+++ b/solution.py
@@ -39,7 +39,7 @@
     s1r, s2r, g1r, g2r, s1c, s2c, g1c, g2c, q1c, q2c, i1c, i2c, prob_v, dl_v,
     dwp, dwi, dwf,
     in_sem, w_sem, out_sem,
-    xs_sem, xr_sem, ds_sem, dr_sem,
+    xs_sem, xr_sem, xd_sem, xf_sem, xfs_sem, ds_sem, dr_sem,
     ps_sem, pr_sem, pds_sem, pdr_sem,
     os_sem, or_sem, dxs_sem, dxr_sem,
     ys_sem, yr_sem,
@@ -109,14 +109,24 @@
         spot = (lax.broadcasted_iota(I32, (blk, n_tok), 0) + j * blk).astype(F32)
         return s1r[...] == spot, s2r[...] == spot
 
-    def send_rows(src, dst, send_sem, recv_sem, j):
-        for d in range(1, ep_size):
-            q = (r + d) % ep_size
-            pltpu.make_async_remote_copy(
-                src_ref=src.at[j, q], dst_ref=dst.at[j, my_place],
-                send_sem=send_sem, recv_sem=recv_sem.at[j],
-                device_id=(k, q), device_id_type=MESH,
-            ).start()
+    chip = r // 2
+    chip_x = chip + 1 - 2 * (chip % 2)
+    chip_y = (chip + 2) % 4
+    chip_d = 3 - chip
+    core = r % 2
+    diag = 2 * chip_d + (k + r) % 2
+    near = [2 * chip_x + core, 2 * chip_y + core, 2 * chip_x + 1 - core, 2 * chip_y + 1 - core, 2 * chip + 1 - core]
+    far = [2 * chip_d + core, 2 * chip_d + 1 - core]
+
+    def place_of(q):
+        return (q % tp_size) * half + q // tp_size
+
+    def send_row(src, dst, send_sem, recv_sem, j, q):
+        pltpu.make_async_remote_copy(
+            src_ref=src.at[j, q], dst_ref=dst.at[j, my_place],
+            send_sem=send_sem, recv_sem=recv_sem.at[j],
+            device_id=(k, q), device_id_type=MESH,
+        ).start()
 
     def wait_recv(view, sem):
         pltpu.make_async_remote_copy(
@@ -138,7 +148,9 @@
         for c in range(0, width, 512):
             rows = dot(pick, x_v[:, c:c + 512]).astype(BF)
             xs[j, :, :, c:c + 512] = rows.reshape(ep_size, cap, 512)
-        send_rows(xs, xr, xs_sem, xr_sem, j)
+        send_row(xs, xr, xs_sem, xd_sem, j, diag)
+        for q in near:
+            send_row(xs, xr, xs_sem, xr_sem, j, q)
         xr[j, my_place] = xs[j, r]
 
     def column(row):
@@ -176,7 +188,8 @@
         for c in range(0, width, 512):
             rows = (gate * dot(pick, dy_v[:, c:c + 512])).astype(BF)
             ds[j, :, :, c:c + 512] = rows.reshape(ep_size, cap, 512)
-        send_rows(ds, dr, ds_sem, dr_sem, j)
+        for q in far + near:
+            send_row(ds, dr, ds_sem, dr_sem, j, q)
         dr[j, my_place] = ds[j, r]
 
     def send_half(src, dst, send_sem, recv_sem, j):
@@ -206,11 +219,29 @@
             def _():
                 dst[j, r] = src[j, k * half + c]
 
+    n_near = len(near)
+    diag_place = place_of(diag)
+
+    def forward_diag(j):
+        wait_recv(xr.at[j, 0], xd_sem.at[j])
+        pltpu.make_async_remote_copy(
+            src_ref=xr.at[j, diag_place], dst_ref=xr.at[j, diag_place],
+            send_sem=xfs_sem, recv_sem=xf_sem.at[j],
+            device_id=(other, r), device_id_type=MESH,
+        ).start()
+
+    forward_diag(0)
+
     @pl.loop(0, n_loc)
     def _(j):
+        @pl.when(j + 1 < n_loc)
+        def _():
+            forward_diag(j + 1)
+
         for c in weight_copies(j):
             c.wait()
-        wait_recv(xr.at[j, pl.ds(0, ep_size - 1)], xr_sem.at[j])
+        wait_recv(xr.at[j, pl.ds(0, n_near)], xr_sem.at[j])
+        wait_recv(xr.at[j, 0], xf_sem.at[j])
         rows = xr[j].reshape(blk, width)
         pa = dot(rows, wa_v[j])
         pb = dot(rows, wb_v[j])
@@ -231,7 +262,7 @@
 
     merge_and_return(ps, pr, pr_sem, orr, os_sem, or_sem, n_loc - 1)
 
-    wait_send(xs.at[:, pl.ds(0, ep_size - 1)], xs_sem)
+    wait_send(xs.at[:, pl.ds(0, n_near + 1)], xs_sem)
 
     @pl.loop(0, n_loc)
     def _(j):
@@ -378,13 +409,16 @@
         c.start()
     finals.append(pltpu.make_async_copy(dx_v, dx_out, in_sem.at[1]))
     wait_send(ds.at[:, pl.ds(0, ep_size - 1)], ds_sem)
+    wait_send(xr.at[:, 0], xfs_sem)
     wait_send(ps.at[:, pl.ds(0, half)], ps_sem)
     wait_send(xs.at[:, pl.ds(0, half)], pds_sem)
     for c in outs + finals:
         c.wait()
 
 
-def weight_kernel(xe, de, h, da, db, ga_out, gb_out, gc_out):
+def weight_kernel(xe, de, h, da, db, y, dwr, ga_out, gb_out, gc_out, y_out, dwr_out):
+    y_out[...] = y[...]
+    dwr_out[...] = dwr[...]
     rows = xe[0]
     ga_out[0] = dot(rows, da[0], TN)
     gb_out[0] = dot(rows, db[0], TN)
@@ -434,7 +468,7 @@
                 pltpu.VMEM((ep_size, n_loc, width), F32), pltpu.VMEM((ep_size, n_loc, width), F32),
                 pltpu.VMEM((ep_size, n_loc, width), F32),
                 dma((3,)), dma((3, n_loc)), dma((5,)),
-                dma(()), dma((n_loc,)), dma(()), dma((n_loc,)),
+                dma(()), dma((n_loc,)), dma((n_loc,)), dma((n_loc,)), dma(()), dma(()), dma((n_loc,)),
                 dma(()), dma((n_loc,)), dma(()), dma((n_loc,)),
                 dma(()), dma((n_loc,)), dma(()), dma((n_loc,)),
                 dma(()), dma(()),
@@ -457,17 +491,20 @@
         xe = xe.reshape(n_loc, blk, width)
         de = de.reshape(n_loc, blk, width)
 
+        y_spec = pl.BlockSpec((n_tok // n_loc, width), lambda e: (e, 0))
+
         def spec(*shape):
             return pl.BlockSpec((1,) + shape, lambda e: (e, 0, 0))
 
-        grad_wa, grad_wb, grad_wc = pl.pallas_call(
+        grad_wa, grad_wb, grad_wc, act_out, grad_router = pl.pallas_call(
             weight_kernel,
             name="weight_grads",
             grid=(n_loc,),
-            in_specs=[spec(blk, width), spec(blk, width), spec(blk, hid), spec(blk, hid), spec(blk, hid)],
-            out_specs=[spec(width, hid), spec(width, hid), spec(hid, width)],
+            in_specs=[spec(blk, width), spec(blk, width), spec(blk, hid), spec(blk, hid), spec(blk, hid), y_spec, spec(n_exp // n_loc, width)],
+            out_specs=[spec(width, hid), spec(width, hid), spec(hid, width), y_spec, spec(n_exp // n_loc, width)],
             out_shape=[
                 sds((n_loc, width, hid), F32), sds((n_loc, width, hid), F32), sds((n_loc, hid, width), F32),
+                sds((n_tok, width), BF), sds((n_loc, n_exp // n_loc, width), F32),
             ],
             compiler_params=pltpu.CompilerParams(
                 dimension_semantics=("arbitrary",), vmem_limit_bytes=67043328
@@ -476,7 +513,7 @@
                 flops=6 * n_loc * blk * width * hid, transcendentals=0,
                 bytes_accessed=12 * n_loc * width * hid + 4 * n_loc * blk * width + 6 * n_loc * blk * hid,
             ),
-        )(xe, de, h, da, db)
+        )(xe, de, h, da, db, act_out, grad_router.reshape(n_loc, n_exp // n_loc, width))
         return act_out, grad_in, grad_wa, grad_wb, grad_wc, grad_router.reshape(n_exp, width).T
 
     return jax.shard_map(

time: 151 us -> 150 us (level)
  Pallas kernels: 140 us -> 142 us
  local copies, waits for them, and re-layouts: 1.98 us -> 0 us
    unnamed x6 -> x0, local copies, waits for them, and re-layouts: 1.98 us -> none
  transfers between devices with their start and end apart: 1 -> 1, of which waited for: 1 -> 0; matrix products, arithmetic and copies ran while one was open for 0% -> 0% of each run, Pallas kernels for 10% -> 11%
where the time goes in v3:
time: 150 us
  Pallas kernels  142 us (95%)
  starting transfers between devices  4.7 us (3%)
  other arithmetic  2.73 us (2%)
    pallas_call x1, Pallas kernels, local_step(): pl.pallas_call(functools.partial(moe_kernel, tp_size, ep_size, cap), name...  125 us
    pallas_call x1, Pallas kernels, local_step(): pl.pallas_call(weight_kernel, name='weight_grads', grid=(n_loc,), in_spec...  16.7 us
    ppermute x1, starting transfers between devices, local_step(): passed = lax.ppermute(grad_in, ('tp', 'ep'), partners)  4.7 us
  transfers between devices with their start and end apart: 1, of which 0 were waited for; matrix products, arithmetic and copies ran while one was open for 0% of the time, Pallas kernels for 11%

profile of v3, /device:TPU:0, one launch (start us, length us, event | category | flops | bytes accessed | tf_op | source)
XLA Modules:
  0.0 149.7 jit_solution(1615317780473262468)
XLA Ops:
  0.6 124.9 %moe.1 = (bf16[512,1536]{1,0:T(8,128)(2,1)}, bf16[512,1536]{1,0:T(8,128)(2,1)}, f32[8,8,1536]{2,1,0:T(8,128)}, bf16[8,8,16,1536]{3,2,1,0:T(8,128)(2,1)}, bf16[8,...) custom-call(s32[1,512]{1,0:T(1,128)} %bitcast.11, ...), custom_call_target="tpu_custom_call" | custom-call | tf_op jit(solution)/shard_map/moe/pallas_call | solution.py:448
  125.5 4.7 %collective-permute-start = (bf16[512,1536]{1,0:T(8,128)(2,1)}, bf16[512,1536]{1,0:T(8,128)(2,1)}, u32[]{:S(2)}, u32[]{:S(2)}) collective-permute-start(bf16[512,1536]{1,0:T(8,128)(2,1)} %get-tuple-element.27), channel_id=1, source_target_pairs={{0,8},{9,1},{2,10},{11,3},{4,12},{13,5},{6,14},{15,7}} | collective-permute-start | bytes 4718600 | tf_op jit(solution)/shard_map/ppermute | solution.py:488
  130.3 16.7 %weight_grads.1 = (f32[8,1536,256]{2,1,0:T(8,128)}, f32[8,1536,256]{2,1,0:T(8,128)}, f32[8,256,1536]{2,1,0:T(8,128)}, bf16[512,1536]{1,0:T(8,128)(2,1)}, f32[8,8,1536]{2,1,0:T(8,128)}) custom-call(bf16[8,128,1536]{2,1,0:T(8,128)(2,1)} %bitcast.8, bf16[8,128,1536]{2,1,0:T(8,128)(2,1)} %bitcast.9, bf16[8,128,256]{2,1,0:T(8,128)(2,1)} %get-tuple-element.21.h, ...), custom_call_target="tpu_custom_call" | custom-call | flops 2415919104 | bytes 45613056 | tf_op jit(solution)/shard_map/weight_grads/pallas_call | solution.py:499
  147.0 0.0 collective-permute-done
  147.0 2.7 %broadcast_select_fusion = bf16[512,1536]{1,0:T(8,128)(2,1)} fusion(bf16[512,1536]{1,0:T(8,128)(2,1)} %get-tuple-element.27, bf16[512,1536]{1,0:T(8,128)(2,1)} %collective-permute-done, pred[]{:T(512)S(6)} %eq.5), kind=kLoop, calls=%fused_computation | loop fusion | flops 786432 | bytes 4718593 | tf_op jit(solution)/shard_map/jit(_where)/select_n | solution.py:490
Async XLA Ops:
  125.5 21.4 %collective-permute-start = (bf16[512,1536]{1,0:T(8,128)(2,1)}, bf16[512,1536]{1,0:T(8,128)(2,1)}, u32[]{:S(2)}, u32[]{:S(2)}) collective-permute-start(bf16[512,1536]{1,0:T(8,128)(2,1)} %get-tuple-element.27), channel_id=1, source_target_pairs={{0,8},{9,1},{2,10},{11,3},{4,12},{13,5},{6,14},{15,7}} | collective-permute-start | bytes 4718600 | tf_op jit(solution)/shard_map/ppermute | solution.py:488

commit v4 on v3

--- a/solution.py
+++ b/solution.py
@@ -12,6 +12,8 @@
 I32 = jnp.int32
 MESH = pl.DeviceIdType.MESH
 GELU_COEF = 0.7978845608028654
+AHEAD = 3
+Y_STEP = 3
 NN = (((1,), (0,)), ((), ()))
 NT = (((1,), (1,)), ((), ()))
 TN = (((0,), (0,)), ((), ()))
@@ -63,8 +65,6 @@
         pltpu.make_async_copy(wr_hbm, wr_v, in_sem.at[2]),
     ]
     ins[0].start()
-    ins[1].start()
-    ins[2].start()
 
     def weight_copies(j):
         return [
@@ -72,11 +72,6 @@
             pltpu.make_async_copy(wb_hbm.at[j], wb_v.at[j], w_sem.at[1, j]),
             pltpu.make_async_copy(wc_hbm.at[j], wc_v.at[j], w_sem.at[2, j]),
         ]
-
-    @pl.loop(0, n_loc)
-    def _(j):
-        for c in weight_copies(j):
-            c.start()
 
     n_dev = tp_size * ep_size
     barrier = pltpu.get_barrier_semaphore()
@@ -138,11 +133,7 @@
             src_ref=view, dst_ref=view, send_sem=sem, recv_sem=sem, device_id=(k, r), device_id_type=MESH
         ).wait_send()
 
-    ins[0].wait()
-    pl.semaphore_wait(barrier, n_dev - 1)
-
-    @pl.loop(0, n_loc)
-    def _(j):
+    def build_x(j):
         m1, m2 = masks(j)
         pick = jnp.where(m1 | m2, 1.0, 0.0).astype(BF)
         for c in range(0, width, 512):
@@ -152,6 +143,21 @@
         for q in near:
             send_row(xs, xr, xs_sem, xr_sem, j, q)
         xr[j, my_place] = xs[j, r]
+
+    ins[0].wait()
+    ins[2].start()
+    ins[1].start()
+
+    @pl.loop(0, n_loc)
+    def _(j):
+        for c in weight_copies(j):
+            c.start()
+
+    pl.semaphore_wait(barrier, n_dev - 1)
+
+    @pl.loop(0, AHEAD)
+    def _(j):
+        build_x(j)
 
     def column(row):
         return jnp.transpose(jnp.broadcast_to(row, (128, n_tok)))
@@ -180,8 +186,7 @@
     g2r[...] = jnp.transpose(g2)[0:1, :]
     ins[1].wait()
 
-    @pl.loop(0, n_loc)
-    def _(j):
+    def build_d(j):
         m1, m2 = masks(j)
         pick = jnp.where(m1 | m2, 1.0, 0.0).astype(BF)
         gate = jnp.sum(jnp.where(m1, g1r[...], 0.0) + jnp.where(m2, g2r[...], 0.0), axis=1, keepdims=True)
@@ -234,6 +239,14 @@
 
     @pl.loop(0, n_loc)
     def _(j):
+        @pl.when(j + AHEAD < n_loc)
+        def _():
+            build_x(j + AHEAD)
+
+        @pl.when(j + AHEAD >= n_loc)
+        def _():
+            build_d(j + AHEAD - n_loc)
+
         @pl.when(j + 1 < n_loc)
         def _():
             forward_diag(j + 1)
@@ -260,12 +273,55 @@
         def _():
             merge_and_return(ps, pr, pr_sem, orr, os_sem, or_sem, j - 1)
 
-    merge_and_return(ps, pr, pr_sem, orr, os_sem, or_sem, n_loc - 1)
+    tb = 128
+    n_tb = n_tok // tb
+
+    def spots(col, toks):
+        lanes = lax.broadcasted_iota(I32, (tb, 128), 1).astype(F32)
+        base = col[toks, :]
+        return jnp.concatenate([base == lanes + float(u * 128) for u in range(n_exp * cap // 128)], axis=1)
+
+    def ship(buf, toks, send_sem, recv_sem):
+        pltpu.make_async_remote_copy(
+            src_ref=buf.at[toks], dst_ref=buf.at[toks], send_sem=send_sem, recv_sem=recv_sem,
+            device_id=(other, r), device_id_type=MESH,
+        ).start()
+
+    def combine_y(t):
+        toks = pl.ds(pl.multiple_of(t * tb, tb), tb)
+        pick1 = jnp.where(spots(s1c, toks), 1.0, 0.0).astype(BF)
+        pick2 = jnp.where(spots(s2c, toks), 1.0, 0.0).astype(BF)
+        dg1 = jnp.zeros((tb, 1), F32)
+        dg2 = jnp.zeros((tb, 1), F32)
+        ga = g1c[toks, 0:1]
+        gb = g2c[toks, 0:1]
+        for c in range(0, width, 512):
+            rows = orr[:, :, :, c:c + 512].reshape(n_exp * cap, 512)
+            o1 = dot(pick1, rows)
+            o2 = dot(pick2, rows)
+            y_v[toks, c:c + 512] = (ga * o1 + gb * o2).astype(BF)
+            dyf = dy_v[toks, c:c + 512].astype(F32)
+            dg1 = dg1 + jnp.sum(dyf * o1, axis=1, keepdims=True)
+            dg2 = dg2 + jnp.sum(dyf * o2, axis=1, keepdims=True)
+        ship(y_v, toks, ys_sem, yr_sem)
+        qa = q1c[toks, 0:1]
+        qb = q2c[toks, 0:1]
+        shared = dg1 * ga + dg2 * gb
+        dq1 = (dg1 - shared) / (qa + qb)
+        dq2 = (dg2 - shared) / (qa + qb)
+        centre = dq1 * qa + dq2 * qb
+        lanes = lax.broadcasted_iota(I32, (tb, n_exp), 1).astype(F32)
+        pull = jnp.where(i1c[toks, :n_exp] == lanes, dq1, 0.0) + jnp.where(i2c[toks, :n_exp] == lanes, dq2, 0.0)
+        dl_v[toks, :] = prob_v[toks, :] * (pull - centre)
 
     wait_send(xs.at[:, pl.ds(0, n_near + 1)], xs_sem)
 
     @pl.loop(0, n_loc)
     def _(j):
+        @pl.when(j + AHEAD < n_loc)
+        def _():
+            build_d(j + AHEAD)
+
         wait_recv(dr.at[j, pl.ds(0, ep_size - 1)], dr_sem.at[j])
         rows = dr[j].reshape(blk, width)
         dh = dot(rows, wc_v[j], NT)
@@ -278,9 +334,23 @@
             xs[j, :, :, c:c + 512] = part.astype(BF).reshape(ep_size, cap, 512)
         send_half(xs, pdr, pds_sem, pdr_sem, j)
 
+        @pl.when(j == 0)
+        def _():
+            merge_and_return(ps, pr, pr_sem, orr, os_sem, or_sem, n_loc - 1)
+
         @pl.when(j > 0)
         def _():
             merge_and_return(xs, pdr, pdr_sem, dxr, dxs_sem, dxr_sem, j - 1)
+
+        @pl.when(owner & (j == Y_STEP))
+        def _():
+            @pl.loop(0, n_loc)
+            def _(i):
+                wait_recv(orr.at[i, pl.ds(0, ep_size - 1)], or_sem.at[i])
+
+        @pl.when(owner & (j >= Y_STEP) & (j < Y_STEP + n_tb))
+        def _():
+            combine_y(j - Y_STEP)
 
     merge_and_return(xs, pdr, pdr_sem, dxr, dxs_sem, dxr_sem, n_loc - 1)
 
@@ -294,54 +364,8 @@
     for c in outs:
         c.start()
 
-    tb = 128
-    n_tb = n_tok // tb
-
-    def spots(col, toks):
-        lanes = lax.broadcasted_iota(I32, (tb, 128), 1).astype(F32)
-        base = col[toks, :]
-        return jnp.concatenate([base == lanes + float(u * 128) for u in range(n_exp * cap // 128)], axis=1)
-
-    def ship(buf, toks, send_sem, recv_sem):
-        pltpu.make_async_remote_copy(
-            src_ref=buf.at[toks], dst_ref=buf.at[toks], send_sem=send_sem, recv_sem=recv_sem,
-            device_id=(other, r), device_id_type=MESH,
-        ).start()
-
     @pl.when(owner)
     def _():
-        @pl.loop(0, n_loc)
-        def _(j):
-            wait_recv(orr.at[j, pl.ds(0, ep_size - 1)], or_sem.at[j])
-
-        @pl.loop(0, n_tb)
-        def _(t):
-            toks = pl.ds(pl.multiple_of(t * tb, tb), tb)
-            pick1 = jnp.where(spots(s1c, toks), 1.0, 0.0).astype(BF)
-            pick2 = jnp.where(spots(s2c, toks), 1.0, 0.0).astype(BF)
-            dg1 = jnp.zeros((tb, 1), F32)
-            dg2 = jnp.zeros((tb, 1), F32)
-            ga = g1c[toks, 0:1]
-            gb = g2c[toks, 0:1]
-            for c in range(0, width, 512):
-                rows = orr[:, :, :, c:c + 512].reshape(n_exp * cap, 512)
-                o1 = dot(pick1, rows)
-                o2 = dot(pick2, rows)
-                y_v[toks, c:c + 512] = (ga * o1 + gb * o2).astype(BF)
-                dyf = dy_v[toks, c:c + 512].astype(F32)
-                dg1 = dg1 + jnp.sum(dyf * o1, axis=1, keepdims=True)
-                dg2 = dg2 + jnp.sum(dyf * o2, axis=1, keepdims=True)
-            ship(y_v, toks, ys_sem, yr_sem)
-            qa = q1c[toks, 0:1]
-            qb = q2c[toks, 0:1]
-            shared = dg1 * ga + dg2 * gb
-            dq1 = (dg1 - shared) / (qa + qb)
-            dq2 = (dg2 - shared) / (qa + qb)
-            centre = dq1 * qa + dq2 * qb
-            lanes = lax.broadcasted_iota(I32, (tb, n_exp), 1).astype(F32)
-            pull = jnp.where(i1c[toks, :n_exp] == lanes, dq1, 0.0) + jnp.where(i2c[toks, :n_exp] == lanes, dq2, 0.0)
-            dl_v[toks, :] = prob_v[toks, :] * (pull - centre)
-
         d_hi, d_mid, d_low = split3(dl_v[...])
         for c in range(0, width, 512):
             xc = x_v[:, c:c + 512]

time: 150 us -> 145 us (0.967)
  Pallas kernels: 142 us -> 137 us
    pallas_call x1, Pallas kernels: 125 us -> 120 us  [local_step(): pl.pallas_call(functools.partial(moe_kernel, tp_size, ep_size, cap), name...]
  transfers between devices with their start and end apart: 1 -> 1, of which waited for: 0 -> 0; matrix products, arithmetic and copies ran while one was open for 0% -> 0% of each run, Pallas kernels for 11% -> 12%
where the time goes in v4:
time: 145 us; the launch traced here: 144 us
  Pallas kernels  137 us (94%)
  starting transfers between devices  4.11 us (3%)
  other arithmetic  2.73 us (2%)
    pallas_call x1, Pallas kernels, local_step(): pl.pallas_call(functools.partial(moe_kernel, tp_size, ep_size, cap), name...  120 us
    pallas_call x1, Pallas kernels, local_step(): pl.pallas_call(weight_kernel, name='weight_grads', grid=(n_loc,), in_spec...  16.7 us
    ppermute x1, starting transfers between devices, local_step(): passed = lax.ppermute(grad_in, ('tp', 'ep'), partners)  4.11 us
  transfers between devices with their start and end apart: 1, of which 0 were waited for; matrix products, arithmetic and copies ran while one was open for 0% of the time, Pallas kernels for 12%

profile of v4, /device:TPU:0, one launch (start us, length us, event | category | flops | bytes accessed | tf_op | source)
XLA Modules:
  0.0 144.5 jit_solution(11171446482640673616)
XLA Ops:
  0.6 120.3 %moe.1 = (bf16[512,1536]{1,0:T(8,128)(2,1)}, bf16[512,1536]{1,0:T(8,128)(2,1)}, f32[8,8,1536]{2,1,0:T(8,128)}, bf16[8,8,16,1536]{3,2,1,0:T(8,128)(2,1)}, bf16[8,...) custom-call(s32[1,512]{1,0:T(1,128)} %bitcast.11, ...), custom_call_target="tpu_custom_call" | custom-call | tf_op jit(solution)/shard_map/moe/pallas_call | solution.py:472
  120.9 4.1 %collective-permute-start = (bf16[512,1536]{1,0:T(8,128)(2,1)}, bf16[512,1536]{1,0:T(8,128)(2,1)}, u32[]{:S(2)}, u32[]{:S(2)}) collective-permute-start(bf16[512,1536]{1,0:T(8,128)(2,1)} %get-tuple-element.27), channel_id=1, source_target_pairs={{0,8},{9,1},{2,10},{11,3},{4,12},{13,5},{6,14},{15,7}} | collective-permute-start | bytes 4718600 | tf_op jit(solution)/shard_map/ppermute | solution.py:512
  125.0 16.7 %weight_grads.1 = (f32[8,1536,256]{2,1,0:T(8,128)}, f32[8,1536,256]{2,1,0:T(8,128)}, f32[8,256,1536]{2,1,0:T(8,128)}, bf16[512,1536]{1,0:T(8,128)(2,1)}, f32[8,8,1536]{2,1,0:T(8,128)}) custom-call(bf16[8,128,1536]{2,1,0:T(8,128)(2,1)} %bitcast.8, bf16[8,128,1536]{2,1,0:T(8,128)(2,1)} %bitcast.9, bf16[8,128,256]{2,1,0:T(8,128)(2,1)} %get-tuple-element.21.h, ...), custom_call_target="tpu_custom_call" | custom-call | flops 2415919104 | bytes 45613056 | tf_op jit(solution)/shard_map/weight_grads/pallas_call | solution.py:523
  141.7 0.0 collective-permute-done
  141.8 2.7 %broadcast_select_fusion = bf16[512,1536]{1,0:T(8,128)(2,1)} fusion(bf16[512,1536]{1,0:T(8,128)(2,1)} %get-tuple-element.27, bf16[512,1536]{1,0:T(8,128)(2,1)} %collective-permute-done, pred[]{:T(512)S(6)} %eq.5), kind=kLoop, calls=%fused_computation | loop fusion | flops 786432 | bytes 4718593 | tf_op jit(solution)/shard_map/jit(_where)/select_n | solution.py:514
Async XLA Ops:
  120.9 20.8 %collective-permute-start = (bf16[512,1536]{1,0:T(8,128)(2,1)}, bf16[512,1536]{1,0:T(8,128)(2,1)}, u32[]{:S(2)}, u32[]{:S(2)}) collective-permute-start(bf16[512,1536]{1,0:T(8,128)(2,1)} %get-tuple-element.27), channel_id=1, source_target_pairs={{0,8},{9,1},{2,10},{11,3},{4,12},{13,5},{6,14},{15,7}} | collective-permute-start | bytes 4718600 | tf_op jit(solution)/shard_map/ppermute | solution.py:512

commit v5 on v4

--- a/solution.py
+++ b/solution.py
@@ -14,6 +14,7 @@
 GELU_COEF = 0.7978845608028654
 AHEAD = 3
 Y_STEP = 3
+Y_INNER = 2
 NN = (((1,), (0,)), ((), ()))
 NT = (((1,), (1,)), ((), ()))
 TN = (((0,), (0,)), ((), ()))
@@ -39,7 +40,7 @@
     xs, ds, xr, dr, h_v, da_v, db_v, bs_v, gv_v,
     ps, pr, pdr, orr, dxr, y_v, dx_v,
     s1r, s2r, g1r, g2r, s1c, s2c, g1c, g2c, q1c, q2c, i1c, i2c, prob_v, dl_v,
-    dwp, dwi, dwf,
+    dwp, dwi, dwf, acc_v,
     in_sem, w_sem, out_sem,
     xs_sem, xr_sem, xd_sem, xf_sem, xfs_sem, ds_sem, dr_sem,
     ps_sem, pr_sem, pds_sem, pdr_sem,
@@ -247,6 +248,10 @@
         def _():
             build_d(j + AHEAD - n_loc)
 
+        @pl.when(j > 0)
+        def _():
+            merge_and_return(ps, pr, pr_sem, orr, os_sem, or_sem, j - 1)
+
         @pl.when(j + 1 < n_loc)
         def _():
             forward_diag(j + 1)
@@ -268,10 +273,6 @@
         for c in range(0, width, 512):
             ps[j, :, :, c:c + 512] = dot(hidden, wc_v[j, :, c:c + 512]).astype(BF).reshape(ep_size, cap, 512)
         send_half(ps, pr, ps_sem, pr_sem, j)
-
-        @pl.when(j > 0)
-        def _():
-            merge_and_return(ps, pr, pr_sem, orr, os_sem, or_sem, j - 1)
 
     tb = 128
     n_tb = n_tok // tb
@@ -315,12 +316,17 @@
         dl_v[toks, :] = prob_v[toks, :] * (pull - centre)
 
     wait_send(xs.at[:, pl.ds(0, n_near + 1)], xs_sem)
+    merge_and_return(ps, pr, pr_sem, orr, os_sem, or_sem, n_loc - 1)
 
     @pl.loop(0, n_loc)
     def _(j):
         @pl.when(j + AHEAD < n_loc)
         def _():
             build_d(j + AHEAD)
+
+        @pl.when(j > 0)
+        def _():
+            merge_and_return(xs, pdr, pdr_sem, dxr, dxs_sem, dxr_sem, j - 1)
 
         wait_recv(dr.at[j, pl.ds(0, ep_size - 1)], dr_sem.at[j])
         rows = dr[j].reshape(blk, width)
@@ -334,25 +340,15 @@
             xs[j, :, :, c:c + 512] = part.astype(BF).reshape(ep_size, cap, 512)
         send_half(xs, pdr, pds_sem, pdr_sem, j)
 
-        @pl.when(j == 0)
-        def _():
-            merge_and_return(ps, pr, pr_sem, orr, os_sem, or_sem, n_loc - 1)
-
-        @pl.when(j > 0)
-        def _():
-            merge_and_return(xs, pdr, pdr_sem, dxr, dxs_sem, dxr_sem, j - 1)
-
         @pl.when(owner & (j == Y_STEP))
         def _():
             @pl.loop(0, n_loc)
             def _(i):
                 wait_recv(orr.at[i, pl.ds(0, ep_size - 1)], or_sem.at[i])
 
-        @pl.when(owner & (j >= Y_STEP) & (j < Y_STEP + n_tb))
+        @pl.when(owner & (j >= Y_STEP) & (j < Y_STEP + Y_INNER))
         def _():
             combine_y(j - Y_STEP)
-
-    merge_and_return(xs, pdr, pdr_sem, dxr, dxs_sem, dxr_sem, n_loc - 1)
 
     outs = [
         pltpu.make_async_copy(xr, xe_out, out_sem.at[0]),
@@ -361,11 +357,38 @@
         pltpu.make_async_copy(da_v, da_out, out_sem.at[3]),
         pltpu.make_async_copy(db_v, db_out, out_sem.at[4]),
     ]
-    for c in outs:
+    for c in outs[:3]:
         c.start()
+
+    split = n_loc - 2
+
+    def pick_both(t):
+        toks = pl.ds(pl.multiple_of(t * tb, tb), tb)
+        return toks, jnp.where(spots(s1c, toks) | spots(s2c, toks), 1.0, 0.0).astype(BF)
+
+    def sum_first(t):
+        toks, pick = pick_both(t)
+        dl = dl_v[toks, :]
+        for c in range(0, width, 512):
+            rows = dxr[0:split, :, :, c:c + 512].reshape(split * blk, 512)
+            router = lax.dot_general(
+                dl, wr_v[:, c:c + 512], NN, precision=lax.Precision.HIGHEST, preferred_element_type=F32
+            )
+            acc_v[toks, c:c + 512] = dot(pick[:, :split * blk], rows) + router
+
+    def sum_last(t):
+        toks, pick = pick_both(t)
+        for c in range(0, width, 512):
+            rows = dxr[split:n_loc, :, :, c:c + 512].reshape((n_loc - split) * blk, 512)
+            dx_v[toks, c:c + 512] = (acc_v[toks, c:c + 512] + dot(pick[:, split * blk:], rows)).astype(BF)
+        pltpu.make_async_copy(dx_v.at[toks], dx_out.at[toks], in_sem.at[1]).start()
 
     @pl.when(owner)
     def _():
+        @pl.loop(Y_INNER, n_tb)
+        def _(t):
+            combine_y(t)
+
         d_hi, d_mid, d_low = split3(dl_v[...])
         for c in range(0, width, 512):
             xc = x_v[:, c:c + 512]
@@ -379,9 +402,19 @@
             ).start()
         dwi[r] = dwp[r]
 
-        @pl.loop(0, n_loc)
+    merge_and_return(xs, pdr, pdr_sem, dxr, dxs_sem, dxr_sem, n_loc - 1)
+    for c in outs[3:]:
+        c.start()
+
+    @pl.when(owner)
+    def _():
+        @pl.loop(0, split)
         def _(j):
             wait_recv(dxr.at[j, pl.ds(0, ep_size - 1)], dxr_sem.at[j])
+
+        @pl.loop(0, n_tb)
+        def _(t):
+            sum_first(t)
 
         wait_recv(dwi.at[pl.ds(0, ep_size - 1)], rr_sem)
         total = dwi[0]
@@ -394,19 +427,14 @@
                 src_ref=dwf.at[r], dst_ref=dwf.at[r], send_sem=fs_sem, recv_sem=fr_sem,
                 device_id=(flat // ep_size, flat % ep_size), device_id_type=MESH,
             ).start()
+
+        @pl.loop(split, n_loc)
+        def _(j):
+            wait_recv(dxr.at[j, pl.ds(0, ep_size - 1)], dxr_sem.at[j])
+
         @pl.loop(0, n_tb)
         def _(t):
-            toks = pl.ds(pl.multiple_of(t * tb, tb), tb)
-            pick = jnp.where(spots(s1c, toks) | spots(s2c, toks), 1.0, 0.0).astype(BF)
-            dl = dl_v[toks, :]
-            for c in range(0, width, 512):
-                rows = dxr[:, :, :, c:c + 512].reshape(n_exp * cap, 512)
-                back = dot(pick, rows)
-                router = lax.dot_general(
-                    dl, wr_v[:, c:c + 512], NN, precision=lax.Precision.HIGHEST, preferred_element_type=F32
-                )
-                dx_v[toks, c:c + 512] = (back + router).astype(BF)
-            pltpu.make_async_copy(dx_v.at[toks], dx_out.at[toks], in_sem.at[1]).start()
+            sum_last(t)
 
         wait_recv(dwf.at[pl.ds(0, ep_size - 1)], fr_sem)
         wait_send(dwp.at[pl.ds(0, ep_size - 1)], rs_sem)
@@ -447,6 +475,22 @@
     ga_out[0] = dot(rows, da[0], TN)
     gb_out[0] = dot(rows, db[0], TN)
     gc_out[0] = dot(h[0], de[0], TN)
+
+
+def settle_kernel(tp_size, pieces, mine, passed, out, buf, in_sem, out_sem):
+    n = buf.shape[0] // pieces
+
+    @pl.when(lax.axis_index("ep") % tp_size == lax.axis_index("tp"))
+    def _():
+        loads = [pltpu.make_async_copy(mine.at[pl.ds(i * n, n)], buf.at[pl.ds(i * n, n)], in_sem.at[i]) for i in range(pieces)]
+        stores = [pltpu.make_async_copy(buf.at[pl.ds(i * n, n)], out.at[pl.ds(i * n, n)], out_sem.at[i]) for i in range(pieces)]
+        for c in loads:
+            c.start()
+        for i in range(pieces):
+            loads[i].wait()
+            stores[i].start()
+        for c in stores:
+            c.wait()
 
 
 def solution(mesh):
@@ -490,7 +534,7 @@
                 row, row, row, row, col, col, col, col, col, col, col, col,
                 pltpu.VMEM((n_tok, n_exp), F32), pltpu.VMEM((n_tok, n_exp), F32),
                 pltpu.VMEM((ep_size, n_loc, width), F32), pltpu.VMEM((ep_size, n_loc, width), F32),
-                pltpu.VMEM((ep_size, n_loc, width), F32),
+                pltpu.VMEM((ep_size, n_loc, width), F32), pltpu.VMEM((n_tok, width), F32),
                 dma((3,)), dma((3, n_loc)), dma((5,)),
                 dma(()), dma((n_loc,)), dma((n_loc,)), dma((n_loc,)), dma(()), dma(()), dma((n_loc,)),
                 dma(()), dma((n_loc,)), dma(()), dma((n_loc,)),
@@ -510,8 +554,6 @@
             ((q % tp_size) * ep_size + q, (1 - q % tp_size) * ep_size + q) for q in range(ep_size)
         ]
         passed = lax.ppermute(grad_in, ("tp", "ep"), partners)
-        owner = lax.axis_index("ep") % tp_size == lax.axis_index("tp")
-        grad_in = jnp.where(owner, grad_in, passed)
         xe = xe.reshape(n_loc, blk, width)
         de = de.reshape(n_loc, blk, width)
 
@@ -538,6 +580,16 @@
                 bytes_accessed=12 * n_loc * width * hid + 4 * n_loc * blk * width + 6 * n_loc * blk * hid,
             ),
         )(xe, de, h, da, db, act_out, grad_router.reshape(n_loc, n_exp // n_loc, width))
+        pieces = n_loc
+        grad_in = pl.pallas_call(
+            functools.partial(settle_kernel, tp_size, pieces),
+            name="settle",
+            in_specs=[any_spec, any_spec],
+            out_specs=any_spec,
+            out_shape=sds((n_tok, width), BF),
+            scratch_shapes=[pltpu.VMEM((n_tok, width), BF), dma((pieces,)), dma((pieces,))],
+            input_output_aliases={1: 0},
+        )(grad_in, passed)
         return act_out, grad_in, grad_wa, grad_wb, grad_wc, grad_router.reshape(n_exp, width).T
 
     return jax.shard_map(

time: 145 us -> 177 us (1.22)
  Pallas kernels: 137 us -> 167 us
  other arithmetic: 2.73 us -> 0 us
  local copies, waits for them, and re-layouts: 0 us -> 2.65 us
  starting transfers between devices: 4.11 us -> 5.99 us
    pallas_call x1, Pallas kernels: 120 us -> 148 us  [local_step(): pl.pallas_call(functools.partial(moe_kernel, tp_size, ep_size, cap), name...]
    select_n x1 -> x0, other arithmetic: 2.73 us -> none  [local_step(): grad_in = jnp.where(owner, grad_in, passed)]
    unnamed x0 -> x1, local copies, waits for them, and re-layouts: none -> 2.65 us
    pallas_call x0 -> x1, Pallas kernels: none -> 2.4 us  [local_step(): pl.pallas_call(functools.partial(settle_kernel, tp_size, pieces), name='s...]
    ppermute x1, starting transfers between devices: 4.11 us -> 5.99 us  [local_step(): passed = lax.ppermute(grad_in, ('tp', 'ep'), partners)]
  transfers between devices with their start and end apart: 1 -> 1, of which waited for: 0 -> 0; matrix products, arithmetic and copies ran while one was open for 0% -> 0% of each run, Pallas kernels for 12% -> 9%
where the time goes in v5:
time: 177 us
  Pallas kernels  167 us (94%)
  starting transfers between devices  5.99 us (3%)
  local copies, waits for them, and re-layouts  2.65 us (1%)
    pallas_call x1, Pallas kernels, local_step(): pl.pallas_call(functools.partial(moe_kernel, tp_size, ep_size, cap), name...  148 us
    pallas_call x1, Pallas kernels, local_step(): pl.pallas_call(weight_kernel, name='weight_grads', grid=(n_loc,), in_spec...  16.7 us
    ppermute x1, starting transfers between devices, local_step(): passed = lax.ppermute(grad_in, ('tp', 'ep'), partners)  5.99 us
  transfers between devices with their start and end apart: 1, of which 0 were waited for; matrix products, arithmetic and copies ran while one was open for 0% of the time, Pallas kernels for 9%

profile of v5, /device:TPU:0, one launch (start us, length us, event | category | flops | bytes accessed | tf_op | source)
XLA Modules:
  0.0 176.5 jit_solution(13317593319132661891)
XLA Ops:
  0.6 148.1 %moe.1 = (bf16[512,1536]{1,0:T(8,128)(2,1)}, bf16[512,1536]{1,0:T(8,128)(2,1)}, f32[8,8,1536]{2,1,0:T(8,128)}, bf16[8,8,16,1536]{3,2,1,0:T(8,128)(2,1)}, bf16[8,...) custom-call(s32[1,512]{1,0:T(1,128)} %bitcast.11, ...), custom_call_target="tpu_custom_call" | custom-call | tf_op jit(solution)/shard_map/moe/pallas_call | solution.py:516
  148.7 6.0 %collective-permute-start = (bf16[512,1536]{1,0:T(8,128)(2,1)}, bf16[512,1536]{1,0:T(8,128)(2,1)}, u32[]{:S(2)}, u32[]{:S(2)}) collective-permute-start(bf16[512,1536]{1,0:T(8,128)(2,1)} %get-tuple-element.27.mine), channel_id=1, source_target_pairs={{0,8},{9,1},{2,10},{11,3},{4,12},{13,5},{6,14},{15,7}} | collective-permute-start | bytes 4718600 | tf_op jit(solution)/shard_map/ppermute | solution.py:556
  154.7 16.7 %weight_grads.1 = (f32[8,1536,256]{2,1,0:T(8,128)}, f32[8,1536,256]{2,1,0:T(8,128)}, f32[8,256,1536]{2,1,0:T(8,128)}, bf16[512,1536]{1,0:T(8,128)(2,1)}, f32[8,8,1536]{2,1,0:T(8,128)}) custom-call(bf16[8,128,1536]{2,1,0:T(8,128)(2,1)} %bitcast.8, bf16[8,128,1536]{2,1,0:T(8,128)(2,1)} %bitcast.9, bf16[8,128,256]{2,1,0:T(8,128)(2,1)} %get-tuple-element.21.h, ...), custom_call_target="tpu_custom_call" | custom-call | flops 2415919104 | bytes 45613056 | tf_op jit(solution)/shard_map/weight_grads/pallas_call | solution.py:565
  171.5 0.0 collective-permute-done.passed
  171.5 2.4 %settle.1 = bf16[512,1536]{1,0:T(8,128)(2,1)} custom-call(bf16[512,1536]{1,0:T(8,128)(2,1)} %get-tuple-element.27.mine, bf16[512,1536]{1,0:T(8,128)(2,1)} %collective-permute-done.passed), custom_call_target="tpu_custom_call", output_to_operand_aliasing={{}: (1, {})} | custom-call | tf_op jit(solution)/shard_map/settle/pallas_call | solution.py:584
  173.9 2.7 %copy.17 = bf16[512,1536]{1,0:T(8,128)(2,1)} copy(bf16[512,1536]{1,0:T(8,128)(2,1)} %settle.1) | data formatting | bytes 3145728
Async XLA Ops:
  148.7 22.7 %collective-permute-start = (bf16[512,1536]{1,0:T(8,128)(2,1)}, bf16[512,1536]{1,0:T(8,128)(2,1)}, u32[]{:S(2)}, u32[]{:S(2)}) collective-permute-start(bf16[512,1536]{1,0:T(8,128)(2,1)} %get-tuple-element.27.mine), channel_id=1, source_target_pairs={{0,8},{9,1},{2,10},{11,3},{4,12},{13,5},{6,14},{15,7}} | collective-permute-start | bytes 4718600 | tf_op jit(solution)/shard_map/ppermute | solution.py:556

commit v6 on v5

--- a/solution.py
+++ b/solution.py
@@ -13,7 +13,8 @@
 MESH = pl.DeviceIdType.MESH
 GELU_COEF = 0.7978845608028654
 AHEAD = 3
-Y_STEP = 3
+LAG = 2
+Y_STEP = 4
 Y_INNER = 2
 NN = (((1,), (0,)), ((), ()))
 NT = (((1,), (1,)), ((), ()))
@@ -248,10 +249,6 @@
         def _():
             build_d(j + AHEAD - n_loc)
 
-        @pl.when(j > 0)
-        def _():
-            merge_and_return(ps, pr, pr_sem, orr, os_sem, or_sem, j - 1)
-
         @pl.when(j + 1 < n_loc)
         def _():
             forward_diag(j + 1)
@@ -273,6 +270,10 @@
         for c in range(0, width, 512):
             ps[j, :, :, c:c + 512] = dot(hidden, wc_v[j, :, c:c + 512]).astype(BF).reshape(ep_size, cap, 512)
         send_half(ps, pr, ps_sem, pr_sem, j)
+
+        @pl.when(j >= LAG)
+        def _():
+            merge_and_return(ps, pr, pr_sem, orr, os_sem, or_sem, j - LAG)
 
     tb = 128
     n_tb = n_tok // tb
@@ -316,17 +317,11 @@
         dl_v[toks, :] = prob_v[toks, :] * (pull - centre)
 
     wait_send(xs.at[:, pl.ds(0, n_near + 1)], xs_sem)
-    merge_and_return(ps, pr, pr_sem, orr, os_sem, or_sem, n_loc - 1)
-
     @pl.loop(0, n_loc)
     def _(j):
         @pl.when(j + AHEAD < n_loc)
         def _():
             build_d(j + AHEAD)
-
-        @pl.when(j > 0)
-        def _():
-            merge_and_return(xs, pdr, pdr_sem, dxr, dxs_sem, dxr_sem, j - 1)
 
         wait_recv(dr.at[j, pl.ds(0, ep_size - 1)], dr_sem.at[j])
         rows = dr[j].reshape(blk, width)
@@ -339,6 +334,15 @@
             part = dot(da, wa_v[j, c:c + 512, :], NT) + dot(db, wb_v[j, c:c + 512, :], NT)
             xs[j, :, :, c:c + 512] = part.astype(BF).reshape(ep_size, cap, 512)
         send_half(xs, pdr, pds_sem, pdr_sem, j)
+
+        @pl.when(j == 0)
+        def _():
+            for i in range(LAG):
+                merge_and_return(ps, pr, pr_sem, orr, os_sem, or_sem, n_loc - LAG + i)
+
+        @pl.when(j >= LAG)
+        def _():
+            merge_and_return(xs, pdr, pdr_sem, dxr, dxs_sem, dxr_sem, j - LAG)
 
         @pl.when(owner & (j == Y_STEP))
         def _():
@@ -382,6 +386,9 @@
             rows = dxr[split:n_loc, :, :, c:c + 512].reshape((n_loc - split) * blk, 512)
             dx_v[toks, c:c + 512] = (acc_v[toks, c:c + 512] + dot(pick[:, split * blk:], rows)).astype(BF)
         pltpu.make_async_copy(dx_v.at[toks], dx_out.at[toks], in_sem.at[1]).start()
+
+    for i in range(LAG - 1):
+        merge_and_return(xs, pdr, pdr_sem, dxr, dxs_sem, dxr_sem, n_loc - LAG + i)
 
     @pl.when(owner)
     def _():
@@ -475,22 +482,6 @@
     ga_out[0] = dot(rows, da[0], TN)
     gb_out[0] = dot(rows, db[0], TN)
     gc_out[0] = dot(h[0], de[0], TN)
-
-
-def settle_kernel(tp_size, pieces, mine, passed, out, buf, in_sem, out_sem):
-    n = buf.shape[0] // pieces
-
-    @pl.when(lax.axis_index("ep") % tp_size == lax.axis_index("tp"))
-    def _():
-        loads = [pltpu.make_async_copy(mine.at[pl.ds(i * n, n)], buf.at[pl.ds(i * n, n)], in_sem.at[i]) for i in range(pieces)]
-        stores = [pltpu.make_async_copy(buf.at[pl.ds(i * n, n)], out.at[pl.ds(i * n, n)], out_sem.at[i]) for i in range(pieces)]
-        for c in loads:
-            c.start()
-        for i in range(pieces):
-            loads[i].wait()
-            stores[i].start()
-        for c in stores:
-            c.wait()
 
 
 def solution(mesh):
@@ -554,6 +545,8 @@
             ((q % tp_size) * ep_size + q, (1 - q % tp_size) * ep_size + q) for q in range(ep_size)
         ]
         passed = lax.ppermute(grad_in, ("tp", "ep"), partners)
+        owner = lax.axis_index("ep") % tp_size == lax.axis_index("tp")
+        grad_in = jnp.where(owner, grad_in, passed)
         xe = xe.reshape(n_loc, blk, width)
         de = de.reshape(n_loc, blk, width)
 
@@ -580,16 +573,6 @@
                 bytes_accessed=12 * n_loc * width * hid + 4 * n_loc * blk * width + 6 * n_loc * blk * hid,
             ),
         )(xe, de, h, da, db, act_out, grad_router.reshape(n_loc, n_exp // n_loc, width))
-        pieces = n_loc
-        grad_in = pl.pallas_call(
-            functools.partial(settle_kernel, tp_size, pieces),
-            name="settle",
-            in_specs=[any_spec, any_spec],
-            out_specs=any_spec,
-            out_shape=sds((n_tok, width), BF),
-            scratch_shapes=[pltpu.VMEM((n_tok, width), BF), dma((pieces,)), dma((pieces,))],
-            input_output_aliases={1: 0},
-        )(grad_in, passed)
         return act_out, grad_in, grad_wa, grad_wb, grad_wc, grad_router.reshape(n_exp, width).T
 
     return jax.shard_map(

time: 177 us -> 144 us (0.81)
  Pallas kernels: 167 us -> 136 us
  starting transfers between devices: 5.99 us -> 3.2 us
  other arithmetic: 0 us -> 2.73 us
  local copies, waits for them, and re-layouts: 2.65 us -> 0 us
    pallas_call x1, Pallas kernels: 148 us -> 119 us  [local_step(): pl.pallas_call(functools.partial(moe_kernel, tp_size, ep_size, cap), name...]
    ppermute x1, starting transfers between devices: 5.99 us -> 3.2 us  [local_step(): passed = lax.ppermute(grad_in, ('tp', 'ep'), partners)]
    select_n x0 -> x1, other arithmetic: none -> 2.73 us  [local_step(): grad_in = jnp.where(owner, grad_in, passed)]
    unnamed x1 -> x0, local copies, waits for them, and re-layouts: 2.65 us -> none
    pallas_call x1 -> x0, Pallas kernels: 2.4 us -> none  [local_step(): pl.pallas_call(functools.partial(settle_kernel, tp_size, pieces), name='s...]
  transfers between devices with their start and end apart: 1 -> 1, of which waited for: 0 -> 0; matrix products, arithmetic and copies ran while one was open for 0% -> 0% of each run, Pallas kernels for 9% -> 12%
where the time goes in v6:
time: 144 us; the launch traced here: 142 us
  Pallas kernels  136 us (94%)
  starting transfers between devices  3.2 us (2%)
  other arithmetic  2.73 us (2%)
    pallas_call x1, Pallas kernels, local_step(): pl.pallas_call(functools.partial(moe_kernel, tp_size, ep_size, cap), name...  119 us
    pallas_call x1, Pallas kernels, local_step(): pl.pallas_call(weight_kernel, name='weight_grads', grid=(n_loc,), in_spec...  16.7 us
    ppermute x1, starting transfers between devices, local_step(): passed = lax.ppermute(grad_in, ('tp', 'ep'), partners)  3.2 us
  transfers between devices with their start and end apart: 1, of which 0 were waited for; matrix products, arithmetic and copies ran while one was open for 0% of the time, Pallas kernels for 12%

profile of v6, /device:TPU:0, one launch (start us, length us, event | category | flops | bytes accessed | tf_op | source)
XLA Modules:
  0.0 142.5 jit_solution(7508222528814335933)
XLA Ops:
  0.6 119.2 %moe.1 = (bf16[512,1536]{1,0:T(8,128)(2,1)}, bf16[512,1536]{1,0:T(8,128)(2,1)}, f32[8,8,1536]{2,1,0:T(8,128)}, bf16[8,8,16,1536]{3,2,1,0:T(8,128)(2,1)}, bf16[8,...) custom-call(s32[1,512]{1,0:T(1,128)} %bitcast.11, ...), custom_call_target="tpu_custom_call" | custom-call | tf_op jit(solution)/shard_map/moe/pallas_call | solution.py:507
  119.8 3.2 %collective-permute-start = (bf16[512,1536]{1,0:T(8,128)(2,1)}, bf16[512,1536]{1,0:T(8,128)(2,1)}, u32[]{:S(2)}, u32[]{:S(2)}) collective-permute-start(bf16[512,1536]{1,0:T(8,128)(2,1)} %get-tuple-element.27), channel_id=1, source_target_pairs={{0,8},{9,1},{2,10},{11,3},{4,12},{13,5},{6,14},{15,7}} | collective-permute-start | bytes 4718600 | tf_op jit(solution)/shard_map/ppermute | solution.py:547
  123.0 16.7 %weight_grads.1 = (f32[8,1536,256]{2,1,0:T(8,128)}, f32[8,1536,256]{2,1,0:T(8,128)}, f32[8,256,1536]{2,1,0:T(8,128)}, bf16[512,1536]{1,0:T(8,128)(2,1)}, f32[8,8,1536]{2,1,0:T(8,128)}) custom-call(bf16[8,128,1536]{2,1,0:T(8,128)(2,1)} %bitcast.8, bf16[8,128,1536]{2,1,0:T(8,128)(2,1)} %bitcast.9, bf16[8,128,256]{2,1,0:T(8,128)(2,1)} %get-tuple-element.21.h, ...), custom_call_target="tpu_custom_call" | custom-call | flops 2415919104 | bytes 45613056 | tf_op jit(solution)/shard_map/weight_grads/pallas_call | solution.py:558
  139.7 0.0 collective-permute-done
  139.8 2.7 %broadcast_select_fusion = bf16[512,1536]{1,0:T(8,128)(2,1)} fusion(bf16[512,1536]{1,0:T(8,128)(2,1)} %get-tuple-element.27, bf16[512,1536]{1,0:T(8,128)(2,1)} %collective-permute-done, pred[]{:T(512)S(6)} %eq.5), kind=kLoop, calls=%fused_computation | loop fusion | flops 786432 | bytes 4718593 | tf_op jit(solution)/shard_map/jit(_where)/select_n | solution.py:549
Async XLA Ops:
  119.8 19.9 %collective-permute-start = (bf16[512,1536]{1,0:T(8,128)(2,1)}, bf16[512,1536]{1,0:T(8,128)(2,1)}, u32[]{:S(2)}, u32[]{:S(2)}) collective-permute-start(bf16[512,1536]{1,0:T(8,128)(2,1)} %get-tuple-element.27), channel_id=1, source_target_pairs={{0,8},{9,1},{2,10},{11,3},{4,12},{13,5},{6,14},{15,7}} | collective-permute-start | bytes 4718600 | tf_op jit(solution)/shard_map/ppermute | solution.py:547

commit v7 on v6

--- a/solution.py
+++ b/solution.py
@@ -12,10 +12,10 @@
 I32 = jnp.int32
 MESH = pl.DeviceIdType.MESH
 GELU_COEF = 0.7978845608028654
-AHEAD = 3
-LAG = 2
-Y_STEP = 4
-Y_INNER = 2
+AHEAD = 8
+LAG = 3
+Y_STEP = 8
+Y_INNER = 0
 NN = (((1,), (0,)), ((), ()))
 NT = (((1,), (1,)), ((), ()))
 TN = (((0,), (0,)), ((), ()))
@@ -35,14 +35,14 @@
 
 def moe_kernel(
     tp_size, ep_size, cap,
-    ids1_ref, ids2_ref, x_hbm, dy_hbm, wr_hbm, wa_hbm, wb_hbm, wc_hbm,
+    ids1_hbm, ids2_hbm, x_hbm, dy_hbm, wr_hbm, wa_hbm, wb_hbm, wc_hbm,
     y_out, dx_out, dwr_out, xe_out, de_out, h_out, da_out, db_out,
     x_v, dy_v, wr_v, wa_v, wb_v, wc_v,
     xs, ds, xr, dr, h_v, da_v, db_v, bs_v, gv_v,
     ps, pr, pdr, orr, dxr, y_v, dx_v,
     s1r, s2r, g1r, g2r, s1c, s2c, g1c, g2c, q1c, q2c, i1c, i2c, prob_v, dl_v,
-    dwp, dwi, dwf, acc_v,
-    in_sem, w_sem, out_sem,
+    dwp, dwi, dwf, acc_v, ids1_ref, ids2_ref,
+    in_sem, w_sem, out_sem, id_sem,
     xs_sem, xr_sem, xd_sem, xf_sem, xfs_sem, ds_sem, dr_sem,
     ps_sem, pr_sem, pds_sem, pdr_sem,
     os_sem, or_sem, dxs_sem, dxr_sem,
@@ -66,6 +66,9 @@
         pltpu.make_async_copy(dy_hbm, dy_v, in_sem.at[1]),
         pltpu.make_async_copy(wr_hbm, wr_v, in_sem.at[2]),
     ]
+    id_loads = [pltpu.make_async_copy(ids1_hbm, ids1_ref, id_sem.at[0]), pltpu.make_async_copy(ids2_hbm, ids2_ref, id_sem.at[1])]
+    for c in id_loads:
+        c.start()
     ins[0].start()
 
     def weight_copies(j):
@@ -81,6 +84,8 @@
         flat = (k * ep_size + r + d) % n_dev
         pl.semaphore_signal(barrier, inc=1, device_id=(flat // ep_size, flat % ep_size), device_id_type=MESH)
 
+    for c in id_loads:
+        c.wait()
     ids1 = ids1_ref[...]
     ids2 = ids2_ref[...]
     e_iota = lax.broadcasted_iota(I32, (n_exp, n_tok), 0)
@@ -241,13 +246,16 @@
 
     @pl.loop(0, n_loc)
     def _(j):
-        @pl.when(j + AHEAD < n_loc)
-        def _():
-            build_x(j + AHEAD)
-
-        @pl.when(j + AHEAD >= n_loc)
-        def _():
-            build_d(j + AHEAD - n_loc)
+        if AHEAD < n_loc:
+            @pl.when(j + AHEAD < n_loc)
+            def _():
+                build_x(j + AHEAD)
+
+            @pl.when(j + AHEAD >= n_loc)
+            def _():
+                build_d(j + AHEAD - n_loc)
+        else:
+            build_d(j)
 
         @pl.when(j + 1 < n_loc)
         def _():
@@ -288,6 +296,11 @@
             src_ref=buf.at[toks], dst_ref=buf.at[toks], send_sem=send_sem, recv_sem=recv_sem,
             device_id=(other, r), device_id_type=MESH,
         ).start()
+
+    def wait_returned():
+        @pl.loop(0, n_loc)
+        def _(i):
+            wait_recv(orr.at[i, pl.ds(0, ep_size - 1)], or_sem.at[i])
 
     def combine_y(t):
         toks = pl.ds(pl.multiple_of(t * tb, tb), tb)
@@ -319,9 +332,10 @@
     wait_send(xs.at[:, pl.ds(0, n_near + 1)], xs_sem)
     @pl.loop(0, n_loc)
     def _(j):
-        @pl.when(j + AHEAD < n_loc)
-        def _():
-            build_d(j + AHEAD)
+        if AHEAD < n_loc:
+            @pl.when(j + AHEAD < n_loc)
+            def _():
+                build_d(j + AHEAD)
 
         wait_recv(dr.at[j, pl.ds(0, ep_size - 1)], dr_sem.at[j])
         rows = dr[j].reshape(blk, width)
@@ -344,15 +358,14 @@
         def _():
             merge_and_return(xs, pdr, pdr_sem, dxr, dxs_sem, dxr_sem, j - LAG)
 
-        @pl.when(owner & (j == Y_STEP))
-        def _():
-            @pl.loop(0, n_loc)
-            def _(i):
-                wait_recv(orr.at[i, pl.ds(0, ep_size - 1)], or_sem.at[i])
-
-        @pl.when(owner & (j >= Y_STEP) & (j < Y_STEP + Y_INNER))
-        def _():
-            combine_y(j - Y_STEP)
+        if Y_INNER > 0:
+            @pl.when(owner & (j == Y_STEP))
+            def _():
+                wait_returned()
+
+            @pl.when(owner & (j >= Y_STEP) & (j < Y_STEP + Y_INNER))
+            def _():
+                combine_y(j - Y_STEP)
 
     outs = [
         pltpu.make_async_copy(xr, xe_out, out_sem.at[0]),
@@ -387,11 +400,11 @@
             dx_v[toks, c:c + 512] = (acc_v[toks, c:c + 512] + dot(pick[:, split * blk:], rows)).astype(BF)
         pltpu.make_async_copy(dx_v.at[toks], dx_out.at[toks], in_sem.at[1]).start()
 
-    for i in range(LAG - 1):
-        merge_and_return(xs, pdr, pdr_sem, dxr, dxs_sem, dxr_sem, n_loc - LAG + i)
-
     @pl.when(owner)
     def _():
+        if Y_INNER == 0:
+            wait_returned()
+
         @pl.loop(Y_INNER, n_tb)
         def _(t):
             combine_y(t)
@@ -409,7 +422,9 @@
             ).start()
         dwi[r] = dwp[r]
 
-    merge_and_return(xs, pdr, pdr_sem, dxr, dxs_sem, dxr_sem, n_loc - 1)
+    for i in range(LAG):
+        merge_and_return(xs, pdr, pdr_sem, dxr, dxs_sem, dxr_sem, n_loc - LAG + i)
+
     for c in outs[3:]:
         c.start()
 
@@ -497,7 +512,6 @@
         half = ep_size // tp_size
         dma = pltpu.SemaphoreType.DMA
         any_spec = pl.BlockSpec(memory_space=pl.ANY)
-        vmem_spec = pl.BlockSpec(memory_space=pltpu.VMEM)
         sds = jax.ShapeDtypeStruct
         rows_shape = (n_loc, ep_size, cap, width)
         half_shape = (n_loc, half, cap, width)
@@ -507,7 +521,7 @@
         outs = pl.pallas_call(
             functools.partial(moe_kernel, tp_size, ep_size, cap),
             name="moe",
-            in_specs=[vmem_spec] * 2 + [any_spec] * 6,
+            in_specs=[any_spec] * 8,
             out_specs=[any_spec] * 8,
             out_shape=[
                 sds((n_tok, width), BF), sds((n_tok, width), BF), sds((ep_size, n_loc, width), F32),
@@ -526,7 +540,8 @@
                 pltpu.VMEM((n_tok, n_exp), F32), pltpu.VMEM((n_tok, n_exp), F32),
                 pltpu.VMEM((ep_size, n_loc, width), F32), pltpu.VMEM((ep_size, n_loc, width), F32),
                 pltpu.VMEM((ep_size, n_loc, width), F32), pltpu.VMEM((n_tok, width), F32),
-                dma((3,)), dma((3, n_loc)), dma((5,)),
+                pltpu.VMEM((1, n_tok), I32), pltpu.VMEM((1, n_tok), I32),
+                dma((3,)), dma((3, n_loc)), dma((5,)), dma((2,)),
                 dma(()), dma((n_loc,)), dma((n_loc,)), dma((n_loc,)), dma(()), dma(()), dma((n_loc,)),
                 dma(()), dma((n_loc,)), dma(()), dma((n_loc,)),
                 dma(()), dma((n_loc,)), dma(()), dma((n_loc,)),

time: 144 us -> 142 us (0.986)
  Pallas kernels: 136 us -> 134 us
    pallas_call x1, Pallas kernels: 119 us -> 117 us  [local_step(): pl.pallas_call(functools.partial(moe_kernel, tp_size, ep_size, cap), name...]
where the time goes in v7:
time: 142 us; the launch traced here: 141 us
  Pallas kernels  134 us (94%)
  starting transfers between devices  3.49 us (2%)
  other arithmetic  2.73 us (2%)
    pallas_call x1, Pallas kernels, local_step(): pl.pallas_call(functools.partial(moe_kernel, tp_size, ep_size, cap), name...  117 us
    pallas_call x1, Pallas kernels, local_step(): pl.pallas_call(weight_kernel, name='weight_grads', grid=(n_loc,), in_spec...  16.7 us
    ppermute x1, starting transfers between devices, local_step(): passed = lax.ppermute(grad_in, ('tp', 'ep'), partners)  3.49 us
  transfers between devices with their start and end apart: 1, of which 0 were waited for; matrix products, arithmetic and copies ran while one was open for 0% of the time, Pallas kernels for 12%

profile of v7, /device:TPU:0, one launch (start us, length us, event | category | flops | bytes accessed | tf_op | source)
XLA Modules:
  0.0 141.0 jit_solution(13241660520168980565)
XLA Ops:
  0.6 117.4 %moe.1 = (bf16[512,1536]{1,0:T(8,128)(2,1)}, bf16[512,1536]{1,0:T(8,128)(2,1)}, f32[8,8,1536]{2,1,0:T(8,128)}, bf16[8,8,16,1536]{3,2,1,0:T(8,128)(2,1)}, bf16[8,...) custom-call(s32[1,512]{1,0:T(1,128)} %bitcast.11, ...), custom_call_target="tpu_custom_call" | custom-call | tf_op jit(solution)/shard_map/moe/pallas_call | solution.py:521
  118.0 3.5 %collective-permute-start = (bf16[512,1536]{1,0:T(8,128)(2,1)}, bf16[512,1536]{1,0:T(8,128)(2,1)}, u32[]{:S(2)}, u32[]{:S(2)}) collective-permute-start(bf16[512,1536]{1,0:T(8,128)(2,1)} %get-tuple-element.27), channel_id=1, source_target_pairs={{0,8},{9,1},{2,10},{11,3},{4,12},{13,5},{6,14},{15,7}} | collective-permute-start | bytes 4718600 | tf_op jit(solution)/shard_map/ppermute | solution.py:562
  121.5 16.7 %weight_grads.1 = (f32[8,1536,256]{2,1,0:T(8,128)}, f32[8,1536,256]{2,1,0:T(8,128)}, f32[8,256,1536]{2,1,0:T(8,128)}, bf16[512,1536]{1,0:T(8,128)(2,1)}, f32[8,8,1536]{2,1,0:T(8,128)}) custom-call(bf16[8,128,1536]{2,1,0:T(8,128)(2,1)} %bitcast.8, bf16[8,128,1536]{2,1,0:T(8,128)(2,1)} %bitcast.9, bf16[8,128,256]{2,1,0:T(8,128)(2,1)} %get-tuple-element.21.h, ...), custom_call_target="tpu_custom_call" | custom-call | flops 2415919104 | bytes 45613056 | tf_op jit(solution)/shard_map/weight_grads/pallas_call | solution.py:573
  138.2 0.0 collective-permute-done
  138.3 2.7 %broadcast_select_fusion = bf16[512,1536]{1,0:T(8,128)(2,1)} fusion(bf16[512,1536]{1,0:T(8,128)(2,1)} %get-tuple-element.27, bf16[512,1536]{1,0:T(8,128)(2,1)} %collective-permute-done, pred[]{:T(512)S(6)} %eq.5), kind=kLoop, calls=%fused_computation | loop fusion | flops 786432 | bytes 4718593 | tf_op jit(solution)/shard_map/jit(_where)/select_n | solution.py:564
Async XLA Ops:
  118.0 20.2 %collective-permute-start = (bf16[512,1536]{1,0:T(8,128)(2,1)}, bf16[512,1536]{1,0:T(8,128)(2,1)}, u32[]{:S(2)}, u32[]{:S(2)}) collective-permute-start(bf16[512,1536]{1,0:T(8,128)(2,1)} %get-tuple-element.27), channel_id=1, source_target_pairs={{0,8},{9,1},{2,10},{11,3},{4,12},{13,5},{6,14},{15,7}} | collective-permute-start | bytes 4718600 | tf_op jit(solution)/shard_map/ppermute | solution.py:562

commit v8 on v6

--- a/solution.py
+++ b/solution.py
@@ -12,10 +12,10 @@
 I32 = jnp.int32
 MESH = pl.DeviceIdType.MESH
 GELU_COEF = 0.7978845608028654
-AHEAD = 3
-LAG = 2
-Y_STEP = 4
-Y_INNER = 2
+AHEAD = 5
+LAG = 3
+Y_STEP = 5
+FORWARD = 2
 NN = (((1,), (0,)), ((), ()))
 NT = (((1,), (1,)), ((), ()))
 TN = (((0,), (0,)), ((), ()))
@@ -35,19 +35,19 @@
 
 def moe_kernel(
     tp_size, ep_size, cap,
-    ids1_ref, ids2_ref, x_hbm, dy_hbm, wr_hbm, wa_hbm, wb_hbm, wc_hbm,
+    ids1_hbm, ids2_hbm, x_hbm, dy_hbm, wr_hbm, wa_hbm, wb_hbm, wc_hbm,
     y_out, dx_out, dwr_out, xe_out, de_out, h_out, da_out, db_out,
     x_v, dy_v, wr_v, wa_v, wb_v, wc_v,
     xs, ds, xr, dr, h_v, da_v, db_v, bs_v, gv_v,
     ps, pr, pdr, orr, dxr, y_v, dx_v,
     s1r, s2r, g1r, g2r, s1c, s2c, g1c, g2c, q1c, q2c, i1c, i2c, prob_v, dl_v,
-    dwp, dwi, dwf, acc_v,
-    in_sem, w_sem, out_sem,
+    dwp, dwi, dwf, acc_v, ids1_ref, ids2_ref,
+    in_sem, w_sem, out_sem, id_sem,
     xs_sem, xr_sem, xd_sem, xf_sem, xfs_sem, ds_sem, dr_sem,
     ps_sem, pr_sem, pds_sem, pdr_sem,
     os_sem, or_sem, dxs_sem, dxr_sem,
     ys_sem, yr_sem,
-    rs_sem, rr_sem, fs_sem, fr_sem,
+    rs_sem, rr_sem, fs_sem, fr_sem, gs_sem, gr_sem,
 ):
     k = lax.axis_index("tp")
     r = lax.axis_index("ep")
@@ -66,6 +66,9 @@
         pltpu.make_async_copy(dy_hbm, dy_v, in_sem.at[1]),
         pltpu.make_async_copy(wr_hbm, wr_v, in_sem.at[2]),
     ]
+    id_loads = [pltpu.make_async_copy(ids1_hbm, ids1_ref, id_sem.at[0]), pltpu.make_async_copy(ids2_hbm, ids2_ref, id_sem.at[1])]
+    for c in id_loads:
+        c.start()
     ins[0].start()
 
     def weight_copies(j):
@@ -81,6 +84,8 @@
         flat = (k * ep_size + r + d) % n_dev
         pl.semaphore_signal(barrier, inc=1, device_id=(flat // ep_size, flat % ep_size), device_id_type=MESH)
 
+    for c in id_loads:
+        c.wait()
     ids1 = ids1_ref[...]
     ids2 = ids2_ref[...]
     e_iota = lax.broadcasted_iota(I32, (n_exp, n_tok), 0)
@@ -157,7 +162,7 @@
 
     pl.semaphore_wait(barrier, n_dev - 1)
 
-    @pl.loop(0, AHEAD)
+    @pl.loop(0, n_loc)
     def _(j):
         build_x(j)
 
@@ -237,21 +242,18 @@
             device_id=(other, r), device_id_type=MESH,
         ).start()
 
-    forward_diag(0)
+    for i in range(FORWARD):
+        forward_diag(i)
 
     @pl.loop(0, n_loc)
     def _(j):
-        @pl.when(j + AHEAD < n_loc)
-        def _():
-            build_x(j + AHEAD)
-
-        @pl.when(j + AHEAD >= n_loc)
+        @pl.when(j >= n_loc - AHEAD)
         def _():
             build_d(j + AHEAD - n_loc)
 
-        @pl.when(j + 1 < n_loc)
-        def _():
-            forward_diag(j + 1)
+        @pl.when(j + FORWARD < n_loc)
+        def _():
+            forward_diag(j + FORWARD)
 
         for c in weight_copies(j):
             c.wait()
@@ -283,7 +285,8 @@
         base = col[toks, :]
         return jnp.concatenate([base == lanes + float(u * 128) for u in range(n_exp * cap // 128)], axis=1)
 
-    def ship(buf, toks, send_sem, recv_sem):
+    def ship(buf, t, send_sem, recv_sem):
+        toks = pl.ds(pl.multiple_of(t * tb, tb), tb)
         pltpu.make_async_remote_copy(
             src_ref=buf.at[toks], dst_ref=buf.at[toks], send_sem=send_sem, recv_sem=recv_sem,
             device_id=(other, r), device_id_type=MESH,
@@ -305,7 +308,6 @@
             dyf = dy_v[toks, c:c + 512].astype(F32)
             dg1 = dg1 + jnp.sum(dyf * o1, axis=1, keepdims=True)
             dg2 = dg2 + jnp.sum(dyf * o2, axis=1, keepdims=True)
-        ship(y_v, toks, ys_sem, yr_sem)
         qa = q1c[toks, 0:1]
         qb = q2c[toks, 0:1]
         shared = dg1 * ga + dg2 * gb
@@ -316,86 +318,7 @@
         pull = jnp.where(i1c[toks, :n_exp] == lanes, dq1, 0.0) + jnp.where(i2c[toks, :n_exp] == lanes, dq2, 0.0)
         dl_v[toks, :] = prob_v[toks, :] * (pull - centre)
 
-    wait_send(xs.at[:, pl.ds(0, n_near + 1)], xs_sem)
-    @pl.loop(0, n_loc)
-    def _(j):
-        @pl.when(j + AHEAD < n_loc)
-        def _():
-            build_d(j + AHEAD)
-
-        wait_recv(dr.at[j, pl.ds(0, ep_size - 1)], dr_sem.at[j])
-        rows = dr[j].reshape(blk, width)
-        dh = dot(rows, wc_v[j], NT)
-        da = (dh * bs_v[j]).astype(BF)
-        db = (dh * gv_v[j]).astype(BF)
-        da_v[j] = da
-        db_v[j] = db
-        for c in range(0, width, 512):
-            part = dot(da, wa_v[j, c:c + 512, :], NT) + dot(db, wb_v[j, c:c + 512, :], NT)
-            xs[j, :, :, c:c + 512] = part.astype(BF).reshape(ep_size, cap, 512)
-        send_half(xs, pdr, pds_sem, pdr_sem, j)
-
-        @pl.when(j == 0)
-        def _():
-            for i in range(LAG):
-                merge_and_return(ps, pr, pr_sem, orr, os_sem, or_sem, n_loc - LAG + i)
-
-        @pl.when(j >= LAG)
-        def _():
-            merge_and_return(xs, pdr, pdr_sem, dxr, dxs_sem, dxr_sem, j - LAG)
-
-        @pl.when(owner & (j == Y_STEP))
-        def _():
-            @pl.loop(0, n_loc)
-            def _(i):
-                wait_recv(orr.at[i, pl.ds(0, ep_size - 1)], or_sem.at[i])
-
-        @pl.when(owner & (j >= Y_STEP) & (j < Y_STEP + Y_INNER))
-        def _():
-            combine_y(j - Y_STEP)
-
-    outs = [
-        pltpu.make_async_copy(xr, xe_out, out_sem.at[0]),
-        pltpu.make_async_copy(dr, de_out, out_sem.at[1]),
-        pltpu.make_async_copy(h_v, h_out, out_sem.at[2]),
-        pltpu.make_async_copy(da_v, da_out, out_sem.at[3]),
-        pltpu.make_async_copy(db_v, db_out, out_sem.at[4]),
-    ]
-    for c in outs[:3]:
-        c.start()
-
-    split = n_loc - 2
-
-    def pick_both(t):
-        toks = pl.ds(pl.multiple_of(t * tb, tb), tb)
-        return toks, jnp.where(spots(s1c, toks) | spots(s2c, toks), 1.0, 0.0).astype(BF)
-
-    def sum_first(t):
-        toks, pick = pick_both(t)
-        dl = dl_v[toks, :]
-        for c in range(0, width, 512):
-            rows = dxr[0:split, :, :, c:c + 512].reshape(split * blk, 512)
-            router = lax.dot_general(
-                dl, wr_v[:, c:c + 512], NN, precision=lax.Precision.HIGHEST, preferred_element_type=F32
-            )
-            acc_v[toks, c:c + 512] = dot(pick[:, :split * blk], rows) + router
-
-    def sum_last(t):
-        toks, pick = pick_both(t)
-        for c in range(0, width, 512):
-            rows = dxr[split:n_loc, :, :, c:c + 512].reshape((n_loc - split) * blk, 512)
-            dx_v[toks, c:c + 512] = (acc_v[toks, c:c + 512] + dot(pick[:, split * blk:], rows)).astype(BF)
-        pltpu.make_async_copy(dx_v.at[toks], dx_out.at[toks], in_sem.at[1]).start()
-
-    for i in range(LAG - 1):
-        merge_and_return(xs, pdr, pdr_sem, dxr, dxs_sem, dxr_sem, n_loc - LAG + i)
-
-    @pl.when(owner)
-    def _():
-        @pl.loop(Y_INNER, n_tb)
-        def _(t):
-            combine_y(t)
-
+    def router_parts():
         d_hi, d_mid, d_low = split3(dl_v[...])
         for c in range(0, width, 512):
             xc = x_v[:, c:c + 512]
@@ -409,31 +332,120 @@
             ).start()
         dwi[r] = dwp[r]
 
-    merge_and_return(xs, pdr, pdr_sem, dxr, dxs_sem, dxr_sem, n_loc - 1)
+    wait_send(xs.at[:, pl.ds(0, n_near + 1)], xs_sem)
+    @pl.loop(0, n_loc)
+    def _(j):
+        @pl.when(j + AHEAD < n_loc)
+        def _():
+            build_d(j + AHEAD)
+
+        wait_recv(dr.at[j, pl.ds(0, ep_size - 1)], dr_sem.at[j])
+        rows = dr[j].reshape(blk, width)
+        dh = dot(rows, wc_v[j], NT)
+        da = (dh * bs_v[j]).astype(BF)
+        db = (dh * gv_v[j]).astype(BF)
+        da_v[j] = da
+        db_v[j] = db
+        for c in range(0, width, 512):
+            part = dot(da, wa_v[j, c:c + 512, :], NT) + dot(db, wb_v[j, c:c + 512, :], NT)
+            xs[j, :, :, c:c + 512] = part.astype(BF).reshape(ep_size, cap, 512)
+        send_half(xs, pdr, pds_sem, pdr_sem, j)
+
+        @pl.when(j == 0)
+        def _():
+            for i in range(LAG):
+                merge_and_return(ps, pr, pr_sem, orr, os_sem, or_sem, n_loc - LAG + i)
+
+        @pl.when(j >= LAG)
+        def _():
+            merge_and_return(xs, pdr, pdr_sem, dxr, dxs_sem, dxr_sem, j - LAG)
+
+        @pl.when(owner & (j == Y_STEP))
+        def _():
+            @pl.loop(0, n_loc)
+            def _(i):
+                wait_recv(orr.at[i, pl.ds(0, ep_size - 1)], or_sem.at[i])
+
+        @pl.when(owner & (j >= Y_STEP) & (j < Y_STEP + n_tb // 2))
+        def _():
+            t0 = 2 * (j - Y_STEP)
+
+            @pl.loop(t0, t0 + 2)
+            def _(t):
+                combine_y(t)
+
+            ship(y_v, j - Y_STEP, ys_sem, yr_sem)
+
+        @pl.when(owner & (j == Y_STEP + n_tb // 2 - 1))
+        def _():
+            router_parts()
+
+    outs = [
+        pltpu.make_async_copy(xr, xe_out, out_sem.at[0]),
+        pltpu.make_async_copy(dr, de_out, out_sem.at[1]),
+        pltpu.make_async_copy(h_v, h_out, out_sem.at[2]),
+        pltpu.make_async_copy(da_v, da_out, out_sem.at[3]),
+        pltpu.make_async_copy(db_v, db_out, out_sem.at[4]),
+    ]
+    for c in outs[:3]:
+        c.start()
+
+    split = n_loc - 2
+
+    def pick_both(t):
+        toks = pl.ds(pl.multiple_of(t * tb, tb), tb)
+        return toks, jnp.where(spots(s1c, toks) | spots(s2c, toks), 1.0, 0.0).astype(BF)
+
+    def sum_first(t):
+        toks, pick = pick_both(t)
+        dl = dl_v[toks, :]
+        for c in range(0, width, 512):
+            rows = dxr[0:split, :, :, c:c + 512].reshape(split * blk, 512)
+            router = lax.dot_general(
+                dl, wr_v[:, c:c + 512], NN, precision=lax.Precision.HIGHEST, preferred_element_type=F32
+            )
+            acc_v[toks, c:c + 512] = dot(pick[:, :split * blk], rows) + router
+
+    def sum_last(t):
+        toks, pick = pick_both(t)
+        for c in range(0, width, 512):
+            rows = dxr[split:n_loc, :, :, c:c + 512].reshape((n_loc - split) * blk, 512)
+            dx_v[toks, c:c + 512] = (acc_v[toks, c:c + 512] + dot(pick[:, split * blk:], rows)).astype(BF)
+        pltpu.make_async_copy(dx_v.at[toks], dx_out.at[toks], in_sem.at[1]).start()
+
+    @pl.when(owner)
+    def _():
+        @pl.loop(n_tb // 2, n_tb)
+        def _(t):
+            ship(y_v, t, ys_sem, yr_sem)
+
+    for i in range(LAG):
+        merge_and_return(xs, pdr, pdr_sem, dxr, dxs_sem, dxr_sem, n_loc - LAG + i)
+
     for c in outs[3:]:
         c.start()
 
     @pl.when(owner)
     def _():
-        @pl.loop(0, split)
-        def _(j):
-            wait_recv(dxr.at[j, pl.ds(0, ep_size - 1)], dxr_sem.at[j])
-
-        @pl.loop(0, n_tb)
-        def _(t):
-            sum_first(t)
-
         wait_recv(dwi.at[pl.ds(0, ep_size - 1)], rr_sem)
         total = dwi[0]
         for q in range(1, ep_size):
             total = total + dwi[q]
         dwf[r] = total
-        for d in range(1, n_dev):
-            flat = (k * ep_size + r + d) % n_dev
+        for d in range(1, ep_size):
+            q = (r + d) % ep_size
             pltpu.make_async_remote_copy(
                 src_ref=dwf.at[r], dst_ref=dwf.at[r], send_sem=fs_sem, recv_sem=fr_sem,
-                device_id=(flat // ep_size, flat % ep_size), device_id_type=MESH,
+                device_id=(q % tp_size, q), device_id_type=MESH,
             ).start()
+
+        @pl.loop(0, split)
+        def _(j):
+            wait_recv(dxr.at[j, pl.ds(0, ep_size - 1)], dxr_sem.at[j])
+
+        @pl.loop(0, n_tb)
+        def _(t):
+            sum_first(t)
 
         @pl.loop(split, n_loc)
         def _(j):
@@ -444,9 +456,13 @@
             sum_last(t)
 
         wait_recv(dwf.at[pl.ds(0, ep_size - 1)], fr_sem)
+        pltpu.make_async_remote_copy(
+            src_ref=dwf, dst_ref=dwf, send_sem=gs_sem, recv_sem=gr_sem,
+            device_id=(k, 2 * chip + 1 - core), device_id_type=MESH,
+        ).start()
         wait_send(dwp.at[pl.ds(0, ep_size - 1)], rs_sem)
-        for half_sends in range(n_dev - 1):
-            wait_send(dwf.at[r], fs_sem)
+        wait_send(dwf.at[pl.ds(0, ep_size - 1)], fs_sem)
+        wait_send(dwf, gs_sem)
         wait_send(y_v, ys_sem)
         wait_send(orr.at[:, pl.ds(0, half - 1)], os_sem)
         wait_send(dxr.at[:, pl.ds(0, half - 1)], dxs_sem)
@@ -456,7 +472,7 @@
         dx_v[...] = jnp.zeros_like(dx_v)
         pltpu.make_async_copy(dx_v, dx_out, in_sem.at[1]).start()
         wait_recv(y_v, yr_sem)
-        wait_recv(dwf, fr_sem)
+        wait_recv(dwf, gr_sem)
         wait_send(orr.at[:, pl.ds(0, half)], os_sem)
         wait_send(dxr.at[:, pl.ds(0, half)], dxs_sem)
 
@@ -497,7 +513,6 @@
         half = ep_size // tp_size
         dma = pltpu.SemaphoreType.DMA
         any_spec = pl.BlockSpec(memory_space=pl.ANY)
-        vmem_spec = pl.BlockSpec(memory_space=pltpu.VMEM)
         sds = jax.ShapeDtypeStruct
         rows_shape = (n_loc, ep_size, cap, width)
         half_shape = (n_loc, half, cap, width)
@@ -507,7 +522,7 @@
         outs = pl.pallas_call(
             functools.partial(moe_kernel, tp_size, ep_size, cap),
             name="moe",
-            in_specs=[vmem_spec] * 2 + [any_spec] * 6,
+            in_specs=[any_spec] * 8,
             out_specs=[any_spec] * 8,
             out_shape=[
                 sds((n_tok, width), BF), sds((n_tok, width), BF), sds((ep_size, n_loc, width), F32),
@@ -526,12 +541,13 @@
                 pltpu.VMEM((n_tok, n_exp), F32), pltpu.VMEM((n_tok, n_exp), F32),
                 pltpu.VMEM((ep_size, n_loc, width), F32), pltpu.VMEM((ep_size, n_loc, width), F32),
                 pltpu.VMEM((ep_size, n_loc, width), F32), pltpu.VMEM((n_tok, width), F32),
-                dma((3,)), dma((3, n_loc)), dma((5,)),
+                pltpu.VMEM((1, n_tok), I32), pltpu.VMEM((1, n_tok), I32),
+                dma((3,)), dma((3, n_loc)), dma((5,)), dma((2,)),
                 dma(()), dma((n_loc,)), dma((n_loc,)), dma((n_loc,)), dma(()), dma(()), dma((n_loc,)),
                 dma(()), dma((n_loc,)), dma(()), dma((n_loc,)),
                 dma(()), dma((n_loc,)), dma(()), dma((n_loc,)),
                 dma(()), dma(()),
-                dma(()), dma(()), dma(()), dma(()),
+                dma(()), dma(()), dma(()), dma(()), dma(()), dma(()),
             ],
             compiler_params=pltpu.CompilerParams(
                 collective_id=0, has_side_effects=True, vmem_limit_bytes=67043328

time: 144 us -> 139 us (0.965)
  Pallas kernels: 136 us -> 131 us
    pallas_call x1, Pallas kernels: 119 us -> 115 us  [local_step(): pl.pallas_call(functools.partial(moe_kernel, tp_size, ep_size, cap), name...]
where the time goes in v8:
time: 139 us; the launch traced here: 138 us
  Pallas kernels  131 us (94%)
  starting transfers between devices  3.43 us (2%)
  other arithmetic  2.73 us (2%)
    pallas_call x1, Pallas kernels, local_step(): pl.pallas_call(functools.partial(moe_kernel, tp_size, ep_size, cap), name...  115 us
    pallas_call x1, Pallas kernels, local_step(): pl.pallas_call(weight_kernel, name='weight_grads', grid=(n_loc,), in_spec...  16.7 us
    ppermute x1, starting transfers between devices, local_step(): passed = lax.ppermute(grad_in, ('tp', 'ep'), partners)  3.43 us
  transfers between devices with their start and end apart: 1, of which 0 were waited for; matrix products, arithmetic and copies ran while one was open for 0% of the time, Pallas kernels for 12%

profile of v8, /device:TPU:0, one launch (start us, length us, event | category | flops | bytes accessed | tf_op | source)
XLA Modules:
  0.0 138.2 jit_solution(15311873505822654048)
XLA Ops:
  0.6 114.7 %moe.1 = (bf16[512,1536]{1,0:T(8,128)(2,1)}, bf16[512,1536]{1,0:T(8,128)(2,1)}, f32[8,8,1536]{2,1,0:T(8,128)}, bf16[8,8,16,1536]{3,2,1,0:T(8,128)(2,1)}, bf16[8,...) custom-call(s32[1,512]{1,0:T(1,128)} %bitcast.11, ...), custom_call_target="tpu_custom_call" | custom-call | tf_op jit(solution)/shard_map/moe/pallas_call | solution.py:522
  115.3 3.4 %collective-permute-start = (bf16[512,1536]{1,0:T(8,128)(2,1)}, bf16[512,1536]{1,0:T(8,128)(2,1)}, u32[]{:S(2)}, u32[]{:S(2)}) collective-permute-start(bf16[512,1536]{1,0:T(8,128)(2,1)} %get-tuple-element.27), channel_id=1, source_target_pairs={{0,8},{9,1},{2,10},{11,3},{4,12},{13,5},{6,14},{15,7}} | collective-permute-start | bytes 4718600 | tf_op jit(solution)/shard_map/ppermute | solution.py:563
  118.8 16.7 %weight_grads.1 = (f32[8,1536,256]{2,1,0:T(8,128)}, f32[8,1536,256]{2,1,0:T(8,128)}, f32[8,256,1536]{2,1,0:T(8,128)}, bf16[512,1536]{1,0:T(8,128)(2,1)}, f32[8,8,1536]{2,1,0:T(8,128)}) custom-call(bf16[8,128,1536]{2,1,0:T(8,128)(2,1)} %bitcast.8, bf16[8,128,1536]{2,1,0:T(8,128)(2,1)} %bitcast.9, bf16[8,128,256]{2,1,0:T(8,128)(2,1)} %get-tuple-element.21.h, ...), custom_call_target="tpu_custom_call" | custom-call | flops 2415919104 | bytes 45613056 | tf_op jit(solution)/shard_map/weight_grads/pallas_call | solution.py:574
  135.5 0.0 collective-permute-done
  135.5 2.7 %broadcast_select_fusion = bf16[512,1536]{1,0:T(8,128)(2,1)} fusion(bf16[512,1536]{1,0:T(8,128)(2,1)} %get-tuple-element.27, bf16[512,1536]{1,0:T(8,128)(2,1)} %collective-permute-done, pred[]{:T(512)S(6)} %eq.5), kind=kLoop, calls=%fused_computation | loop fusion | flops 786432 | bytes 4718593 | tf_op jit(solution)/shard_map/jit(_where)/select_n | solution.py:565
Async XLA Ops:
  115.3 20.2 %collective-permute-start = (bf16[512,1536]{1,0:T(8,128)(2,1)}, bf16[512,1536]{1,0:T(8,128)(2,1)}, u32[]{:S(2)}, u32[]{:S(2)}) collective-permute-start(bf16[512,1536]{1,0:T(8,128)(2,1)} %get-tuple-element.27), channel_id=1, source_target_pairs={{0,8},{9,1},{2,10},{11,3},{4,12},{13,5},{6,14},{15,7}} | collective-permute-start | bytes 4718600 | tf_op jit(solution)/shard_map/ppermute | solution.py:563

commit v9 on v8

--- a/solution.py
+++ b/solution.py
@@ -16,6 +16,7 @@
 LAG = 3
 Y_STEP = 5
 FORWARD = 2
+VIA_TP = 6
 NN = (((1,), (0,)), ((), ()))
 NT = (((1,), (1,)), ((), ()))
 TN = (((0,), (0,)), ((), ()))
@@ -140,14 +141,15 @@
             src_ref=view, dst_ref=view, send_sem=sem, recv_sem=sem, device_id=(k, r), device_id_type=MESH
         ).wait_send()
 
-    def build_x(j):
+    def build_x(j, via_tp):
         m1, m2 = masks(j)
         pick = jnp.where(m1 | m2, 1.0, 0.0).astype(BF)
         for c in range(0, width, 512):
             rows = dot(pick, x_v[:, c:c + 512]).astype(BF)
             xs[j, :, :, c:c + 512] = rows.reshape(ep_size, cap, 512)
-        send_row(xs, xr, xs_sem, xd_sem, j, diag)
-        for q in near:
+        if via_tp:
+            send_row(xs, xr, xs_sem, xd_sem, j, diag)
+        for q in near if via_tp else far + near:
             send_row(xs, xr, xs_sem, xr_sem, j, q)
         xr[j, my_place] = xs[j, r]
 
@@ -162,9 +164,13 @@
 
     pl.semaphore_wait(barrier, n_dev - 1)
 
-    @pl.loop(0, n_loc)
+    @pl.loop(0, VIA_TP)
     def _(j):
-        build_x(j)
+        build_x(j, True)
+
+    @pl.loop(VIA_TP, n_loc)
+    def _(j):
+        build_x(j, False)
 
     def column(row):
         return jnp.transpose(jnp.broadcast_to(row, (128, n_tok)))
@@ -251,14 +257,22 @@
         def _():
             build_d(j + AHEAD - n_loc)
 
-        @pl.when(j + FORWARD < n_loc)
+        @pl.when(j + FORWARD < VIA_TP)
         def _():
             forward_diag(j + FORWARD)
 
         for c in weight_copies(j):
             c.wait()
-        wait_recv(xr.at[j, pl.ds(0, n_near)], xr_sem.at[j])
-        wait_recv(xr.at[j, 0], xf_sem.at[j])
+
+        @pl.when(j < VIA_TP)
+        def _():
+            wait_recv(xr.at[j, pl.ds(0, n_near)], xr_sem.at[j])
+            wait_recv(xr.at[j, 0], xf_sem.at[j])
+
+        @pl.when(j >= VIA_TP)
+        def _():
+            wait_recv(xr.at[j, pl.ds(0, ep_size - 1)], xr_sem.at[j])
+
         rows = xr[j].reshape(blk, width)
         pa = dot(rows, wa_v[j])
         pb = dot(rows, wb_v[j])
@@ -332,101 +346,7 @@
             ).start()
         dwi[r] = dwp[r]
 
-    wait_send(xs.at[:, pl.ds(0, n_near + 1)], xs_sem)
-    @pl.loop(0, n_loc)
-    def _(j):
-        @pl.when(j + AHEAD < n_loc)
-        def _():
-            build_d(j + AHEAD)
-
-        wait_recv(dr.at[j, pl.ds(0, ep_size - 1)], dr_sem.at[j])
-        rows = dr[j].reshape(blk, width)
-        dh = dot(rows, wc_v[j], NT)
-        da = (dh * bs_v[j]).astype(BF)
-        db = (dh * gv_v[j]).astype(BF)
-        da_v[j] = da
-        db_v[j] = db
-        for c in range(0, width, 512):
-            part = dot(da, wa_v[j, c:c + 512, :], NT) + dot(db, wb_v[j, c:c + 512, :], NT)
-            xs[j, :, :, c:c + 512] = part.astype(BF).reshape(ep_size, cap, 512)
-        send_half(xs, pdr, pds_sem, pdr_sem, j)
-
-        @pl.when(j == 0)
-        def _():
-            for i in range(LAG):
-                merge_and_return(ps, pr, pr_sem, orr, os_sem, or_sem, n_loc - LAG + i)
-
-        @pl.when(j >= LAG)
-        def _():
-            merge_and_return(xs, pdr, pdr_sem, dxr, dxs_sem, dxr_sem, j - LAG)
-
-        @pl.when(owner & (j == Y_STEP))
-        def _():
-            @pl.loop(0, n_loc)
-            def _(i):
-                wait_recv(orr.at[i, pl.ds(0, ep_size - 1)], or_sem.at[i])
-
-        @pl.when(owner & (j >= Y_STEP) & (j < Y_STEP + n_tb // 2))
-        def _():
-            t0 = 2 * (j - Y_STEP)
-
-            @pl.loop(t0, t0 + 2)
-            def _(t):
-                combine_y(t)
-
-            ship(y_v, j - Y_STEP, ys_sem, yr_sem)
-
-        @pl.when(owner & (j == Y_STEP + n_tb // 2 - 1))
-        def _():
-            router_parts()
-
-    outs = [
-        pltpu.make_async_copy(xr, xe_out, out_sem.at[0]),
-        pltpu.make_async_copy(dr, de_out, out_sem.at[1]),
-        pltpu.make_async_copy(h_v, h_out, out_sem.at[2]),
-        pltpu.make_async_copy(da_v, da_out, out_sem.at[3]),
-        pltpu.make_async_copy(db_v, db_out, out_sem.at[4]),
-    ]
-    for c in outs[:3]:
-        c.start()
-
-    split = n_loc - 2
-
-    def pick_both(t):
-        toks = pl.ds(pl.multiple_of(t * tb, tb), tb)
-        return toks, jnp.where(spots(s1c, toks) | spots(s2c, toks), 1.0, 0.0).astype(BF)
-
-    def sum_first(t):
-        toks, pick = pick_both(t)
-        dl = dl_v[toks, :]
-        for c in range(0, width, 512):
-            rows = dxr[0:split, :, :, c:c + 512].reshape(split * blk, 512)
-            router = lax.dot_general(
-                dl, wr_v[:, c:c + 512], NN, precision=lax.Precision.HIGHEST, preferred_element_type=F32
-            )
-            acc_v[toks, c:c + 512] = dot(pick[:, :split * blk], rows) + router
-
-    def sum_last(t):
-        toks, pick = pick_both(t)
-        for c in range(0, width, 512):
-            rows = dxr[split:n_loc, :, :, c:c + 512].reshape((n_loc - split) * blk, 512)
-            dx_v[toks, c:c + 512] = (acc_v[toks, c:c + 512] + dot(pick[:, split * blk:], rows)).astype(BF)
-        pltpu.make_async_copy(dx_v.at[toks], dx_out.at[toks], in_sem.at[1]).start()
-
-    @pl.when(owner)
-    def _():
-        @pl.loop(n_tb // 2, n_tb)
-        def _(t):
-            ship(y_v, t, ys_sem, yr_sem)
-
-    for i in range(LAG):
-        merge_and_return(xs, pdr, pdr_sem, dxr, dxs_sem, dxr_sem, n_loc - LAG + i)
-
-    for c in outs[3:]:
-        c.start()
-
-    @pl.when(owner)
-    def _():
+    def router_sum():
         wait_recv(dwi.at[pl.ds(0, ep_size - 1)], rr_sem)
         total = dwi[0]
         for q in range(1, ep_size):
@@ -439,6 +359,107 @@
                 device_id=(q % tp_size, q), device_id_type=MESH,
             ).start()
 
+    wait_send(xs.at[pl.ds(0, VIA_TP), pl.ds(0, n_near + 1)], xs_sem)
+    wait_send(xs.at[pl.ds(VIA_TP, n_loc - VIA_TP), pl.ds(0, ep_size - 1)], xs_sem)
+    @pl.loop(0, n_loc)
+    def _(j):
+        @pl.when(j + AHEAD < n_loc)
+        def _():
+            build_d(j + AHEAD)
+
+        wait_recv(dr.at[j, pl.ds(0, ep_size - 1)], dr_sem.at[j])
+        rows = dr[j].reshape(blk, width)
+        dh = dot(rows, wc_v[j], NT)
+        da = (dh * bs_v[j]).astype(BF)
+        db = (dh * gv_v[j]).astype(BF)
+        da_v[j] = da
+        db_v[j] = db
+        for c in range(0, width, 512):
+            part = dot(da, wa_v[j, c:c + 512, :], NT) + dot(db, wb_v[j, c:c + 512, :], NT)
+            xs[j, :, :, c:c + 512] = part.astype(BF).reshape(ep_size, cap, 512)
+        send_half(xs, pdr, pds_sem, pdr_sem, j)
+
+        @pl.when(j == 0)
+        def _():
+            for i in range(LAG):
+                merge_and_return(ps, pr, pr_sem, orr, os_sem, or_sem, n_loc - LAG + i)
+
+        @pl.when(j >= LAG)
+        def _():
+            merge_and_return(xs, pdr, pdr_sem, dxr, dxs_sem, dxr_sem, j - LAG)
+
+        @pl.when(owner & (j == Y_STEP))
+        def _():
+            @pl.loop(0, n_loc)
+            def _(i):
+                wait_recv(orr.at[i, pl.ds(0, ep_size - 1)], or_sem.at[i])
+
+        @pl.when(owner & (j >= Y_STEP) & (j < Y_STEP + n_tb // 2))
+        def _():
+            t0 = 2 * (j - Y_STEP)
+
+            @pl.loop(t0, t0 + 2)
+            def _(t):
+                combine_y(t)
+
+            ship(y_v, j - Y_STEP, ys_sem, yr_sem)
+
+        @pl.when(owner & (j == Y_STEP + n_tb // 2 - 1))
+        def _():
+            router_parts()
+
+    outs = [
+        pltpu.make_async_copy(xr, xe_out, out_sem.at[0]),
+        pltpu.make_async_copy(dr, de_out, out_sem.at[1]),
+        pltpu.make_async_copy(h_v, h_out, out_sem.at[2]),
+        pltpu.make_async_copy(da_v, da_out, out_sem.at[3]),
+        pltpu.make_async_copy(db_v, db_out, out_sem.at[4]),
+    ]
+    for c in outs[:3]:
+        c.start()
+
+    split = n_loc - 2
+
+    def pick_both(t):
+        toks = pl.ds(pl.multiple_of(t * tb, tb), tb)
+        return toks, jnp.where(spots(s1c, toks) | spots(s2c, toks), 1.0, 0.0).astype(BF)
+
+    def sum_first(t):
+        toks, pick = pick_both(t)
+        dl = dl_v[toks, :]
+        for c in range(0, width, 512):
+            rows = dxr[0:split, :, :, c:c + 512].reshape(split * blk, 512)
+            router = lax.dot_general(
+                dl, wr_v[:, c:c + 512], NN, precision=lax.Precision.HIGHEST, preferred_element_type=F32
+            )
+            acc_v[toks, c:c + 512] = dot(pick[:, :split * blk], rows) + router
+
+    def sum_last(t):
+        toks, pick = pick_both(t)
+        for c in range(0, width, 512):
+            rows = dxr[split:n_loc, :, :, c:c + 512].reshape((n_loc - split) * blk, 512)
+            dx_v[toks, c:c + 512] = (acc_v[toks, c:c + 512] + dot(pick[:, split * blk:], rows)).astype(BF)
+        pltpu.make_async_copy(dx_v.at[toks], dx_out.at[toks], in_sem.at[1]).start()
+
+    for c in outs[3:]:
+        c.start()
+
+    @pl.when(owner)
+    def _():
+        ship(y_v, n_tb - 2, ys_sem, yr_sem)
+
+    for i in range(LAG - 1):
+        merge_and_return(xs, pdr, pdr_sem, dxr, dxs_sem, dxr_sem, n_loc - LAG + i)
+
+    @pl.when(owner)
+    def _():
+        router_sum()
+        ship(y_v, n_tb - 1, ys_sem, yr_sem)
+
+    merge_and_return(xs, pdr, pdr_sem, dxr, dxs_sem, dxr_sem, n_loc - 1)
+
+    @pl.when(owner)
+    def _():
         @pl.loop(0, split)
         def _(j):
             wait_recv(dxr.at[j, pl.ds(0, ep_size - 1)], dxr_sem.at[j])
@@ -484,7 +505,7 @@
         c.start()
     finals.append(pltpu.make_async_copy(dx_v, dx_out, in_sem.at[1]))
     wait_send(ds.at[:, pl.ds(0, ep_size - 1)], ds_sem)
-    wait_send(xr.at[:, 0], xfs_sem)
+    wait_send(xr.at[pl.ds(0, VIA_TP), 0], xfs_sem)
     wait_send(ps.at[:, pl.ds(0, half)], ps_sem)
     wait_send(xs.at[:, pl.ds(0, half)], pds_sem)
     for c in outs + finals:

time: 139 us -> 139 us (level)
  starting transfers between devices: 3.43 us -> 5.59 us
  Pallas kernels: 131 us -> 129 us
    pallas_call x1, Pallas kernels: 115 us -> 113 us  [local_step(): pl.pallas_call(functools.partial(moe_kernel, tp_size, ep_size, cap), name...]
    ppermute x1, starting transfers between devices: 3.43 us -> 5.59 us  [local_step(): passed = lax.ppermute(grad_in, ('tp', 'ep'), partners)]
where the time goes in v9:
time: 139 us; the launch traced here: 138 us
  Pallas kernels  129 us (93%)
  starting transfers between devices  5.59 us (4%)
  other arithmetic  2.73 us (2%)
    pallas_call x1, Pallas kernels, local_step(): pl.pallas_call(functools.partial(moe_kernel, tp_size, ep_size, cap), name...  113 us
    pallas_call x1, Pallas kernels, local_step(): pl.pallas_call(weight_kernel, name='weight_grads', grid=(n_loc,), in_spec...  16.7 us
    ppermute x1, starting transfers between devices, local_step(): passed = lax.ppermute(grad_in, ('tp', 'ep'), partners)  5.59 us
  transfers between devices with their start and end apart: 1, of which 0 were waited for; matrix products, arithmetic and copies ran while one was open for 0% of the time, Pallas kernels for 12%

profile of v9, /device:TPU:0, one launch (start us, length us, event | category | flops | bytes accessed | tf_op | source)
XLA Modules:
  0.0 138.2 jit_solution(8598499541938088559)
XLA Ops:
  0.6 112.5 %moe.1 = (bf16[512,1536]{1,0:T(8,128)(2,1)}, bf16[512,1536]{1,0:T(8,128)(2,1)}, f32[8,8,1536]{2,1,0:T(8,128)}, bf16[8,8,16,1536]{3,2,1,0:T(8,128)(2,1)}, bf16[8,...) custom-call(s32[1,512]{1,0:T(1,128)} %bitcast.11, ...), custom_call_target="tpu_custom_call" | custom-call | tf_op jit(solution)/shard_map/moe/pallas_call | solution.py:543
  113.2 5.6 %collective-permute-start = (bf16[512,1536]{1,0:T(8,128)(2,1)}, bf16[512,1536]{1,0:T(8,128)(2,1)}, u32[]{:S(2)}, u32[]{:S(2)}) collective-permute-start(bf16[512,1536]{1,0:T(8,128)(2,1)} %get-tuple-element.27), channel_id=1, source_target_pairs={{0,8},{9,1},{2,10},{11,3},{4,12},{13,5},{6,14},{15,7}} | collective-permute-start | bytes 4718600 | tf_op jit(solution)/shard_map/ppermute | solution.py:584
  118.7 16.7 %weight_grads.1 = (f32[8,1536,256]{2,1,0:T(8,128)}, f32[8,1536,256]{2,1,0:T(8,128)}, f32[8,256,1536]{2,1,0:T(8,128)}, bf16[512,1536]{1,0:T(8,128)(2,1)}, f32[8,8,1536]{2,1,0:T(8,128)}) custom-call(bf16[8,128,1536]{2,1,0:T(8,128)(2,1)} %bitcast.8, bf16[8,128,1536]{2,1,0:T(8,128)(2,1)} %bitcast.9, bf16[8,128,256]{2,1,0:T(8,128)(2,1)} %get-tuple-element.21.h, ...), custom_call_target="tpu_custom_call" | custom-call | flops 2415919104 | bytes 45613056 | tf_op jit(solution)/shard_map/weight_grads/pallas_call | solution.py:595
  135.5 0.0 collective-permute-done
  135.5 2.7 %broadcast_select_fusion = bf16[512,1536]{1,0:T(8,128)(2,1)} fusion(bf16[512,1536]{1,0:T(8,128)(2,1)} %get-tuple-element.27, bf16[512,1536]{1,0:T(8,128)(2,1)} %collective-permute-done, pred[]{:T(512)S(6)} %eq.5), kind=kLoop, calls=%fused_computation | loop fusion | flops 786432 | bytes 4718593 | tf_op jit(solution)/shard_map/jit(_where)/select_n | solution.py:586
Async XLA Ops:
  113.2 22.3 %collective-permute-start = (bf16[512,1536]{1,0:T(8,128)(2,1)}, bf16[512,1536]{1,0:T(8,128)(2,1)}, u32[]{:S(2)}, u32[]{:S(2)}) collective-permute-start(bf16[512,1536]{1,0:T(8,128)(2,1)} %get-tuple-element.27), channel_id=1, source_target_pairs={{0,8},{9,1},{2,10},{11,3},{4,12},{13,5},{6,14},{15,7}} | collective-permute-start | bytes 4718600 | tf_op jit(solution)/shard_map/ppermute | solution.py:584

commit v10 on v9

--- a/solution.py
+++ b/solution.py
@@ -16,7 +16,7 @@
 LAG = 3
 Y_STEP = 5
 FORWARD = 2
-VIA_TP = 6
+VIA_TP = 4
 NN = (((1,), (0,)), ((), ()))
 NT = (((1,), (1,)), ((), ()))
 TN = (((0,), (0,)), ((), ()))
@@ -302,7 +302,7 @@
     def ship(buf, t, send_sem, recv_sem):
         toks = pl.ds(pl.multiple_of(t * tb, tb), tb)
         pltpu.make_async_remote_copy(
-            src_ref=buf.at[toks], dst_ref=buf.at[toks], send_sem=send_sem, recv_sem=recv_sem,
+            src_ref=buf.at[toks], dst_ref=buf.at[toks], send_sem=send_sem, recv_sem=recv_sem.at[t],
             device_id=(other, r), device_id_type=MESH,
         ).start()
 
@@ -455,6 +455,7 @@
     def _():
         router_sum()
         ship(y_v, n_tb - 1, ys_sem, yr_sem)
+        pltpu.make_async_copy(y_v, y_out, in_sem.at[0]).start()
 
     merge_and_return(xs, pdr, pdr_sem, dxr, dxs_sem, dxr_sem, n_loc - 1)
 
@@ -468,19 +469,20 @@
         def _(t):
             sum_first(t)
 
-        @pl.loop(split, n_loc)
-        def _(j):
-            wait_recv(dxr.at[j, pl.ds(0, ep_size - 1)], dxr_sem.at[j])
-
-        @pl.loop(0, n_tb)
-        def _(t):
-            sum_last(t)
-
         wait_recv(dwf.at[pl.ds(0, ep_size - 1)], fr_sem)
         pltpu.make_async_remote_copy(
             src_ref=dwf, dst_ref=dwf, send_sem=gs_sem, recv_sem=gr_sem,
             device_id=(k, 2 * chip + 1 - core), device_id_type=MESH,
         ).start()
+
+        @pl.loop(split, n_loc)
+        def _(j):
+            wait_recv(dxr.at[j, pl.ds(0, ep_size - 1)], dxr_sem.at[j])
+
+        @pl.loop(0, n_tb)
+        def _(t):
+            sum_last(t)
+
         wait_send(dwp.at[pl.ds(0, ep_size - 1)], rs_sem)
         wait_send(dwf.at[pl.ds(0, ep_size - 1)], fs_sem)
         wait_send(dwf, gs_sem)
@@ -492,18 +494,20 @@
     def _():
         dx_v[...] = jnp.zeros_like(dx_v)
         pltpu.make_async_copy(dx_v, dx_out, in_sem.at[1]).start()
-        wait_recv(y_v, yr_sem)
+        for t in range(n_tb):
+            toks = pl.ds(t * tb, tb)
+            wait_recv(y_v.at[toks], yr_sem.at[t])
+            pltpu.make_async_copy(y_v.at[toks], y_out.at[toks], in_sem.at[0]).start()
         wait_recv(dwf, gr_sem)
         wait_send(orr.at[:, pl.ds(0, half)], os_sem)
         wait_send(dxr.at[:, pl.ds(0, half)], dxs_sem)
 
     finals = [
+        pltpu.make_async_copy(dwf, dwr_out, in_sem.at[2]),
         pltpu.make_async_copy(y_v, y_out, in_sem.at[0]),
-        pltpu.make_async_copy(dwf, dwr_out, in_sem.at[2]),
+        pltpu.make_async_copy(dx_v, dx_out, in_sem.at[1]),
     ]
-    for c in finals:
-        c.start()
-    finals.append(pltpu.make_async_copy(dx_v, dx_out, in_sem.at[1]))
+    finals[0].start()
     wait_send(ds.at[:, pl.ds(0, ep_size - 1)], ds_sem)
     wait_send(xr.at[pl.ds(0, VIA_TP), 0], xfs_sem)
     wait_send(ps.at[:, pl.ds(0, half)], ps_sem)
@@ -567,7 +571,7 @@
                 dma(()), dma((n_loc,)), dma((n_loc,)), dma((n_loc,)), dma(()), dma(()), dma((n_loc,)),
                 dma(()), dma((n_loc,)), dma(()), dma((n_loc,)),
                 dma(()), dma((n_loc,)), dma(()), dma((n_loc,)),
-                dma(()), dma(()),
+                dma(()), dma((n_tok // 128,)),
                 dma(()), dma(()), dma(()), dma(()), dma(()), dma(()),
             ],
             compiler_params=pltpu.CompilerParams(

time: 139 us -> 140 us (level)
  Pallas kernels: 129 us -> 131 us
    pallas_call x1, Pallas kernels: 113 us -> 114 us  [local_step(): pl.pallas_call(functools.partial(moe_kernel, tp_size, ep_size, cap), name...]
where the time goes in v10:
time: 140 us
  Pallas kernels  131 us (94%)
  starting transfers between devices  5.74 us (4%)
  other arithmetic  2.73 us (2%)
    pallas_call x1, Pallas kernels, local_step(): pl.pallas_call(functools.partial(moe_kernel, tp_size, ep_size, cap), name...  114 us
    pallas_call x1, Pallas kernels, local_step(): pl.pallas_call(weight_kernel, name='weight_grads', grid=(n_loc,), in_spec...  16.7 us
    ppermute x1, starting transfers between devices, local_step(): passed = lax.ppermute(grad_in, ('tp', 'ep'), partners)  5.74 us
  transfers between devices with their start and end apart: 1, of which 0 were waited for; matrix products, arithmetic and copies ran while one was open for 0% of the time, Pallas kernels for 12%

profile of v10, /device:TPU:0, one launch (start us, length us, event | category | flops | bytes accessed | tf_op | source)
XLA Modules:
  0.0 139.9 jit_solution(14384922458937075571)
XLA Ops:
  0.6 114.1 %moe.1 = (bf16[512,1536]{1,0:T(8,128)(2,1)}, bf16[512,1536]{1,0:T(8,128)(2,1)}, f32[8,8,1536]{2,1,0:T(8,128)}, bf16[8,8,16,1536]{3,2,1,0:T(8,128)(2,1)}, bf16[8,...) custom-call(s32[1,512]{1,0:T(1,128)} %bitcast.11, ...), custom_call_target="tpu_custom_call" | custom-call | tf_op jit(solution)/shard_map/moe/pallas_call | solution.py:547
  114.7 5.7 %collective-permute-start = (bf16[512,1536]{1,0:T(8,128)(2,1)}, bf16[512,1536]{1,0:T(8,128)(2,1)}, u32[]{:S(2)}, u32[]{:S(2)}) collective-permute-start(bf16[512,1536]{1,0:T(8,128)(2,1)} %get-tuple-element.27), channel_id=1, source_target_pairs={{0,8},{9,1},{2,10},{11,3},{4,12},{13,5},{6,14},{15,7}} | collective-permute-start | bytes 4718600 | tf_op jit(solution)/shard_map/ppermute | solution.py:588
  120.5 16.7 %weight_grads.1 = (f32[8,1536,256]{2,1,0:T(8,128)}, f32[8,1536,256]{2,1,0:T(8,128)}, f32[8,256,1536]{2,1,0:T(8,128)}, bf16[512,1536]{1,0:T(8,128)(2,1)}, f32[8,8,1536]{2,1,0:T(8,128)}) custom-call(bf16[8,128,1536]{2,1,0:T(8,128)(2,1)} %bitcast.8, bf16[8,128,1536]{2,1,0:T(8,128)(2,1)} %bitcast.9, bf16[8,128,256]{2,1,0:T(8,128)(2,1)} %get-tuple-element.21.h, ...), custom_call_target="tpu_custom_call" | custom-call | flops 2415919104 | bytes 45613056 | tf_op jit(solution)/shard_map/weight_grads/pallas_call | solution.py:599
  137.2 0.0 collective-permute-done
  137.2 2.7 %broadcast_select_fusion = bf16[512,1536]{1,0:T(8,128)(2,1)} fusion(bf16[512,1536]{1,0:T(8,128)(2,1)} %get-tuple-element.27, bf16[512,1536]{1,0:T(8,128)(2,1)} %collective-permute-done, pred[]{:T(512)S(6)} %eq.5), kind=kLoop, calls=%fused_computation | loop fusion | flops 786432 | bytes 4718593 | tf_op jit(solution)/shard_map/jit(_where)/select_n | solution.py:590
Async XLA Ops:
  114.7 22.5 %collective-permute-start = (bf16[512,1536]{1,0:T(8,128)(2,1)}, bf16[512,1536]{1,0:T(8,128)(2,1)}, u32[]{:S(2)}, u32[]{:S(2)}) collective-permute-start(bf16[512,1536]{1,0:T(8,128)(2,1)} %get-tuple-element.27), channel_id=1, source_target_pairs={{0,8},{9,1},{2,10},{11,3},{4,12},{13,5},{6,14},{15,7}} | collective-permute-start | bytes 4718600 | tf_op jit(solution)/shard_map/ppermute | solution.py:588

commit v11 on v10

--- a/solution.py
+++ b/solution.py
@@ -16,7 +16,7 @@
 LAG = 3
 Y_STEP = 5
 FORWARD = 2
-VIA_TP = 4
+VIA_TP = 7
 NN = (((1,), (0,)), ((), ()))
 NT = (((1,), (1,)), ((), ()))
 TN = (((0,), (0,)), ((), ()))
@@ -607,7 +607,7 @@
                 sds((n_tok, width), BF), sds((n_loc, n_exp // n_loc, width), F32),
             ],
             compiler_params=pltpu.CompilerParams(
-                dimension_semantics=("arbitrary",), vmem_limit_bytes=67043328
+                dimension_semantics=("arbitrary",), vmem_limit_bytes=63743328
             ),
             cost_estimate=pl.CostEstimate(
                 flops=6 * n_loc * blk * width * hid, transcendentals=0,

time: 140 us -> 136 us (0.971)
  Pallas kernels: 131 us -> 128 us
  other arithmetic: 2.73 us -> 1.31 us
    pallas_call x1, Pallas kernels: 114 us -> 111 us  [local_step(): pl.pallas_call(functools.partial(moe_kernel, tp_size, ep_size, cap), name...]
    select_n x1, other arithmetic: 2.73 us -> 1.31 us  [local_step(): grad_in = jnp.where(owner, grad_in, passed)]
  transfers between devices with their start and end apart: 1 -> 1, of which waited for: 0 -> 1; matrix products, arithmetic and copies ran while one was open for 0% -> 0% of each run, Pallas kernels for 12% -> 12%
where the time goes in v11:
time: 136 us; the launch traced here: 135 us
  Pallas kernels  128 us (94%)
  starting transfers between devices  4.62 us (3%)
    pallas_call x1, Pallas kernels, local_step(): pl.pallas_call(functools.partial(moe_kernel, tp_size, ep_size, cap), name...  111 us
    pallas_call x1, Pallas kernels, local_step(): pl.pallas_call(weight_kernel, name='weight_grads', grid=(n_loc,), in_spec...  16.9 us
    ppermute x1, starting transfers between devices, local_step(): passed = lax.ppermute(grad_in, ('tp', 'ep'), partners)  4.62 us
  transfers between devices with their start and end apart: 1, of which 1 were waited for; matrix products, arithmetic and copies ran while one was open for 0% of the time, Pallas kernels for 12%

profile of v11, /device:TPU:0, one launch (start us, length us, event | category | flops | bytes accessed | tf_op | source)
XLA Modules:
  0.0 135.4 jit_solution(8957943507531875434)
XLA Ops:
  0.6 111.0 %moe.1 = (bf16[512,1536]{1,0:T(8,128)(2,1)}, bf16[512,1536]{1,0:T(8,128)(2,1)}, f32[8,8,1536]{2,1,0:T(8,128)}, bf16[8,8,16,1536]{3,2,1,0:T(8,128)(2,1)}, bf16[8,...) custom-call(s32[1,512]{1,0:T(1,128)} %bitcast.11, ...), custom_call_target="tpu_custom_call" | custom-call | tf_op jit(solution)/shard_map/moe/pallas_call | solution.py:547
  111.7 4.6 %collective-permute-start = (bf16[512,1536]{1,0:T(8,128)(2,1)}, bf16[512,1536]{1,0:T(8,128)(2,1)S(1)}, u32[]{:S(2)}, u32[]{:S(2)}) collective-permute-start(bf16[512,1536]{1,0:T(8,128)(2,1)} %get-tuple-element.27), channel_id=1, source_target_pairs={{0,8},{9,1},{2,10},{11,3},{4,12},{13,5},{6,14},{15,7}} | collective-permute-start | bytes 4718600 | tf_op jit(solution)/shard_map/ppermute | solution.py:588
  116.3 0.0 copy-start
  116.3 16.9 %weight_grads.1 = (f32[8,1536,256]{2,1,0:T(8,128)}, f32[8,1536,256]{2,1,0:T(8,128)}, f32[8,256,1536]{2,1,0:T(8,128)}, bf16[512,1536]{1,0:T(8,128)(2,1)}, f32[8,8,1536]{2,1,0:T(8,128)}) custom-call(bf16[8,128,1536]{2,1,0:T(8,128)(2,1)} %bitcast.8, bf16[8,128,1536]{2,1,0:T(8,128)(2,1)} %bitcast.9, bf16[8,128,256]{2,1,0:T(8,128)(2,1)} %get-tuple-element.21.h, ...), custom_call_target="tpu_custom_call" | custom-call | flops 2415919104 | bytes 45613056 | tf_op jit(solution)/shard_map/weight_grads/pallas_call | solution.py:599
  133.2 0.9 collective-permute-done
  134.1 0.0 copy-done
  134.1 1.3 broadcast_select_fusion
Async XLA Ops:
  111.7 22.4 %collective-permute-start = (bf16[512,1536]{1,0:T(8,128)(2,1)}, bf16[512,1536]{1,0:T(8,128)(2,1)S(1)}, u32[]{:S(2)}, u32[]{:S(2)}) collective-permute-start(bf16[512,1536]{1,0:T(8,128)(2,1)} %get-tuple-element.27), channel_id=1, source_target_pairs={{0,8},{9,1},{2,10},{11,3},{4,12},{13,5},{6,14},{15,7}} | collective-permute-start | bytes 4718600 | tf_op jit(solution)/shard_map/ppermute | solution.py:588
  116.3 17.8 %copy-start = (bf16[512,1536]{1,0:T(8,128)(2,1)S(1)}, bf16[512,1536]{1,0:T(8,128)(2,1)}, u32[]{:S(2)}) copy-start(bf16[512,1536]{1,0:T(8,128)(2,1)} %get-tuple-element.27) | copy-start | bytes 4718596

commit v12 on v11

--- a/solution.py
+++ b/solution.py
@@ -12,11 +12,11 @@
 I32 = jnp.int32
 MESH = pl.DeviceIdType.MESH
 GELU_COEF = 0.7978845608028654
-AHEAD = 5
+AHEAD = 4
 LAG = 3
-Y_STEP = 5
+Y_STEP = 4
 FORWARD = 2
-VIA_TP = 7
+VIA_TP = 8
 NN = (((1,), (0,)), ((), ()))
 NT = (((1,), (1,)), ((), ()))
 TN = (((0,), (0,)), ((), ()))
@@ -168,9 +168,10 @@
     def _(j):
         build_x(j, True)
 
-    @pl.loop(VIA_TP, n_loc)
-    def _(j):
-        build_x(j, False)
+    if VIA_TP < n_loc:
+        @pl.loop(VIA_TP, n_loc)
+        def _(j):
+            build_x(j, False)
 
     def column(row):
         return jnp.transpose(jnp.broadcast_to(row, (128, n_tok)))
@@ -269,9 +270,10 @@
             wait_recv(xr.at[j, pl.ds(0, n_near)], xr_sem.at[j])
             wait_recv(xr.at[j, 0], xf_sem.at[j])
 
-        @pl.when(j >= VIA_TP)
-        def _():
-            wait_recv(xr.at[j, pl.ds(0, ep_size - 1)], xr_sem.at[j])
+        if VIA_TP < n_loc:
+            @pl.when(j >= VIA_TP)
+            def _():
+                wait_recv(xr.at[j, pl.ds(0, ep_size - 1)], xr_sem.at[j])
 
         rows = xr[j].reshape(blk, width)
         pa = dot(rows, wa_v[j])
@@ -360,7 +362,8 @@
             ).start()
 
     wait_send(xs.at[pl.ds(0, VIA_TP), pl.ds(0, n_near + 1)], xs_sem)
-    wait_send(xs.at[pl.ds(VIA_TP, n_loc - VIA_TP), pl.ds(0, ep_size - 1)], xs_sem)
+    if VIA_TP < n_loc:
+        wait_send(xs.at[pl.ds(VIA_TP, n_loc - VIA_TP), pl.ds(0, ep_size - 1)], xs_sem)
     @pl.loop(0, n_loc)
     def _(j):
         @pl.when(j + AHEAD < n_loc)

time: 136 us -> 136 us (level)
  no operation moved by 1% of the time
where the time goes in v12:
time: 136 us; the launch traced here: 135 us
  Pallas kernels  128 us (94%)
  starting transfers between devices  4.62 us (3%)
    pallas_call x1, Pallas kernels, local_step(): pl.pallas_call(functools.partial(moe_kernel, tp_size, ep_size, cap), name...  111 us
    pallas_call x1, Pallas kernels, local_step(): pl.pallas_call(weight_kernel, name='weight_grads', grid=(n_loc,), in_spec...  16.9 us
    ppermute x1, starting transfers between devices, local_step(): passed = lax.ppermute(grad_in, ('tp', 'ep'), partners)  4.62 us
  transfers between devices with their start and end apart: 1, of which 1 were waited for; matrix products, arithmetic and copies ran while one was open for 0% of the time, Pallas kernels for 12%

profile of v12, /device:TPU:0, one launch (start us, length us, event | category | flops | bytes accessed | tf_op | source)
XLA Modules:
  0.0 135.5 jit_solution(8653347738163460924)
XLA Ops:
  0.6 111.1 %moe.1 = (bf16[512,1536]{1,0:T(8,128)(2,1)}, bf16[512,1536]{1,0:T(8,128)(2,1)}, f32[8,8,1536]{2,1,0:T(8,128)}, bf16[8,8,16,1536]{3,2,1,0:T(8,128)(2,1)}, bf16[8,...) custom-call(s32[1,512]{1,0:T(1,128)} %bitcast.11, ...), custom_call_target="tpu_custom_call" | custom-call | tf_op jit(solution)/shard_map/moe/pallas_call | solution.py:550
  111.7 4.6 %collective-permute-start = (bf16[512,1536]{1,0:T(8,128)(2,1)}, bf16[512,1536]{1,0:T(8,128)(2,1)S(1)}, u32[]{:S(2)}, u32[]{:S(2)}) collective-permute-start(bf16[512,1536]{1,0:T(8,128)(2,1)} %get-tuple-element.27), channel_id=1, source_target_pairs={{0,8},{9,1},{2,10},{11,3},{4,12},{13,5},{6,14},{15,7}} | collective-permute-start | bytes 4718600 | tf_op jit(solution)/shard_map/ppermute | solution.py:591
  116.4 0.0 copy-start
  116.4 16.9 %weight_grads.1 = (f32[8,1536,256]{2,1,0:T(8,128)}, f32[8,1536,256]{2,1,0:T(8,128)}, f32[8,256,1536]{2,1,0:T(8,128)}, bf16[512,1536]{1,0:T(8,128)(2,1)}, f32[8,8,1536]{2,1,0:T(8,128)}) custom-call(bf16[8,128,1536]{2,1,0:T(8,128)(2,1)} %bitcast.8, bf16[8,128,1536]{2,1,0:T(8,128)(2,1)} %bitcast.9, bf16[8,128,256]{2,1,0:T(8,128)(2,1)} %get-tuple-element.21.h, ...), custom_call_target="tpu_custom_call" | custom-call | flops 2415919104 | bytes 45613056 | tf_op jit(solution)/shard_map/weight_grads/pallas_call | solution.py:602
  133.3 0.9 collective-permute-done
  134.2 0.0 copy-done
  134.2 1.3 broadcast_select_fusion
Async XLA Ops:
  111.7 22.4 %collective-permute-start = (bf16[512,1536]{1,0:T(8,128)(2,1)}, bf16[512,1536]{1,0:T(8,128)(2,1)S(1)}, u32[]{:S(2)}, u32[]{:S(2)}) collective-permute-start(bf16[512,1536]{1,0:T(8,128)(2,1)} %get-tuple-element.27), channel_id=1, source_target_pairs={{0,8},{9,1},{2,10},{11,3},{4,12},{13,5},{6,14},{15,7}} | collective-permute-start | bytes 4718600 | tf_op jit(solution)/shard_map/ppermute | solution.py:591
  116.4 17.8 %copy-start = (bf16[512,1536]{1,0:T(8,128)(2,1)S(1)}, bf16[512,1536]{1,0:T(8,128)(2,1)}, u32[]{:S(2)}) copy-start(bf16[512,1536]{1,0:T(8,128)(2,1)} %get-tuple-element.27) | copy-start | bytes 4718596

commit v13 on v12

--- a/solution.py
+++ b/solution.py
@@ -17,6 +17,7 @@
 Y_STEP = 4
 FORWARD = 2
 VIA_TP = 8
+EARLY = 2
 NN = (((1,), (0,)), ((), ()))
 NT = (((1,), (1,)), ((), ()))
 TN = (((0,), (0,)), ((), ()))
@@ -141,12 +142,14 @@
             src_ref=view, dst_ref=view, send_sem=sem, recv_sem=sem, device_id=(k, r), device_id_type=MESH
         ).wait_send()
 
-    def build_x(j, via_tp):
+    def gather_x(j):
         m1, m2 = masks(j)
         pick = jnp.where(m1 | m2, 1.0, 0.0).astype(BF)
         for c in range(0, width, 512):
             rows = dot(pick, x_v[:, c:c + 512]).astype(BF)
             xs[j, :, :, c:c + 512] = rows.reshape(ep_size, cap, 512)
+
+    def send_x(j, via_tp):
         if via_tp:
             send_row(xs, xr, xs_sem, xd_sem, j, diag)
         for q in near if via_tp else far + near:
@@ -162,16 +165,26 @@
         for c in weight_copies(j):
             c.start()
 
+    @pl.loop(0, EARLY)
+    def _(j):
+        gather_x(j)
+
     pl.semaphore_wait(barrier, n_dev - 1)
 
-    @pl.loop(0, VIA_TP)
+    @pl.loop(0, EARLY)
     def _(j):
-        build_x(j, True)
+        send_x(j, True)
+
+    @pl.loop(EARLY, VIA_TP)
+    def _(j):
+        gather_x(j)
+        send_x(j, True)
 
     if VIA_TP < n_loc:
         @pl.loop(VIA_TP, n_loc)
         def _(j):
-            build_x(j, False)
+            gather_x(j)
+            send_x(j, False)
 
     def column(row):
         return jnp.transpose(jnp.broadcast_to(row, (128, n_tok)))
@@ -450,6 +463,8 @@
     @pl.when(owner)
     def _():
         ship(y_v, n_tb - 2, ys_sem, yr_sem)
+        ship(y_v, n_tb - 1, ys_sem, yr_sem)
+        pltpu.make_async_copy(y_v, y_out, in_sem.at[0]).start()
 
     for i in range(LAG - 1):
         merge_and_return(xs, pdr, pdr_sem, dxr, dxs_sem, dxr_sem, n_loc - LAG + i)
@@ -457,8 +472,6 @@
     @pl.when(owner)
     def _():
         router_sum()
-        ship(y_v, n_tb - 1, ys_sem, yr_sem)
-        pltpu.make_async_copy(y_v, y_out, in_sem.at[0]).start()
 
     merge_and_return(xs, pdr, pdr_sem, dxr, dxs_sem, dxr_sem, n_loc - 1)
 

time: 136 us -> 138 us (1.015)
  Pallas kernels: 128 us -> 131 us
  starting transfers between devices: 4.62 us -> 2.14 us
    pallas_call x1, Pallas kernels: 111 us -> 114 us  [local_step(): pl.pallas_call(functools.partial(moe_kernel, tp_size, ep_size, cap), name...]
    ppermute x1, starting transfers between devices: 4.62 us -> 2.14 us  [local_step(): passed = lax.ppermute(grad_in, ('tp', 'ep'), partners)]
where the time goes in v13:
time: 138 us; the launch traced here: 136 us
  Pallas kernels  131 us (95%)
  starting transfers between devices  2.14 us (2%)
    pallas_call x1, Pallas kernels, local_step(): pl.pallas_call(functools.partial(moe_kernel, tp_size, ep_size, cap), name...  114 us
    pallas_call x1, Pallas kernels, local_step(): pl.pallas_call(weight_kernel, name='weight_grads', grid=(n_loc,), in_spec...  16.9 us
  transfers between devices with their start and end apart: 1, of which 1 were waited for; matrix products, arithmetic and copies ran while one was open for 0% of the time, Pallas kernels for 12%

profile of v13, /device:TPU:0, one launch (start us, length us, event | category | flops | bytes accessed | tf_op | source)
XLA Modules:
  0.0 136.3 jit_solution(8936235573718327155)
XLA Ops:
  0.6 114.4 %moe.1 = (bf16[512,1536]{1,0:T(8,128)(2,1)}, bf16[512,1536]{1,0:T(8,128)(2,1)}, f32[8,8,1536]{2,1,0:T(8,128)}, bf16[8,8,16,1536]{3,2,1,0:T(8,128)(2,1)}, bf16[8,...) custom-call(s32[1,512]{1,0:T(1,128)} %bitcast.11, ...), custom_call_target="tpu_custom_call" | custom-call | tf_op jit(solution)/shard_map/moe/pallas_call | solution.py:563
  115.1 2.1 %collective-permute-start = (bf16[512,1536]{1,0:T(8,128)(2,1)}, bf16[512,1536]{1,0:T(8,128)(2,1)S(1)}, u32[]{:S(2)}, u32[]{:S(2)}) collective-permute-start(bf16[512,1536]{1,0:T(8,128)(2,1)} %get-tuple-element.27), channel_id=1, source_target_pairs={{0,8},{9,1},{2,10},{11,3},{4,12},{13,5},{6,14},{15,7}} | collective-permute-start | bytes 4718600 | tf_op jit(solution)/shard_map/ppermute | solution.py:604
  117.3 0.0 copy-start
  117.3 16.9 %weight_grads.1 = (f32[8,1536,256]{2,1,0:T(8,128)}, f32[8,1536,256]{2,1,0:T(8,128)}, f32[8,256,1536]{2,1,0:T(8,128)}, bf16[512,1536]{1,0:T(8,128)(2,1)}, f32[8,8,1536]{2,1,0:T(8,128)}) custom-call(bf16[8,128,1536]{2,1,0:T(8,128)(2,1)} %bitcast.8, bf16[8,128,1536]{2,1,0:T(8,128)(2,1)} %bitcast.9, bf16[8,128,256]{2,1,0:T(8,128)(2,1)} %get-tuple-element.21.h, ...), custom_call_target="tpu_custom_call" | custom-call | flops 2415919104 | bytes 45613056 | tf_op jit(solution)/shard_map/weight_grads/pallas_call | solution.py:615
  134.1 0.9 collective-permute-done
  135.0 0.0 copy-done
  135.0 1.3 broadcast_select_fusion
Async XLA Ops:
  115.1 19.9 %collective-permute-start = (bf16[512,1536]{1,0:T(8,128)(2,1)}, bf16[512,1536]{1,0:T(8,128)(2,1)S(1)}, u32[]{:S(2)}, u32[]{:S(2)}) collective-permute-start(bf16[512,1536]{1,0:T(8,128)(2,1)} %get-tuple-element.27), channel_id=1, source_target_pairs={{0,8},{9,1},{2,10},{11,3},{4,12},{13,5},{6,14},{15,7}} | collective-permute-start | bytes 4718600 | tf_op jit(solution)/shard_map/ppermute | solution.py:604
  117.3 17.8 %copy-start = (bf16[512,1536]{1,0:T(8,128)(2,1)S(1)}, bf16[512,1536]{1,0:T(8,128)(2,1)}, u32[]{:S(2)}) copy-start(bf16[512,1536]{1,0:T(8,128)(2,1)} %get-tuple-element.27) | copy-start | bytes 4718596

commit v14 on v13

--- a/solution.py
+++ b/solution.py
@@ -16,7 +16,8 @@
 LAG = 3
 Y_STEP = 4
 FORWARD = 2
-VIA_TP = 8
+VIA_TP = 7
+BACK_LAG = 2
 EARLY = 2
 NN = (((1,), (0,)), ((), ()))
 NT = (((1,), (1,)), ((), ()))
@@ -400,9 +401,9 @@
             for i in range(LAG):
                 merge_and_return(ps, pr, pr_sem, orr, os_sem, or_sem, n_loc - LAG + i)
 
-        @pl.when(j >= LAG)
-        def _():
-            merge_and_return(xs, pdr, pdr_sem, dxr, dxs_sem, dxr_sem, j - LAG)
+        @pl.when(j >= BACK_LAG)
+        def _():
+            merge_and_return(xs, pdr, pdr_sem, dxr, dxs_sem, dxr_sem, j - BACK_LAG)
 
         @pl.when(owner & (j == Y_STEP))
         def _():
@@ -463,15 +464,15 @@
     @pl.when(owner)
     def _():
         ship(y_v, n_tb - 2, ys_sem, yr_sem)
-        ship(y_v, n_tb - 1, ys_sem, yr_sem)
-        pltpu.make_async_copy(y_v, y_out, in_sem.at[0]).start()
-
-    for i in range(LAG - 1):
-        merge_and_return(xs, pdr, pdr_sem, dxr, dxs_sem, dxr_sem, n_loc - LAG + i)
+
+    for i in range(BACK_LAG - 1):
+        merge_and_return(xs, pdr, pdr_sem, dxr, dxs_sem, dxr_sem, n_loc - BACK_LAG + i)
 
     @pl.when(owner)
     def _():
         router_sum()
+        ship(y_v, n_tb - 1, ys_sem, yr_sem)
+        pltpu.make_async_copy(y_v, y_out, in_sem.at[0]).start()
 
     merge_and_return(xs, pdr, pdr_sem, dxr, dxs_sem, dxr_sem, n_loc - 1)
 

time: 138 us -> 136 us (0.986)
  Pallas kernels: 131 us -> 128 us
  starting transfers between devices: 2.14 us -> 4.62 us
    pallas_call x1, Pallas kernels: 114 us -> 111 us  [local_step(): pl.pallas_call(functools.partial(moe_kernel, tp_size, ep_size, cap), name...]
    ppermute x1, starting transfers between devices: 2.14 us -> 4.62 us  [local_step(): passed = lax.ppermute(grad_in, ('tp', 'ep'), partners)]
where the time goes in v14:
time: 136 us; the launch traced here: 135 us
  Pallas kernels  128 us (94%)
  starting transfers between devices  4.62 us (3%)
    pallas_call x1, Pallas kernels, local_step(): pl.pallas_call(functools.partial(moe_kernel, tp_size, ep_size, cap), name...  111 us
    pallas_call x1, Pallas kernels, local_step(): pl.pallas_call(weight_kernel, name='weight_grads', grid=(n_loc,), in_spec...  16.9 us
    ppermute x1, starting transfers between devices, local_step(): passed = lax.ppermute(grad_in, ('tp', 'ep'), partners)  4.62 us
  transfers between devices with their start and end apart: 1, of which 1 were waited for; matrix products, arithmetic and copies ran while one was open for 0% of the time, Pallas kernels for 12%

profile of v14, /device:TPU:0, one launch (start us, length us, event | category | flops | bytes accessed | tf_op | source)
XLA Modules:
  0.0 135.4 jit_solution(17893858655266558548)
XLA Ops:
  0.6 111.0 %moe.1 = (bf16[512,1536]{1,0:T(8,128)(2,1)}, bf16[512,1536]{1,0:T(8,128)(2,1)}, f32[8,8,1536]{2,1,0:T(8,128)}, bf16[8,8,16,1536]{3,2,1,0:T(8,128)(2,1)}, bf16[8,...) custom-call(s32[1,512]{1,0:T(1,128)} %bitcast.11, ...), custom_call_target="tpu_custom_call" | custom-call | tf_op jit(solution)/shard_map/moe/pallas_call | solution.py:564
  111.7 4.6 %collective-permute-start = (bf16[512,1536]{1,0:T(8,128)(2,1)}, bf16[512,1536]{1,0:T(8,128)(2,1)S(1)}, u32[]{:S(2)}, u32[]{:S(2)}) collective-permute-start(bf16[512,1536]{1,0:T(8,128)(2,1)} %get-tuple-element.27), channel_id=1, source_target_pairs={{0,8},{9,1},{2,10},{11,3},{4,12},{13,5},{6,14},{15,7}} | collective-permute-start | bytes 4718600 | tf_op jit(solution)/shard_map/ppermute | solution.py:605
  116.3 0.0 copy-start
  116.3 16.9 %weight_grads.1 = (f32[8,1536,256]{2,1,0:T(8,128)}, f32[8,1536,256]{2,1,0:T(8,128)}, f32[8,256,1536]{2,1,0:T(8,128)}, bf16[512,1536]{1,0:T(8,128)(2,1)}, f32[8,8,1536]{2,1,0:T(8,128)}) custom-call(bf16[8,128,1536]{2,1,0:T(8,128)(2,1)} %bitcast.8, bf16[8,128,1536]{2,1,0:T(8,128)(2,1)} %bitcast.9, bf16[8,128,256]{2,1,0:T(8,128)(2,1)} %get-tuple-element.21.h, ...), custom_call_target="tpu_custom_call" | custom-call | flops 2415919104 | bytes 45613056 | tf_op jit(solution)/shard_map/weight_grads/pallas_call | solution.py:616
  133.2 0.9 collective-permute-done
  134.1 0.0 copy-done
  134.1 1.3 broadcast_select_fusion
Async XLA Ops:
  111.7 22.4 %collective-permute-start = (bf16[512,1536]{1,0:T(8,128)(2,1)}, bf16[512,1536]{1,0:T(8,128)(2,1)S(1)}, u32[]{:S(2)}, u32[]{:S(2)}) collective-permute-start(bf16[512,1536]{1,0:T(8,128)(2,1)} %get-tuple-element.27), channel_id=1, source_target_pairs={{0,8},{9,1},{2,10},{11,3},{4,12},{13,5},{6,14},{15,7}} | collective-permute-start | bytes 4718600 | tf_op jit(solution)/shard_map/ppermute | solution.py:605
  116.3 17.8 %copy-start = (bf16[512,1536]{1,0:T(8,128)(2,1)S(1)}, bf16[512,1536]{1,0:T(8,128)(2,1)}, u32[]{:S(2)}) copy-start(bf16[512,1536]{1,0:T(8,128)(2,1)} %get-tuple-element.27) | copy-start | bytes 4718596

commit v15 on v14

--- a/solution.py
+++ b/solution.py
@@ -421,6 +421,10 @@
 
             ship(y_v, j - Y_STEP, ys_sem, yr_sem)
 
+        @pl.when(owner & (j == Y_STEP + n_tb // 2))
+        def _():
+            ship(y_v, n_tb // 2, ys_sem, yr_sem)
+
         @pl.when(owner & (j == Y_STEP + n_tb // 2 - 1))
         def _():
             router_parts()
@@ -460,10 +464,6 @@
 
     for c in outs[3:]:
         c.start()
-
-    @pl.when(owner)
-    def _():
-        ship(y_v, n_tb - 2, ys_sem, yr_sem)
 
     for i in range(BACK_LAG - 1):
         merge_and_return(xs, pdr, pdr_sem, dxr, dxs_sem, dxr_sem, n_loc - BACK_LAG + i)

time: 136 us -> 136 us (level)
  Pallas kernels: 128 us -> 130 us
  starting transfers between devices: 4.62 us -> 2.93 us
    ppermute x1, starting transfers between devices: 4.62 us -> 2.93 us  [local_step(): passed = lax.ppermute(grad_in, ('tp', 'ep'), partners)]
    pallas_call x1, Pallas kernels: 111 us -> 113 us  [local_step(): pl.pallas_call(functools.partial(moe_kernel, tp_size, ep_size, cap), name...]
where the time goes in v15:
time: 136 us; the launch traced here: 135 us
  Pallas kernels  130 us (96%)
  starting transfers between devices  2.93 us (2%)
    pallas_call x1, Pallas kernels, local_step(): pl.pallas_call(functools.partial(moe_kernel, tp_size, ep_size, cap), name...  113 us
    pallas_call x1, Pallas kernels, local_step(): pl.pallas_call(weight_kernel, name='weight_grads', grid=(n_loc,), in_spec...  16.9 us
    ppermute x1, starting transfers between devices, local_step(): passed = lax.ppermute(grad_in, ('tp', 'ep'), partners)  2.93 us
  transfers between devices with their start and end apart: 1, of which 1 were waited for; matrix products, arithmetic and copies ran while one was open for 0% of the time, Pallas kernels for 12%

profile of v15, /device:TPU:0, one launch (start us, length us, event | category | flops | bytes accessed | tf_op | source)
XLA Modules:
  0.0 135.3 jit_solution(5184321553985678754)
XLA Ops:
  0.6 112.6 %moe.1 = (bf16[512,1536]{1,0:T(8,128)(2,1)}, bf16[512,1536]{1,0:T(8,128)(2,1)}, f32[8,8,1536]{2,1,0:T(8,128)}, bf16[8,8,16,1536]{3,2,1,0:T(8,128)(2,1)}, bf16[8,...) custom-call(s32[1,512]{1,0:T(1,128)} %bitcast.11, ...), custom_call_target="tpu_custom_call" | custom-call | tf_op jit(solution)/shard_map/moe/pallas_call | solution.py:564
  113.3 2.9 %collective-permute-start = (bf16[512,1536]{1,0:T(8,128)(2,1)}, bf16[512,1536]{1,0:T(8,128)(2,1)S(1)}, u32[]{:S(2)}, u32[]{:S(2)}) collective-permute-start(bf16[512,1536]{1,0:T(8,128)(2,1)} %get-tuple-element.27), channel_id=1, source_target_pairs={{0,8},{9,1},{2,10},{11,3},{4,12},{13,5},{6,14},{15,7}} | collective-permute-start | bytes 4718600 | tf_op jit(solution)/shard_map/ppermute | solution.py:605
  116.2 0.0 copy-start
  116.2 16.9 %weight_grads.1 = (f32[8,1536,256]{2,1,0:T(8,128)}, f32[8,1536,256]{2,1,0:T(8,128)}, f32[8,256,1536]{2,1,0:T(8,128)}, bf16[512,1536]{1,0:T(8,128)(2,1)}, f32[8,8,1536]{2,1,0:T(8,128)}) custom-call(bf16[8,128,1536]{2,1,0:T(8,128)(2,1)} %bitcast.8, bf16[8,128,1536]{2,1,0:T(8,128)(2,1)} %bitcast.9, bf16[8,128,256]{2,1,0:T(8,128)(2,1)} %get-tuple-element.21.h, ...), custom_call_target="tpu_custom_call" | custom-call | flops 2415919104 | bytes 45613056 | tf_op jit(solution)/shard_map/weight_grads/pallas_call | solution.py:616
  133.1 0.9 collective-permute-done
  134.0 0.0 copy-done
  134.0 1.3 broadcast_select_fusion
Async XLA Ops:
  113.3 20.7 %collective-permute-start = (bf16[512,1536]{1,0:T(8,128)(2,1)}, bf16[512,1536]{1,0:T(8,128)(2,1)S(1)}, u32[]{:S(2)}, u32[]{:S(2)}) collective-permute-start(bf16[512,1536]{1,0:T(8,128)(2,1)} %get-tuple-element.27), channel_id=1, source_target_pairs={{0,8},{9,1},{2,10},{11,3},{4,12},{13,5},{6,14},{15,7}} | collective-permute-start | bytes 4718600 | tf_op jit(solution)/shard_map/ppermute | solution.py:605
  116.2 17.8 %copy-start = (bf16[512,1536]{1,0:T(8,128)(2,1)S(1)}, bf16[512,1536]{1,0:T(8,128)(2,1)}, u32[]{:S(2)}) copy-start(bf16[512,1536]{1,0:T(8,128)(2,1)} %get-tuple-element.27) | copy-start | bytes 4718596

commit v16 on v15

--- a/solution.py
+++ b/solution.py
@@ -16,7 +16,7 @@
 LAG = 3
 Y_STEP = 4
 FORWARD = 2
-VIA_TP = 7
+VIA_TP = 6
 BACK_LAG = 2
 EARLY = 2
 NN = (((1,), (0,)), ((), ()))

time: 136 us -> 137 us (level)
  no operation moved by 1% of the time
where the time goes in v16:
time: 137 us; the launch traced here: 136 us
  Pallas kernels  131 us (96%)
  starting transfers between devices  2.96 us (2%)
    pallas_call x1, Pallas kernels, local_step(): pl.pallas_call(functools.partial(moe_kernel, tp_size, ep_size, cap), name...  114 us
    pallas_call x1, Pallas kernels, local_step(): pl.pallas_call(weight_kernel, name='weight_grads', grid=(n_loc,), in_spec...  16.9 us
    ppermute x1, starting transfers between devices, local_step(): passed = lax.ppermute(grad_in, ('tp', 'ep'), partners)  2.96 us
  transfers between devices with their start and end apart: 1, of which 1 were waited for; matrix products, arithmetic and copies ran while one was open for 0% of the time, Pallas kernels for 12%

profile of v16, /device:TPU:0, one launch (start us, length us, event | category | flops | bytes accessed | tf_op | source)
XLA Modules:
  0.0 136.4 jit_solution(12000834883220316874)
XLA Ops:
  0.6 113.7 %moe.1 = (bf16[512,1536]{1,0:T(8,128)(2,1)}, bf16[512,1536]{1,0:T(8,128)(2,1)}, f32[8,8,1536]{2,1,0:T(8,128)}, bf16[8,8,16,1536]{3,2,1,0:T(8,128)(2,1)}, bf16[8,...) custom-call(s32[1,512]{1,0:T(1,128)} %bitcast.11, ...), custom_call_target="tpu_custom_call" | custom-call | tf_op jit(solution)/shard_map/moe/pallas_call | solution.py:564
  114.3 3.0 %collective-permute-start = (bf16[512,1536]{1,0:T(8,128)(2,1)}, bf16[512,1536]{1,0:T(8,128)(2,1)S(1)}, u32[]{:S(2)}, u32[]{:S(2)}) collective-permute-start(bf16[512,1536]{1,0:T(8,128)(2,1)} %get-tuple-element.27), channel_id=1, source_target_pairs={{0,8},{9,1},{2,10},{11,3},{4,12},{13,5},{6,14},{15,7}} | collective-permute-start | bytes 4718600 | tf_op jit(solution)/shard_map/ppermute | solution.py:605
  117.3 0.0 copy-start
  117.3 16.9 %weight_grads.1 = (f32[8,1536,256]{2,1,0:T(8,128)}, f32[8,1536,256]{2,1,0:T(8,128)}, f32[8,256,1536]{2,1,0:T(8,128)}, bf16[512,1536]{1,0:T(8,128)(2,1)}, f32[8,8,1536]{2,1,0:T(8,128)}) custom-call(bf16[8,128,1536]{2,1,0:T(8,128)(2,1)} %bitcast.8, bf16[8,128,1536]{2,1,0:T(8,128)(2,1)} %bitcast.9, bf16[8,128,256]{2,1,0:T(8,128)(2,1)} %get-tuple-element.21.h, ...), custom_call_target="tpu_custom_call" | custom-call | flops 2415919104 | bytes 45613056 | tf_op jit(solution)/shard_map/weight_grads/pallas_call | solution.py:616
  134.2 0.9 collective-permute-done
  135.1 0.0 copy-done
  135.1 1.3 broadcast_select_fusion
Async XLA Ops:
  114.3 20.8 %collective-permute-start = (bf16[512,1536]{1,0:T(8,128)(2,1)}, bf16[512,1536]{1,0:T(8,128)(2,1)S(1)}, u32[]{:S(2)}, u32[]{:S(2)}) collective-permute-start(bf16[512,1536]{1,0:T(8,128)(2,1)} %get-tuple-element.27), channel_id=1, source_target_pairs={{0,8},{9,1},{2,10},{11,3},{4,12},{13,5},{6,14},{15,7}} | collective-permute-start | bytes 4718600 | tf_op jit(solution)/shard_map/ppermute | solution.py:605
  117.3 17.8 %copy-start = (bf16[512,1536]{1,0:T(8,128)(2,1)S(1)}, bf16[512,1536]{1,0:T(8,128)(2,1)}, u32[]{:S(2)}) copy-start(bf16[512,1536]{1,0:T(8,128)(2,1)} %get-tuple-element.27) | copy-start | bytes 4718596

commit v17 on v16

--- a/solution.py
+++ b/solution.py
@@ -16,7 +16,7 @@
 LAG = 3
 Y_STEP = 4
 FORWARD = 2
-VIA_TP = 6
+VIA_TP = 8
 BACK_LAG = 2
 EARLY = 2
 NN = (((1,), (0,)), ((), ()))

time: 137 us -> 136 us (level)
  Pallas kernels: 131 us -> 129 us
where the time goes in v17:
time: 136 us; the launch traced here: 135 us
  Pallas kernels  129 us (95%)
  starting transfers between devices  2.96 us (2%)
    pallas_call x1, Pallas kernels, local_step(): pl.pallas_call(functools.partial(moe_kernel, tp_size, ep_size, cap), name...  113 us
    pallas_call x1, Pallas kernels, local_step(): pl.pallas_call(weight_kernel, name='weight_grads', grid=(n_loc,), in_spec...  16.9 us
    ppermute x1, starting transfers between devices, local_step(): passed = lax.ppermute(grad_in, ('tp', 'ep'), partners)  2.96 us
  transfers between devices with their start and end apart: 1, of which 1 were waited for; matrix products, arithmetic and copies ran while one was open for 0% of the time, Pallas kernels for 12%

profile of v17, /device:TPU:0, one launch (start us, length us, event | category | flops | bytes accessed | tf_op | source)
XLA Modules:
  0.0 135.3 jit_solution(4527354559565648496)
XLA Ops:
  0.6 112.5 %moe.1 = (bf16[512,1536]{1,0:T(8,128)(2,1)}, bf16[512,1536]{1,0:T(8,128)(2,1)}, f32[8,8,1536]{2,1,0:T(8,128)}, bf16[8,8,16,1536]{3,2,1,0:T(8,128)(2,1)}, bf16[8,...) custom-call(s32[1,512]{1,0:T(1,128)} %bitcast.11, ...), custom_call_target="tpu_custom_call" | custom-call | tf_op jit(solution)/shard_map/moe/pallas_call | solution.py:564
  113.2 3.0 %collective-permute-start = (bf16[512,1536]{1,0:T(8,128)(2,1)}, bf16[512,1536]{1,0:T(8,128)(2,1)S(1)}, u32[]{:S(2)}, u32[]{:S(2)}) collective-permute-start(bf16[512,1536]{1,0:T(8,128)(2,1)} %get-tuple-element.27), channel_id=1, source_target_pairs={{0,8},{9,1},{2,10},{11,3},{4,12},{13,5},{6,14},{15,7}} | collective-permute-start | bytes 4718600 | tf_op jit(solution)/shard_map/ppermute | solution.py:605
  116.2 0.0 copy-start
  116.2 16.9 %weight_grads.1 = (f32[8,1536,256]{2,1,0:T(8,128)}, f32[8,1536,256]{2,1,0:T(8,128)}, f32[8,256,1536]{2,1,0:T(8,128)}, bf16[512,1536]{1,0:T(8,128)(2,1)}, f32[8,8,1536]{2,1,0:T(8,128)}) custom-call(bf16[8,128,1536]{2,1,0:T(8,128)(2,1)} %bitcast.8, bf16[8,128,1536]{2,1,0:T(8,128)(2,1)} %bitcast.9, bf16[8,128,256]{2,1,0:T(8,128)(2,1)} %get-tuple-element.21.h, ...), custom_call_target="tpu_custom_call" | custom-call | flops 2415919104 | bytes 45613056 | tf_op jit(solution)/shard_map/weight_grads/pallas_call | solution.py:616
  133.0 0.9 collective-permute-done
  133.9 0.0 copy-done
  133.9 1.3 broadcast_select_fusion
Async XLA Ops:
  113.2 20.8 %collective-permute-start = (bf16[512,1536]{1,0:T(8,128)(2,1)}, bf16[512,1536]{1,0:T(8,128)(2,1)S(1)}, u32[]{:S(2)}, u32[]{:S(2)}) collective-permute-start(bf16[512,1536]{1,0:T(8,128)(2,1)} %get-tuple-element.27), channel_id=1, source_target_pairs={{0,8},{9,1},{2,10},{11,3},{4,12},{13,5},{6,14},{15,7}} | collective-permute-start | bytes 4718600 | tf_op jit(solution)/shard_map/ppermute | solution.py:605
  116.2 17.8 %copy-start = (bf16[512,1536]{1,0:T(8,128)(2,1)S(1)}, bf16[512,1536]{1,0:T(8,128)(2,1)}, u32[]{:S(2)}) copy-start(bf16[512,1536]{1,0:T(8,128)(2,1)} %get-tuple-element.27) | copy-start | bytes 4718596

commit v18 on v17

--- a/solution.py
+++ b/solution.py
@@ -12,9 +12,9 @@
 I32 = jnp.int32
 MESH = pl.DeviceIdType.MESH
 GELU_COEF = 0.7978845608028654
-AHEAD = 4
+AHEAD = 3
 LAG = 3
-Y_STEP = 4
+Y_STEP = 3
 FORWARD = 2
 VIA_TP = 8
 BACK_LAG = 2

time: 136 us -> 136 us (level)
  no operation moved by 1% of the time
where the time goes in v18:
time: 136 us; the launch traced here: 135 us
  Pallas kernels  129 us (95%)
  starting transfers between devices  3.11 us (2%)
    pallas_call x1, Pallas kernels, local_step(): pl.pallas_call(functools.partial(moe_kernel, tp_size, ep_size, cap), name...  113 us
    pallas_call x1, Pallas kernels, local_step(): pl.pallas_call(weight_kernel, name='weight_grads', grid=(n_loc,), in_spec...  16.9 us
    ppermute x1, starting transfers between devices, local_step(): passed = lax.ppermute(grad_in, ('tp', 'ep'), partners)  3.11 us
  transfers between devices with their start and end apart: 1, of which 1 were waited for; matrix products, arithmetic and copies ran while one was open for 0% of the time, Pallas kernels for 12%

profile of v18, /device:TPU:0, one launch (start us, length us, event | category | flops | bytes accessed | tf_op | source)
XLA Modules:
  0.0 135.4 jit_solution(6201138592187470532)
XLA Ops:
  0.6 112.5 %moe.1 = (bf16[512,1536]{1,0:T(8,128)(2,1)}, bf16[512,1536]{1,0:T(8,128)(2,1)}, f32[8,8,1536]{2,1,0:T(8,128)}, bf16[8,8,16,1536]{3,2,1,0:T(8,128)(2,1)}, bf16[8,...) custom-call(s32[1,512]{1,0:T(1,128)} %bitcast.11, ...), custom_call_target="tpu_custom_call" | custom-call | tf_op jit(solution)/shard_map/moe/pallas_call | solution.py:564
  113.2 3.1 %collective-permute-start = (bf16[512,1536]{1,0:T(8,128)(2,1)}, bf16[512,1536]{1,0:T(8,128)(2,1)S(1)}, u32[]{:S(2)}, u32[]{:S(2)}) collective-permute-start(bf16[512,1536]{1,0:T(8,128)(2,1)} %get-tuple-element.27), channel_id=1, source_target_pairs={{0,8},{9,1},{2,10},{11,3},{4,12},{13,5},{6,14},{15,7}} | collective-permute-start | bytes 4718600 | tf_op jit(solution)/shard_map/ppermute | solution.py:605
  116.3 0.0 copy-start
  116.3 16.9 %weight_grads.1 = (f32[8,1536,256]{2,1,0:T(8,128)}, f32[8,1536,256]{2,1,0:T(8,128)}, f32[8,256,1536]{2,1,0:T(8,128)}, bf16[512,1536]{1,0:T(8,128)(2,1)}, f32[8,8,1536]{2,1,0:T(8,128)}) custom-call(bf16[8,128,1536]{2,1,0:T(8,128)(2,1)} %bitcast.8, bf16[8,128,1536]{2,1,0:T(8,128)(2,1)} %bitcast.9, bf16[8,128,256]{2,1,0:T(8,128)(2,1)} %get-tuple-element.21.h, ...), custom_call_target="tpu_custom_call" | custom-call | flops 2415919104 | bytes 45613056 | tf_op jit(solution)/shard_map/weight_grads/pallas_call | solution.py:616
  133.2 0.9 collective-permute-done
  134.1 0.0 copy-done
  134.1 1.3 broadcast_select_fusion
Async XLA Ops:
  113.2 20.9 %collective-permute-start = (bf16[512,1536]{1,0:T(8,128)(2,1)}, bf16[512,1536]{1,0:T(8,128)(2,1)S(1)}, u32[]{:S(2)}, u32[]{:S(2)}) collective-permute-start(bf16[512,1536]{1,0:T(8,128)(2,1)} %get-tuple-element.27), channel_id=1, source_target_pairs={{0,8},{9,1},{2,10},{11,3},{4,12},{13,5},{6,14},{15,7}} | collective-permute-start | bytes 4718600 | tf_op jit(solution)/shard_map/ppermute | solution.py:605
  116.3 17.8 %copy-start = (bf16[512,1536]{1,0:T(8,128)(2,1)S(1)}, bf16[512,1536]{1,0:T(8,128)(2,1)}, u32[]{:S(2)}) copy-start(bf16[512,1536]{1,0:T(8,128)(2,1)} %get-tuple-element.27) | copy-start | bytes 4718596
